TPU v7x, 256 devices: a whole 4x4x8 slice. The times are simulated.
256 devices in a mesh: curve: 64 (over y, z, core), sub: 4 (over x).
Axes of the slice: x: 4, y: 4, z: 8, core: 2. Of those that a mesh axis runs over, the one named last changes fastest.
Arguments:
- forcing: float32 [12, 6144, 1024], P(None, 'curve', 'sub'), may hold values from -10 to 10
- metric: float32 [6144, 1024], P('curve', 'sub'), may hold values from 0.25 to 4
- jacobian: float32 [6144, 1024], P('curve', 'sub'), may hold values from 0.5 to 2
- mode_scale: float32 [12], replicated, may hold values from 0.1 to 10
Outputs:
- solution: float32 [12, 6144, 1024], P(None, 'curve', 'sub')
- residual: float32 [12, 6144, 1024], P(None, 'curve', 'sub')
All inputs are finite; a program needn't handle non-finite values.
Results may differ from a plain program's by a relative error of at most 0.0003.
Values sent between devices are 32-bit elements; how exact they have to be, the bound alone decides.
No kernel may reach another device: no remote copies, remote signals or barrier semaphores. Data moves between devices by JAX's collectives and lax.ppermute only.
A program may use at most 64 MiB of HBM per device.

v0:
```python
import functools
import math

import jax
import jax.numpy as jnp
import numpy as np
from jax import lax
from jax.sharding import Mesh
from jax.sharding import PartitionSpec as P

ITERS = 3
CURVE_SUB = ("curve_0", "curve_1", "curve_2", "sub")
CURVE = ("curve_0", "curve_1", "curve_2")


def extended(cells, sides, width):
    for axis, dim in sides:
        count = lax.axis_size(axis)
        head = lax.slice_in_dim(cells, 0, width, axis=dim)
        tail = lax.slice_in_dim(cells, cells.shape[dim] - width, cells.shape[dim], axis=dim)
        cells = jnp.concatenate(
            [
                lax.ppermute(tail, axis, [(i, (i + 1) % count) for i in range(count)]),
                cells,
                lax.ppermute(head, axis, [((i + 1) % count, i) for i in range(count)]),
            ],
            axis=dim,
        )
    return cells


def one_axis_at_a_time(x, axes):
    return functools.reduce(lax.psum, axes, x)


def gll_tables():
    points = np.array([-1.0, -1.0 / math.sqrt(5.0), 1.0 / math.sqrt(5.0), 1.0])
    weights = np.array([1.0 / 6.0, 5.0 / 6.0, 5.0 / 6.0, 1.0 / 6.0])
    factor = np.array(
        [np.prod([points[j] - points[m] for m in range(4) if m != j]) for j in range(4)]
    )
    slopes = np.zeros((4, 4))
    for i in range(4):
        for j in range(4):
            if i != j:
                slopes[i, j] = factor[i] / (factor[j] * (points[i] - points[j]))
        slopes[i, i] = sum((1.0 / (points[i] - points[m]) for m in range(4) if m != i))
    return (slopes, weights)


def line_tables(count):
    phase = jnp.arange(count, dtype=jnp.int32) % 4
    on_edge = (phase == 0) | (phase == 3)
    line_w = jnp.where(on_edge, jnp.float32(1.0 / 6.0), jnp.float32(5.0 / 6.0))
    line_mult = jnp.where(on_edge, jnp.float32(2.0), jnp.float32(1.0))
    return (line_w, line_mult)


def combine(padded, axis_dim):
    length = padded.shape[axis_dim] - 2
    center = lax.slice_in_dim(padded, 1, length + 1, axis=axis_dim)
    next_row = lax.slice_in_dim(padded, 2, length + 2, axis=axis_dim)
    before = lax.slice_in_dim(padded, 0, length, axis=axis_dim)
    phase = lax.broadcasted_iota(jnp.int32, center.shape, axis_dim) % 4
    return center + jnp.where(phase == 3, next_row, 0.0) + jnp.where(phase == 0, before, 0.0)


def assemble(values):
    padded = extended(values, ((CURVE, 1), ("sub", 2)), 1)
    return combine(combine(padded, 1), 2)


def along_rows(table, values):
    mode_count, row_count, col_count = values.shape
    shaped = values.reshape(mode_count, row_count // 4, 4, col_count)
    result = jnp.einsum("ka,mxkc->mxac", table, shaped, precision=lax.Precision.HIGHEST)
    return result.reshape(mode_count, row_count, col_count)


def along_cols(table, values):
    lead = values.shape[:-1]
    col_count = values.shape[-1]
    shaped = values.reshape(lead + (col_count // 128, 128))
    result = jnp.matmul(shaped, table, precision=lax.Precision.HIGHEST)
    return result.reshape(lead + (col_count,))


def shards(forcing, metric, jacobian, mode_scale):
    slopes_np = gll_tables()[0]
    slopes = jnp.asarray(slopes_np, jnp.float32)
    col_block = jnp.asarray(np.kron(np.eye(32), slopes_np), jnp.float32)
    col_block_t = jnp.transpose(col_block)
    squared = slopes * slopes
    col_squared = col_block * col_block
    row_w, row_mult = line_tables(metric.shape[0])
    col_w, col_mult = line_tables(metric.shape[1])
    grid_w = row_w[:, None] * col_w[None, :]
    inv_count = (1.0 / (row_mult[:, None] * col_mult[None, :]))[None]
    mass_w = jacobian * grid_w
    flux_w = metric * grid_w
    scale3 = mode_scale[:, None, None]
    mode_count = forcing.shape[0]

    def inner(left, right):
        return jnp.sum(left * right * inv_count, axis=(1, 2))

    lap_terms = along_rows(squared, flux_w[None])[0] + along_cols(col_squared, flux_w)
    stacked = jnp.concatenate([forcing * mass_w[None], mass_w[None], lap_terms[None]], axis=0)
    assembled = assemble(stacked)
    rhs = assembled[:mode_count]
    precond = assembled[mode_count][None] + scale3 * assembled[mode_count + 1][None]
    solution = jnp.zeros_like(rhs)
    residual = rhs
    direction = jnp.zeros_like(rhs)
    along = jnp.zeros_like(rhs)
    rho_old = jnp.ones((mode_count,), jnp.float32)
    step_old = jnp.ones((mode_count,), jnp.float32)
    for iteration in range(ITERS):
        zvec = residual / precond
        grad_x = along_rows(jnp.transpose(slopes), zvec)
        grad_y = along_cols(col_block_t, zvec)
        lap = along_rows(slopes, flux_w[None] * grad_x) + along_cols(
            col_block, flux_w[None] * grad_y
        )
        image = assemble(mass_w[None] * zvec + scale3 * lap)
        rho_next, curve_sum = (
            one_axis_at_a_time(inner(residual, zvec), CURVE_SUB),
            one_axis_at_a_time(inner(image, zvec), CURVE_SUB),
        )
        if iteration == 0:
            step_len = rho_next / curve_sum
            direction = zvec
            along = image
        else:
            mixing = rho_next / rho_old
            step_len = rho_next / (curve_sum - mixing * rho_next / step_old)
            direction = zvec + mixing[:, None, None] * direction
            along = image + mixing[:, None, None] * along
        solution = solution + step_len[:, None, None] * direction
        residual = residual - step_len[:, None, None] * along
        rho_old = rho_next
        step_old = step_len
    return (solution, residual)


def solution(mesh):
    torus = Mesh(
        mesh.devices.reshape(4, 8, 2, mesh.shape["sub"]), ("curve_0", "curve_1", "curve_2", "sub")
    )
    in_specs = (P(None, CURVE, "sub"), P(CURVE, "sub"), P(CURVE, "sub"), P())
    out_specs = (P(None, CURVE, "sub"), P(None, CURVE, "sub"))
    return jax.shard_map(
        shards, mesh=torus, in_specs=in_specs, out_specs=out_specs, check_vma=False
    )
```

profile of v0, /device:TPU:40, one launch (start us, length us, event | category | flops | bytes accessed | tf_op | source)
XLA Modules:
  0.0 263.6 jit_solution(1248867511350576800)
XLA Ops:
  3.7 1.7 collective-permute-start.1
  10.1 2.8 %collective-permute-start.3 = (f32[14,98,1]{1,2,0:T(1,128)S(1)}, f32[14,98,1]{1,2,0:T(1,128)S(1)}, u32[]{:S(2)}, u32[]{:S(2)}) collective-permute-start(f32[14,98,1]{1,2,0:T(1,128)S(1)} %copy.19), channel_id=1, source_target_pairs={{1,0},{2,1},{3,2},{0,3},{5,4},{6,5},{7,6},{4,7},{9,8},{10,9},{11,1... | collective-permute-start | bytes 16472 | tf_op jit(solution)/shard_map/ppermute | solution.py:25
  13.1 4.8 %collective-permute-done.2 = f32[14,98,1]{1,2,0:T(1,128)S(1)} collective-permute-done((f32[14,98,1]{1,2,0:T(1,128)S(1)}, f32[14,98,1]{1,2,0:T(1,128)S(1)}, u32[]{:S(2)}, u32[]{:S(2)}) %collective-permute-start.2) | collective-permute-done | bytes 5520 | tf_op jit(solution)/shard_map/ppermute | solution.py:23
  23.2 2.1 convolution_bitcast_fusion.6
  26.6 3.4 %fusion.16 = f32[12,24,4,256]{3,2,1,0:T(4,128)S(1)} fusion(f32[12,24,4,256]{3,2,1,0:T(4,128)} %reshape.158, f32[4,4,1,1]{1,0,3,2:T(4,128)S(1)} %copy-done.15, f32[24,4,256]{2,1,0:T(4,128)S(1)} %reshape.155), kind=kOutput, calls=%fused_computation.40 | convolution fusion | flops 14450688 | bytes 2457664 | tf_op jit(solution)/shard_map/ka,mxkc->mxac/dot_general | solution.py:76
  30.0 2.2 convolution_bitcast_fusion.7
  33.6 2.0 fusion.36
  41.2 1.9 copy.26
  44.0 2.0 collective-permute-start.6
  50.1 1.8 copy.29
  52.0 1.9 pad_maximum_fusion.1
  54.8 1.9 multiply_reduce_fusion.4
  56.7 8.7 %all-reduce.8 = (f32[12]{0:T(128)S(1)}, f32[12]{0:T(128)S(1)}) all-reduce(f32[12]{0:T(128)S(1)} %get-tuple-element.7, f32[12]{0:T(128)S(1)} %get-tuple-element.6), channel_id=1, replica_groups=mesh['curve_0'=4,'curve_1'=8,'curve_2'=2,'sub'=4] {'curve_0'}, use_global_device_ids=true, to_apply=%region_1.2 | all-reduce | flops 24 | bytes 192 | tf_op jit(solution)/shard_map/psum | solution.py:33
  65.4 23.1 %all-reduce.2 = (f32[12]{0:T(128)S(1)}, f32[12]{0:T(128)S(1)}) all-reduce(f32[12]{0:T(128)S(1)} %get-tuple-element.24, f32[12]{0:T(128)S(1)} %get-tuple-element.25), channel_id=1, replica_groups=mesh['curve_0'=4,'curve_1'=8,'curve_2'=2,'sub'=4] {'curve_1'}, use_global_device_ids=true, to_apply=%region_2.3 | all-reduce | flops 24 | bytes 192 | tf_op jit(solution)/shard_map/psum | solution.py:33
  88.5 2.5 all-reduce.11
  91.0 9.0 %all-reduce.5 = (f32[12]{0:T(128)S(1)}, f32[12]{0:T(128)S(1)}) all-reduce(f32[12]{0:T(128)S(1)} %get-tuple-element.30, f32[12]{0:T(128)S(1)} %get-tuple-element.31), channel_id=1, replica_groups=mesh['curve_0'=4,'curve_1'=8,'curve_2'=2,'sub'=4] {'sub'}, use_global_device_ids=true, to_apply=%region_4.5 | all-reduce | flops 24 | bytes 192 | tf_op jit(solution)/shard_map/psum | solution.py:33
  103.3 2.1 convolution_bitcast_fusion.3
  106.7 2.6 reshape.162
  109.3 3.4 %fusion.15 = f32[12,24,4,256]{3,2,1,0:T(4,128)S(1)} fusion(f32[12,24,4,256]{3,2,1,0:T(4,128)} %reshape.162, f32[4,4,1,1]{1,0,3,2:T(4,128)S(1)} %copy-done.16, f32[24,4,256]{2,1,0:T(4,128)S(1)} %copy-done.6), kind=kOutput, calls=%fused_computation.36 | convolution fusion | flops 14450688 | bytes 2457664 | tf_op jit(solution)/shard_map/ka,mxkc->mxac/dot_general | solution.py:76
  112.7 3.2 %convolution_bitcast_fusion.4 = f32[12,24,4,256]{3,2,1,0:T(4,128)} fusion(f32[12,24,4,256]{3,2,1,0:T(4,128)S(1)} %fusion.15, f32[4,4,1,1]{1,0,3,2:T(4,128)S(1)} %copy-done.16), kind=kOutput, calls=%fused_computation.34 | convolution fusion | flops 14155776 | bytes 2359360 | tf_op jit(solution)/shard_map/ka,mxkc->mxac/dot_general | solution.py:76
  115.9 2.6 reshape.163
  118.5 2.0 fusion.34
  120.6 1.7 collective-permute-start.9
  126.2 1.9 copy.33
  130.1 2.2 collective-permute-start.11
  134.2 1.8 copy.36
  136.1 2.3 pad_maximum_fusion.2
  139.4 1.9 multiply_reduce_fusion.2
  141.3 7.7 %all-reduce.7 = (f32[12]{0:T(128)S(1)}, f32[12]{0:T(128)S(1)}) all-reduce(f32[12]{0:T(128)S(1)} %get-tuple-element.5, f32[12]{0:T(128)S(1)} %get-tuple-element.4), channel_id=1, replica_groups=mesh['curve_0'=4,'curve_1'=8,'curve_2'=2,'sub'=4] {'curve_0'}, use_global_device_ids=true, to_apply=%region_11.12 | all-reduce | flops 24 | bytes 192 | tf_op jit(solution)/shard_map/psum | solution.py:33
  149.0 17.5 %all-reduce.1 = (f32[12]{0:T(128)S(1)}, f32[12]{0:T(128)S(1)}) all-reduce(f32[12]{0:T(128)S(1)} %get-tuple-element.22, f32[12]{0:T(128)S(1)} %get-tuple-element.23), channel_id=1, replica_groups=mesh['curve_0'=4,'curve_1'=8,'curve_2'=2,'sub'=4] {'curve_1'}, use_global_device_ids=true, to_apply=%region_12.13 | all-reduce | flops 24 | bytes 192 | tf_op jit(solution)/shard_map/psum | solution.py:33
  166.4 2.5 all-reduce.10
  168.9 10.9 %all-reduce.4 = (f32[12]{0:T(128)S(1)}, f32[12]{0:T(128)S(1)}) all-reduce(f32[12]{0:T(128)S(1)} %get-tuple-element.28, f32[12]{0:T(128)S(1)} %get-tuple-element.29), channel_id=1, replica_groups=mesh['curve_0'=4,'curve_1'=8,'curve_2'=2,'sub'=4] {'sub'}, use_global_device_ids=true, to_apply=%region_14.15 | all-reduce | flops 24 | bytes 192 | tf_op jit(solution)/shard_map/psum | solution.py:33
  180.4 2.1 fusion.49
  183.7 2.1 convolution_bitcast_fusion
  187.1 2.6 reshape.166
  189.7 3.4 %fusion.14 = f32[12,24,4,256]{3,2,1,0:T(4,128)S(1)} fusion(f32[12,24,4,256]{3,2,1,0:T(4,128)} %reshape.166, f32[4,4,1,1]{1,0,3,2:T(4,128)S(1)} %copy-done.17, f32[24,4,256]{2,1,0:T(4,128)S(1)} %copy-done.7), kind=kOutput, calls=%fused_computation.32 | convolution fusion | flops 14450688 | bytes 2457664 | tf_op jit(solution)/shard_map/ka,mxkc->mxac/dot_general | solution.py:76
  193.1 3.2 %convolution_bitcast_fusion.1 = f32[12,24,4,256]{3,2,1,0:T(4,128)} fusion(f32[12,24,4,256]{3,2,1,0:T(4,128)S(1)} %fusion.14, f32[4,4,1,1]{1,0,3,2:T(4,128)S(1)} %copy-done.17), kind=kOutput, calls=%fused_computation.30 | convolution fusion | flops 14155776 | bytes 2359360 | tf_op jit(solution)/shard_map/ka,mxkc->mxac/dot_general | solution.py:76
  196.3 2.6 %reshape.167 = f32[12,96,256]{2,1,0:T(8,128)} reshape(f32[12,24,4,256]{3,2,1,0:T(4,128)} %convolution_bitcast_fusion.1) | data formatting | bytes 2359296 | tf_op jit(solution)/shard_map/reshape | solution.py:77
  198.9 2.4 fusion.32
  201.6 1.7 collective-permute-start.13
  207.6 3.3 %collective-permute-start.15 = (f32[12,98,1]{1,2,0:T(1,128)S(1)}, f32[12,98,1]{1,2,0:T(1,128)S(1)}, u32[]{:S(2)}, u32[]{:S(2)}) collective-permute-start(f32[12,98,1]{1,2,0:T(1,128)S(1)} %copy.41), channel_id=1, source_target_pairs={{1,0},{2,1},{3,2},{0,3},{5,4},{6,5},{7,6},{4,7},{9,8},{10,9},{11,1... | collective-permute-start | bytes 14120 | tf_op jit(solution)/shard_map/ppermute | solution.py:25
  213.6 2.3 pad_maximum_fusion.3
  217.3 1.9 multiply_reduce_fusion
  219.2 8.5 %all-reduce.6 = (f32[12]{0:T(128)S(1)}, f32[12]{0:T(128)S(1)}) all-reduce(f32[12]{0:T(128)S(1)} %get-tuple-element.3, f32[12]{0:T(128)S(1)} %get-tuple-element.2), channel_id=1, replica_groups=mesh['curve_0'=4,'curve_1'=8,'curve_2'=2,'sub'=4] {'curve_0'}, use_global_device_ids=true, to_apply=%region_21.22 | all-reduce | flops 24 | bytes 192 | tf_op jit(solution)/shard_map/psum | solution.py:33
  227.7 17.5 %all-reduce = (f32[12]{0:T(128)S(1)}, f32[12]{0:T(128)S(1)}) all-reduce(f32[12]{0:T(128)S(1)} %get-tuple-element.20, f32[12]{0:T(128)S(1)} %get-tuple-element.21), channel_id=1, replica_groups=mesh['curve_0'=4,'curve_1'=8,'curve_2'=2,'sub'=4] {'curve_1'}, use_global_device_ids=true, to_apply=%region_22.23 | all-reduce | flops 24 | bytes 192 | tf_op jit(solution)/shard_map/psum | solution.py:33
  245.2 2.5 all-reduce.9
  247.7 10.9 %all-reduce.3 = (f32[12]{0:T(128)S(1)}, f32[12]{0:T(128)S(1)}) all-reduce(f32[12]{0:T(128)S(1)} %get-tuple-element.26, f32[12]{0:T(128)S(1)} %get-tuple-element.27), channel_id=1, replica_groups=mesh['curve_0'=4,'curve_1'=8,'curve_2'=2,'sub'=4] {'sub'}, use_global_device_ids=true, to_apply=%region_24.25 | all-reduce | flops 24 | bytes 192 | tf_op jit(solution)/shard_map/psum | solution.py:33
  258.6 4.8 %multiply_subtract_fusion = (f32[12,96,256]{2,1,0:T(8,128)}, f32[12,96,256]{2,1,0:T(8,128)}) fusion(f32[12,96,256]{2,1,0:T(8,128)} %copy-done, f32[12,96,256]{2,1,0:T(8,128)} %get-tuple-element.34, f32[12]{0:T(128)S(1)} %get-tuple-element.33, f32[12]{0:T(128)S(1)} %get-tuple-element.32, f32[12,96,256]{2,1,0:T(8,128)} %get-tuple-element.40, ...), kind=kLoop, calls=%fused_computation.78 | loop fusion | flops 5898240 | bytes 9634080 | tf_op jit(solution)/shard_map/sub | solution.py:140
  (214 shorter events, 51.8 us)
Async XLA Ops:
  0.6 2.5 copy-start.54
  0.6 2.9 %copy-start.11 = (f32[12,96,256]{2,1,0:T(8,128)S(1)}, f32[12,96,256]{2,1,0:T(8,128)}, u32[]{:S(2)}) copy-start(f32[12,96,256]{2,1,0:T(8,128)} %param.6) | copy-start | bytes 3538948
  1.8 24.8 %copy-start.5 = (f32[24,4,256]{2,1,0:T(4,128)}, f32[24,4,256]{2,1,0:T(4,128)S(1)}, u32[]{:S(2)}) copy-start(f32[24,4,256]{2,1,0:T(4,128)S(1)} %reshape.155) | copy-start | bytes 294916
  3.6 3.2 %collective-permute-start = (f32[14,1,256]{2,1,0:T(1,128)S(1)}, f32[14,1,256]{2,1,0:T(1,128)S(1)}, u32[]{:S(2)}, u32[]{:S(2)}) collective-permute-start(f32[14,1,256]{2,1,0:T(1,128)S(1)} %get-tuple-element.48), channel_id=1, source_target_pairs={{0,4},{4,8},{8,12},{12,16},{16,20},{20,24},{24,28},{28,32},{32,36}... | collective-permute-start | bytes 43016 | tf_op jit(solution)/shard_map/ppermute | solution.py:23
  3.7 3.2 %collective-permute-start.1 = (f32[14,1,256]{2,1,0:T(1,128)S(1)}, f32[14,1,256]{2,1,0:T(1,128)S(1)}, u32[]{:S(2)}, u32[]{:S(2)}) collective-permute-start(f32[14,1,256]{2,1,0:T(1,128)S(1)} %get-tuple-element.49), channel_id=1, source_target_pairs={{4,0},{8,4},{12,8},{16,12},{20,16},{24,20},{28,24},{32,28},{36,32}... | collective-permute-start | bytes 43016 | tf_op jit(solution)/shard_map/ppermute | solution.py:25
  6.1 13.6 %copy-start.34 = (s32[96]{0:T(128)}, s32[96]{0:T(128)S(1)}, u32[]{:S(2)}) copy-start(s32[96]{0:T(128)S(1)} %get-tuple-element.66) | copy-start | bytes 1156
  6.1 13.6 %copy-start.38 = (s32[96]{0:T(128)}, s32[96]{0:T(128)S(1)}, u32[]{:S(2)}) copy-start(s32[96]{0:T(128)S(1)} %get-tuple-element.67) | copy-start | bytes 1156
  6.1 14.2 %copy-start.26 = (s32[256]{0:T(256)}, s32[256]{0:T(256)S(1)}, u32[]{:S(2)}) copy-start(s32[256]{0:T(256)S(1)} %get-tuple-element.68) | copy-start | bytes 3076
  6.1 14.2 %copy-start.30 = (s32[256]{0:T(256)}, s32[256]{0:T(256)S(1)}, u32[]{:S(2)}) copy-start(s32[256]{0:T(256)S(1)} %get-tuple-element.69) | copy-start | bytes 3076
  6.1 15.3 %copy-start.12 = (f32[96,2,128]{2,0,1:T(8,128)}, f32[96,2,128]{2,0,1:T(8,128)S(1)}, u32[]{:S(2)}) copy-start(f32[96,2,128]{2,0,1:T(8,128)S(1)} %copy_bitcast_fusion) | copy-start | bytes 294916
  6.1 13.5 %copy-start.42 = (pred[96]{0:T(512)(128)(4,1)}, pred[96]{0:T(512)(128)(4,1)S(1)}, u32[]{:S(2)}) copy-start(pred[96]{0:T(512)(128)(4,1)S(1)} %compare_and_fusion.1) | copy-start | bytes 292
  10.1 8.1 %collective-permute-start.3 = (f32[14,98,1]{1,2,0:T(1,128)S(1)}, f32[14,98,1]{1,2,0:T(1,128)S(1)}, u32[]{:S(2)}, u32[]{:S(2)}) collective-permute-start(f32[14,98,1]{1,2,0:T(1,128)S(1)} %copy.19), channel_id=1, source_target_pairs={{1,0},{2,1},{3,2},{0,3},{5,4},{6,5},{7,6},{4,7},{9,8},{10,9},{11,1... | collective-permute-start | bytes 16472 | tf_op jit(solution)/shard_map/ppermute | solution.py:25
  12.9 5.0 %collective-permute-start.2 = (f32[14,98,1]{1,2,0:T(1,128)S(1)}, f32[14,98,1]{1,2,0:T(1,128)S(1)}, u32[]{:S(2)}, u32[]{:S(2)}) collective-permute-start(f32[14,98,1]{1,2,0:T(1,128)S(1)} %copy.18), channel_id=1, source_target_pairs={{0,1},{1,2},{2,3},{3,0},{4,5},{5,6},{6,7},{7,4},{8,9},{9,10},{10,1... | collective-permute-start | bytes 16472 | tf_op jit(solution)/shard_map/ppermute | solution.py:23
  13.1 7.2 %copy-start.46 = (pred[256]{0:T(512)(128)(4,1)}, pred[256]{0:T(512)(128)(4,1)S(1)}, u32[]{:S(2)}) copy-start(pred[256]{0:T(512)(128)(4,1)S(1)} %compare_and_fusion) | copy-start | bytes 772
  35.6 3.2 %collective-permute-start.4 = (f32[12,1,256]{2,1,0:T(1,128)S(1)}, f32[12,1,256]{2,1,0:T(1,128)S(1)}, u32[]{:S(2)}, u32[]{:S(2)}) collective-permute-start(f32[12,1,256]{2,1,0:T(1,128)S(1)} %get-tuple-element.62), channel_id=1, source_target_pairs={{0,4},{4,8},{8,12},{12,16},{16,20},{20,24},{24,28},{28,32},{32,36}... | collective-permute-start | bytes 36872 | tf_op jit(solution)/shard_map/ppermute | solution.py:23
  36.3 2.8 %collective-permute-start.5 = (f32[12,1,256]{2,1,0:T(1,128)S(1)}, f32[12,1,256]{2,1,0:T(1,128)S(1)}, u32[]{:S(2)}, u32[]{:S(2)}) collective-permute-start(f32[12,1,256]{2,1,0:T(1,128)S(1)} %get-tuple-element.63), channel_id=1, source_target_pairs={{4,0},{8,4},{12,8},{16,12},{20,16},{24,20},{28,24},{32,28},{36,32}... | collective-permute-start | bytes 36872 | tf_op jit(solution)/shard_map/ppermute | solution.py:25
  44.0 6.1 %collective-permute-start.7 = (f32[12,98,1]{1,2,0:T(1,128)}, f32[12,98,1]{1,2,0:T(1,128)}, u32[]{:S(2)}, u32[]{:S(2)}) collective-permute-start(f32[12,98,1]{1,2,0:T(1,128)} %copy.27), channel_id=1, source_target_pairs={{1,0},{2,1},{3,2},{0,3},{5,4},{6,5},{7,6},{4,7},{9,8},{10,9},{11,1... | collective-permute-start | bytes 14120 | tf_op jit(solution)/shard_map/ppermute | solution.py:25
  44.0 5.2 %collective-permute-start.6 = (f32[12,98,1]{1,2,0:T(1,128)}, f32[12,98,1]{1,2,0:T(1,128)}, u32[]{:S(2)}, u32[]{:S(2)}) collective-permute-start(f32[12,98,1]{1,2,0:T(1,128)} %copy.26), channel_id=1, source_target_pairs={{0,1},{1,2},{2,3},{3,0},{4,5},{5,6},{6,7},{7,4},{8,9},{9,10},{10,1... | collective-permute-start | bytes 14120 | tf_op jit(solution)/shard_map/ppermute | solution.py:23
  106.7 2.6 copy-start.6
  106.7 2.6 copy-start.16
  120.5 4.6 %copy-start.3 = (f32[12,96,256]{2,1,0:T(8,128)}, f32[12,96,256]{2,1,0:T(8,128)S(1)}, u32[]{:S(2)}) copy-start(f32[12,96,256]{2,1,0:T(8,128)S(1)} %fusion.34) | copy-start | bytes 3538948
  120.5 3.2 %collective-permute-start.8 = (f32[12,1,256]{2,1,0:T(1,128)S(1)}, f32[12,1,256]{2,1,0:T(1,128)S(1)}, u32[]{:S(2)}, u32[]{:S(2)}) collective-permute-start(f32[12,1,256]{2,1,0:T(1,128)S(1)} %get-tuple-element.60), channel_id=1, source_target_pairs={{0,4},{4,8},{8,12},{12,16},{16,20},{20,24},{24,28},{28,32},{32,36}... | collective-permute-start | bytes 36872 | tf_op jit(solution)/shard_map/ppermute | solution.py:23
  120.6 3.1 %collective-permute-start.9 = (f32[12,1,256]{2,1,0:T(1,128)S(1)}, f32[12,1,256]{2,1,0:T(1,128)S(1)}, u32[]{:S(2)}, u32[]{:S(2)}) collective-permute-start(f32[12,1,256]{2,1,0:T(1,128)S(1)} %get-tuple-element.61), channel_id=1, source_target_pairs={{4,0},{8,4},{12,8},{16,12},{20,16},{24,20},{28,24},{32,28},{36,32}... | collective-permute-start | bytes 36872 | tf_op jit(solution)/shard_map/ppermute | solution.py:25
  128.1 5.2 %collective-permute-start.10 = (f32[12,98,1]{1,2,0:T(1,128)}, f32[12,98,1]{1,2,0:T(1,128)}, u32[]{:S(2)}, u32[]{:S(2)}) collective-permute-start(f32[12,98,1]{1,2,0:T(1,128)} %copy.33), channel_id=1, source_target_pairs={{0,1},{1,2},{2,3},{3,0},{4,5},{5,6},{6,7},{7,4},{8,9},{9,10},{10,1... | collective-permute-start | bytes 14120 | tf_op jit(solution)/shard_map/ppermute | solution.py:23
  130.1 4.1 %collective-permute-start.11 = (f32[12,98,1]{1,2,0:T(1,128)}, f32[12,98,1]{1,2,0:T(1,128)}, u32[]{:S(2)}, u32[]{:S(2)}) collective-permute-start(f32[12,98,1]{1,2,0:T(1,128)} %copy.34), channel_id=1, source_target_pairs={{1,0},{2,1},{3,2},{0,3},{5,4},{6,5},{7,6},{4,7},{9,8},{10,9},{11,1... | collective-permute-start | bytes 14120 | tf_op jit(solution)/shard_map/ppermute | solution.py:25
  136.1 2.4 copy-start.36
  136.1 2.4 copy-start.40
  136.1 2.4 copy-start.44
  139.4 40.4 %copy-start.61 = (f32[12]{0:T(128)S(1)}, f32[12]{0:T(128)}, u32[]{:S(2)}) copy-start(f32[12]{0:T(128)} %copy-done.60) | copy-start | bytes 148
  139.4 40.4 %copy-start.63 = (f32[12]{0:T(128)S(1)}, f32[12]{0:T(128)}, u32[]{:S(2)}) copy-start(f32[12]{0:T(128)} %copy-done.62) | copy-start | bytes 148
  180.3 2.2 copy-start.50
  180.3 2.2 copy-start.52
  182.6 3.2 %copy-start = (f32[12,96,256]{2,1,0:T(8,128)}, f32[12,96,256]{2,1,0:T(8,128)S(1)}, u32[]{:S(2)}) copy-start(f32[12,96,256]{2,1,0:T(8,128)S(1)} %get-tuple-element.36) | copy-start | bytes 3538948
  187.1 2.6 copy-start.7
  187.1 2.6 copy-start.17
  201.3 3.6 %copy-start.2 = (f32[12,96,256]{2,1,0:T(8,128)}, f32[12,96,256]{2,1,0:T(8,128)S(1)}, u32[]{:S(2)}) copy-start(f32[12,96,256]{2,1,0:T(8,128)S(1)} %fusion.32) | copy-start | bytes 3538948
  201.3 3.4 %collective-permute-start.12 = (f32[12,1,256]{2,1,0:T(1,128)S(1)}, f32[12,1,256]{2,1,0:T(1,128)S(1)}, u32[]{:S(2)}, u32[]{:S(2)}) collective-permute-start(f32[12,1,256]{2,1,0:T(1,128)S(1)} %get-tuple-element.58), channel_id=1, source_target_pairs={{0,4},{4,8},{8,12},{12,16},{16,20},{20,24},{24,28},{28,32},{32,36}... | collective-permute-start | bytes 36872 | tf_op jit(solution)/shard_map/ppermute | solution.py:23
  201.6 3.1 %collective-permute-start.13 = (f32[12,1,256]{2,1,0:T(1,128)S(1)}, f32[12,1,256]{2,1,0:T(1,128)S(1)}, u32[]{:S(2)}, u32[]{:S(2)}) collective-permute-start(f32[12,1,256]{2,1,0:T(1,128)S(1)} %get-tuple-element.59), channel_id=1, source_target_pairs={{4,0},{8,4},{12,8},{16,12},{20,16},{24,20},{28,24},{32,28},{36,32}... | collective-permute-start | bytes 36872 | tf_op jit(solution)/shard_map/ppermute | solution.py:25
  207.3 4.9 %collective-permute-start.14 = (f32[12,98,1]{1,2,0:T(1,128)S(1)}, f32[12,98,1]{1,2,0:T(1,128)S(1)}, u32[]{:S(2)}, u32[]{:S(2)}) collective-permute-start(f32[12,98,1]{1,2,0:T(1,128)S(1)} %copy.40), channel_id=1, source_target_pairs={{0,1},{1,2},{2,3},{3,0},{4,5},{5,6},{6,7},{7,4},{8,9},{9,10},{10,1... | collective-permute-start | bytes 14120 | tf_op jit(solution)/shard_map/ppermute | solution.py:23
  207.6 4.9 %collective-permute-start.15 = (f32[12,98,1]{1,2,0:T(1,128)S(1)}, f32[12,98,1]{1,2,0:T(1,128)S(1)}, u32[]{:S(2)}, u32[]{:S(2)}) collective-permute-start(f32[12,98,1]{1,2,0:T(1,128)S(1)} %copy.41), channel_id=1, source_target_pairs={{1,0},{2,1},{3,2},{0,3},{5,4},{6,5},{7,6},{4,7},{9,8},{10,9},{11,1... | collective-permute-start | bytes 14120 | tf_op jit(solution)/shard_map/ppermute | solution.py:25
  213.6 2.3 copy-start.37
  213.6 2.3 copy-start.41
  213.6 2.4 copy-start.45
  217.3 41.3 %copy-start.56 = (f32[12]{0:T(128)S(1)}, f32[12]{0:T(128)}, u32[]{:S(2)}) copy-start(f32[12]{0:T(128)} %copy-done.55) | copy-start | bytes 148
  217.3 41.3 %copy-start.57 = (f32[12]{0:T(128)S(1)}, f32[12]{0:T(128)}, u32[]{:S(2)}) copy-start(f32[12]{0:T(128)} %get-tuple-element.38) | copy-start | bytes 148
  217.3 41.3 %copy-start.51 = (f32[12]{0:T(128)S(1)}, f32[12]{0:T(128)}, u32[]{:S(2)}) copy-start(f32[12]{0:T(128)} %copy-done.50) | copy-start | bytes 148
  217.3 41.3 %copy-start.53 = (f32[12]{0:T(128)S(1)}, f32[12]{0:T(128)}, u32[]{:S(2)}) copy-start(f32[12]{0:T(128)} %copy-done.52) | copy-start | bytes 148
  217.3 41.3 %copy-start.59 = (f32[12]{0:T(128)S(1)}, f32[12]{0:T(128)}, u32[]{:S(2)}) copy-start(f32[12]{0:T(128)} %copy-done.58) | copy-start | bytes 148
  (32 other events, 35.0 us)
where the time goes:
time: 269 us; the launch traced here: 264 us
  blocking collectives  121 us (45%)
  local copies, waits for them, and re-layouts  39.5 us (15%)
  other arithmetic  38.9 us (14%)
  matrix products  29.8 us (11%)
  starting transfers between devices  19.4 us (7%)
  waiting for transfers between devices  13.2 us (5%)
    psum x12, blocking collectives, one_axis_at_a_time(): return functools.reduce(lax.psum, axes, x)  121 us
    dot_general x7, matrix products, along_rows(): jnp.einsum('ka,mxkc->mxac', table, shaped, precision=lax.Precision.HIGHEST)  19 us
    ppermute x8, starting transfers between devices, extended(): lax.ppermute(head, axis, [((i + 1) % count, i) for i in range(count)])  14.8 us
    ppermute x8, waiting for transfers between devices, extended(): lax.ppermute(tail, axis, [(i, (i + 1) % count) for i in range(count)])  12.9 us
    slice x11, local copies, waits for them, and re-layouts, extended(): lax.slice_in_dim(cells, cells.shape[dim] - width, cells.shape[dim], axis=...  11.2 us
    dot_general x7, matrix products, along_cols(): result = jnp.matmul(shaped, table, precision=lax.Precision.HIGHEST)  10.8 us
    concatenate x8, other arithmetic, extended(): jnp.concatenate([lax.ppermute(tail, axis, [(i, (i + 1) % count) for i in...  8.18 us
    reshape x3, local copies, waits for them, and re-layouts, along_rows(): return result.reshape(mode_count, row_count, col_count)  6.69 us
  transfers between devices with their start and end apart: 16, of which 9 were waited for; matrix products, arithmetic and copies ran while one was open for 2% of the time, Pallas kernels for 0%

commit v1 on v0

v1 whole, which is shorter than its diff:
```python
import functools
import math

import jax
import jax.numpy as jnp
import numpy as np
from jax import lax
from jax.experimental import pallas as pl
from jax.experimental.pallas import tpu as pltpu
from jax.sharding import PartitionSpec as P

GHOST = 4
PACK = 4
LANES = 128
AXES = ("curve", "sub")


def gll_tables():
    points = np.array([-1.0, -1.0 / math.sqrt(5.0), 1.0 / math.sqrt(5.0), 1.0])
    weights = np.array([1.0 / 6.0, 5.0 / 6.0, 5.0 / 6.0, 1.0 / 6.0])
    factor = np.array(
        [np.prod([points[j] - points[m] for m in range(4) if m != j]) for j in range(4)]
    )
    slopes = np.zeros((4, 4))
    for i in range(4):
        for j in range(4):
            if i != j:
                slopes[i, j] = factor[i] / (factor[j] * (points[i] - points[j]))
        slopes[i, i] = sum((1.0 / (points[i] - points[m]) for m in range(4) if m != i))
    return (slopes, weights)


SLOPES, WEIGHTS = gll_tables()
PAIRS = [(a, k) for a in range(4) for k in range(a + 1, 4)]


def plane(group, a, b):
    return (group * 4 + a) * 4 + b


def spread_kernel(rows, f_ref, metric_ref, jacobian_ref, up_ref, down_ref, t_ref, low_ref, high_ref, xs, xt):
    half = pl.program_id(0)
    own = rows // 4
    groups = f_ref.shape[0] // PACK
    per_half = LANES // 4
    for group in range(groups + 1):
        for a in range(4):
            at = group * 4 + a
            for m in range(PACK):
                if group < groups:
                    index = group * PACK + m
                    mine = f_ref[index, pl.ds(a, own, stride=4), :]
                else:
                    index = groups * PACK + m % 2
                    mine = (metric_ref, jacobian_ref)[m % 2][pl.ds(a, own, stride=4), :]
                xs[at, pl.ds(m, own, stride=PACK), :] = mine
                xs[at, pl.ds(own * PACK + m, GHOST, stride=PACK), :] = down_ref[
                    index, pl.ds(a, GHOST, stride=4), :
                ]
                xs[at, pl.ds((own + GHOST) * PACK + m, GHOST, stride=PACK), :] = up_ref[
                    index, pl.ds(a, GHOST, stride=4), :
                ]
            xt[at] = xs[at].T
            for b in range(4):
                t_ref[at * 4 + b] = xt[at, pl.ds(b, per_half, stride=4), :]

    @pl.when(half == 0)
    def _():
        for p in range(t_ref.shape[0]):
            low_ref[p] = t_ref[p, :GHOST, :]

    @pl.when(half == pl.num_programs(0) - 1)
    def _():
        for p in range(t_ref.shape[0]):
            high_ref[p] = t_ref[p, per_half - GHOST :, :]


def line_operator(coefs, values):
    out = [None] * 4
    for (a, k), coef in zip(PAIRS, coefs):
        flow = coef * (values[k] - values[a])
        out[a] = flow if out[a] is None else out[a] + flow
        out[k] = -flow if out[k] is None else out[k] - flow
    return out


def krylov_kernel(
    own_rows,
    t_ref,
    right_ref,
    left_ref,
    scale_ref,
    u0_ref,
    u1_ref,
    u2_ref,
    w_ref,
    mass_sum_ref,
    lap_sum_ref,
    part_ref,
    mass_ref,
    krow,
    kcol,
    minv,
    edge,
):
    groups = u0_ref.shape[0] // 16
    cols = t_ref.shape[1]
    total = u0_ref.shape[1]
    tiles = total // 8
    lane = lax.broadcasted_iota(jnp.int32, (8, LANES), 1)

    def next_row(x):
        return pltpu.roll(x, LANES - PACK, 1)

    def prev_row(x):
        return pltpu.roll(x, PACK, 1)

    def join_rows(first, last):
        shared = last + next_row(first)
        return prev_row(shared), shared

    def tile(t):
        return pl.ds(pl.multiple_of(t * 8, 8), 8)

    def set_edge(t, i, first, last):
        edge[2 * i, pl.ds(pl.multiple_of(t * 8 + 8, 8), 8), :] = first
        edge[2 * i + 1, pl.ds(pl.multiple_of(t * 8 + 8, 8), 8), :] = last

    def join_cols(i):
        edge[2 * i, total + 8 : total + 16, :] = edge[2 * i, 8:16, :]
        edge[2 * i + 1, 0:8, :] = edge[2 * i + 1, total : total + 8, :]
        first = edge[2 * i, 8 : total + 8, :] + edge[2 * i + 1, 7 : total + 7, :]
        last = edge[2 * i + 1, 8 : total + 8, :] + edge[2 * i, 9 : total + 9, :]
        return first, last

    def coefficients(t, fetch):
        even = lane % 2 == 0
        flux = [[None] * 4 for _ in range(4)]
        mass = [[None] * 4 for _ in range(4)]
        for a in range(4):
            for b in range(4):
                x = fetch(plane(groups, a, b))
                w = np.float32(WEIGHTS[a] * WEIGHTS[b])
                flux[a][b] = jnp.where(even, x, pltpu.roll(x, 1, 1)) * w
                mass[a][b] = jnp.where(even, pltpu.roll(x, LANES - 1, 1), x) * w
                mass_ref[a * 4 + b, tile(t), :] = mass[a][b]
        lap = [[None] * 4 for _ in range(4)]

        def add(a, b, value):
            lap[a][b] = value if lap[a][b] is None else lap[a][b] + value

        for line in range(4):
            for i, (p, q) in enumerate(PAIRS):
                c = [np.float32(SLOPES[j, p] * SLOPES[j, q]) for j in range(4)]
                kr = sum(flux[j][line] * c[j] for j in range(4))
                kc = sum(flux[line][j] * c[j] for j in range(4))
                krow[line * 6 + i, tile(t), :] = kr
                kcol[line * 6 + i, tile(t), :] = kc
                add(p, line, -kr)
                add(q, line, -kr)
                add(line, p, -kc)
                add(line, q, -kc)
        for values, out, base in ((mass, mass_sum_ref, 0), (lap, lap_sum_ref, 4)):
            for b in range(4):
                first, last = join_rows(values[0][b], values[3][b])
                column = [first, values[1][b], values[2][b], last]
                for a in range(4):
                    if b in (1, 2):
                        out[a * 4 + b, tile(t), :] = column[a]
                    else:
                        edge[2 * (base + a) + b // 3, pl.ds(pl.multiple_of(t * 8 + 8, 8), 8), :] = column[a]

    def own_tile(t):
        return lambda p: t_ref[p, tile(t), :]

    def ghost_tile(p):
        return jnp.concatenate([right_ref[p], left_ref[p]], axis=0)

    pl.loop(0, cols // 8)(lambda t: coefficients(t, own_tile(t)))
    coefficients(cols // 8, ghost_tile)
    for i in range(8):
        first, last = join_cols(i)
        out = (mass_sum_ref, lap_sum_ref)[i // 4]
        a = i % 4
        out[a * 4] = first
        out[a * 4 + 3] = last

    @pl.loop(0, 16)
    def _(p):
        mass_sum = mass_sum_ref[p]
        lap_sum = lap_sum_ref[p]
        for group in range(groups):
            minv[group * 16 + p] = 1.0 / (mass_sum + scale_ref[group : group + 1, :] * lap_sum)

    def source(t, fetch):
        for group in range(groups):
            for b in range(4):
                column = [
                    fetch(plane(group, a, b)) * mass_ref[a * 4 + b, tile(t), :] for a in range(4)
                ]
                for a in range(4):
                    w_ref[plane(group, a, b), tile(t), :] = column[a]
                column[0], column[3] = join_rows(column[0], column[3])
                for a in range(4):
                    p = plane(group, a, b)
                    if b in (1, 2):
                        u0_ref[p, tile(t), :] = column[a] * minv[p, tile(t), :]
                    else:
                        edge[2 * (group * 4 + a) + b // 3, pl.ds(pl.multiple_of(t * 8 + 8, 8), 8), :] = column[a]

    pl.loop(0, cols // 8)(lambda t: source(t, own_tile(t)))
    source(cols // 8, ghost_tile)

    @pl.loop(0, groups * 4)
    def _(i):
        first, last = join_cols(i)
        u0_ref[i * 4] = first * minv[i * 4]
        u0_ref[i * 4 + 3] = last * minv[i * 4 + 3]

    zero = jnp.zeros((8, LANES), jnp.float32)

    def first_moment(t, sums):
        sums = list(sums)
        for group in range(groups):
            for p in range(group * 16, group * 16 + 16):
                sums[group] += w_ref[p, tile(t), :] * u0_ref[p, tile(t), :]
        return tuple(sums)

    moments = [lax.fori_loop(0, cols // 8, first_moment, (zero,) * groups)]

    def apply(now_ref, old_ref, new_ref):
        def body(t, sums):
            sums = list(sums)
            own = (t < cols // 8).astype(jnp.float32)
            for group in range(groups):
                u = [[now_ref[plane(group, a, b), tile(t), :] for b in range(4)] for a in range(4)]
                lap = [[None] * 4 for _ in range(4)]
                for line in range(4):
                    out = line_operator(
                        [krow[line * 6 + i, tile(t), :] for i in range(6)],
                        [u[a][line] for a in range(4)],
                    )
                    for a in range(4):
                        lap[a][line] = out[a]
                for line in range(4):
                    out = line_operator(
                        [kcol[line * 6 + i, tile(t), :] for i in range(6)], u[line]
                    )
                    for b in range(4):
                        lap[line][b] = lap[line][b] + out[b]
                scale = scale_ref[group : group + 1, :]
                with_now, with_old = zero, zero
                y = [[None] * 4 for _ in range(4)]
                for a in range(4):
                    for b in range(4):
                        y[a][b] = mass_ref[a * 4 + b, tile(t), :] * u[a][b] + scale * lap[a][b]
                        with_now += u[a][b] * y[a][b]
                        if old_ref is not None:
                            with_old += old_ref[plane(group, a, b), tile(t), :] * y[a][b]
                sums[group] += own * with_now
                if old_ref is not None:
                    sums[groups + group] += own * with_old
                for b in range(4):
                    column = [y[a][b] for a in range(4)]
                    column[0], column[3] = join_rows(column[0], column[3])
                    for a in range(4):
                        p = plane(group, a, b)
                        if b in (1, 2):
                            if new_ref is None:
                                w_ref[p, tile(t), :] = column[a]
                            else:
                                new_ref[p, tile(t), :] = column[a] * minv[p, tile(t), :] - u[a][b]
                        else:
                            edge[2 * (group * 4 + a) + b // 3, pl.ds(pl.multiple_of(t * 8 + 8, 8), 8), :] = column[a]
            return tuple(sums)

        count = groups * (1 if old_ref is None else 2)
        sums = lax.fori_loop(0, tiles, body, (zero,) * count)

        @pl.loop(0, groups * 4)
        def _(i):
            for b, value in zip((0, 3), join_cols(i)):
                p = i * 4 + b
                if new_ref is None:
                    w_ref[p] = value
                else:
                    new_ref[p] = value * minv[p] - now_ref[p]

        return [sums[i * groups : (i + 1) * groups] for i in range(count // groups)]

    (g00,) = apply(u0_ref, None, u1_ref)
    g11, g01 = apply(u1_ref, u0_ref, u2_ref)
    g22, g12 = apply(u2_ref, u1_ref, None)
    rows = [jnp.sum(x, axis=0, keepdims=True) for q in (moments[0], g00, g01, g11, g12, g22) for x in q]
    rows += [jnp.zeros((1, LANES), jnp.float32)] * (-len(rows) % 8)
    table = jnp.concatenate(rows, axis=0)
    lanes = lax.broadcasted_iota(jnp.int32, table.shape, 1)
    lines = lax.broadcasted_iota(jnp.int32, table.shape, 0)
    table = jnp.where(lanes < own_rows // 4 * PACK, table, 0.0)
    shift = PACK
    while shift < LANES:
        table = table + pltpu.roll(table, shift, 1)
        shift *= 2
    table = jnp.where(lanes // PACK == lines, table, 0.0)
    part_ref[...] = jnp.broadcast_to(jnp.sum(table, axis=0, keepdims=True), part_ref.shape)


def combine_kernel(
    parts_ref, scale_ref, u0_ref, u1_ref, u2_ref, w_ref, mass_sum_ref, lap_sum_ref, sol_hbm, res_hbm, sol, res, xs, xt, sems
):
    halves, modes, rows, _ = sol.shape
    groups = modes // PACK
    own = rows // 4
    per_half = LANES // 4
    total = jnp.sum(parts_ref[...], axis=0, keepdims=True)
    table = jnp.broadcast_to(total, (24, LANES))
    lanes = lax.broadcasted_iota(jnp.int32, table.shape, 1)
    lines = lax.broadcasted_iota(jnp.int32, table.shape, 0)
    table = jnp.where(lanes // PACK == lines, table, 0.0)
    shift = PACK
    while shift < LANES:
        table = table + pltpu.roll(table, shift, 1)
        shift *= 2
    b0, g00, g01, g11, g12, g22 = [table[q * groups : (q + 1) * groups] for q in range(6)]
    g02 = g11
    b1 = g00 - b0
    b2 = g01 - b1
    l10 = g01 / g00
    l20 = g02 / g00
    d1 = g11 - l10 * g01
    t12 = g12 - l20 * g01
    l21 = t12 / d1
    d2 = g22 - l20 * g02 - l21 * t12
    y1 = b1 - l10 * b0
    y2 = b2 - l20 * b0 - l21 * y1
    c2 = y2 / d2
    c1 = y1 / d1 - l21 * c2
    c0 = b0 / g00 - l10 * c1 - l20 * c2
    copies = []
    for half in range(halves):
        span = slice(half * per_half, (half + 1) * per_half)
        for group in range(groups):
            k0, k1, k2 = [c[group : group + 1, :] for c in (c0, c1, c2)]
            scale = scale_ref[group : group + 1, :]
            for a in range(4):
                slot = group * 4 + a
                for b in range(4):
                    p = plane(group, a, b)
                    u0, u1, u2 = u0_ref[p, span, :], u1_ref[p, span, :], u2_ref[p, span, :]
                    diag = mass_sum_ref[a * 4 + b, span, :] + scale * lap_sum_ref[a * 4 + b, span, :]
                    xs[0, slot, pl.ds(b, per_half, stride=4), :] = k0 * u0 + k1 * u1 + k2 * u2
                    xs[1, slot, pl.ds(b, per_half, stride=4), :] = (
                        diag * (u0 - k0 * (u1 + u0) - k1 * (u2 + u1)) - k2 * w_ref[p, span, :]
                    )
                for i, out in enumerate((sol, res)):
                    xt[i, slot] = xs[i, slot].T
                    for m in range(PACK):
                        out[half, group * PACK + m, pl.ds(a, own, stride=4), :] = xt[
                            i, slot, pl.ds(m, own, stride=PACK), :
                        ]
        for i, (out, hbm) in enumerate(((sol, sol_hbm), (res, res_hbm))):
            copy = pltpu.make_async_copy(
                out.at[half], hbm.at[:, :, pl.ds(half * LANES, LANES)], sems.at[half, i]
            )
            copy.start()
            copies.append(copy)
    for copy in copies:
        copy.wait()


def shards(forcing, metric, jacobian, mode_scale):
    modes, rows, cols = forcing.shape
    groups = modes // PACK
    halo = 4 * GHOST
    f32 = jnp.float32

    def shift(x, axis, step):
        count = lax.axis_size(axis)
        return lax.ppermute(x, axis, [(i, (i + step) % count) for i in range(count)])

    def stack(span):
        return jnp.concatenate([forcing[:, span], metric[None, span], jacobian[None, span]], axis=0)

    up = shift(stack(slice(rows - halo, rows)), "curve", 1)
    down = shift(stack(slice(0, halo)), "curve", -1)

    planes = 16 * (groups + 1)
    ecols = cols // 4
    halves = cols // LANES
    per_half = LANES // 4
    whole = lambda *shape: pl.BlockSpec(shape, lambda h: (0,) * len(shape))
    spread, low, high = pl.pallas_call(
        functools.partial(spread_kernel, rows),
        grid=(halves,),
        in_specs=[
            pl.BlockSpec((modes, rows, LANES), lambda h: (0, 0, h)),
            pl.BlockSpec((rows, LANES), lambda h: (0, h)),
            pl.BlockSpec((rows, LANES), lambda h: (0, h)),
            pl.BlockSpec((modes + 2, halo, LANES), lambda h: (0, 0, h)),
            pl.BlockSpec((modes + 2, halo, LANES), lambda h: (0, 0, h)),
        ],
        out_specs=[
            pl.BlockSpec((planes, per_half, LANES), lambda h: (0, h, 0)),
            whole(planes, GHOST, LANES),
            whole(planes, GHOST, LANES),
        ],
        out_shape=[
            jax.ShapeDtypeStruct((planes, ecols, LANES), f32),
            jax.ShapeDtypeStruct((planes, GHOST, LANES), f32),
            jax.ShapeDtypeStruct((planes, GHOST, LANES), f32),
        ],
        scratch_shapes=[pltpu.VMEM((planes // 4, LANES, LANES), f32)] * 2,
        name="spread",
    )(forcing, metric, jacobian, up, down)

    left = shift(high, "sub", 1)
    right = shift(low, "sub", -1)
    scale = jnp.tile(mode_scale.reshape(groups, PACK), (1, LANES // PACK))

    total = ecols + 2 * GHOST
    state = jax.ShapeDtypeStruct((16 * groups, total, LANES), f32)
    shared = jax.ShapeDtypeStruct((16, total, LANES), f32)
    devices = lax.axis_size(AXES[0]) * lax.axis_size(AXES[1])
    vmem = pl.BlockSpec(memory_space=pltpu.VMEM)
    u0, u1, u2, w3, mass_sum, lap_sum, part = pl.pallas_call(
        functools.partial(krylov_kernel, rows),
        in_specs=[vmem] * 4,
        out_specs=[vmem] * 7,
        out_shape=[state] * 4 + [shared] * 2 + [jax.ShapeDtypeStruct((devices, LANES), f32)],
        scratch_shapes=[
            pltpu.VMEM((16, total, LANES), f32),
            pltpu.VMEM((24, total, LANES), f32),
            pltpu.VMEM((24, total, LANES), f32),
            pltpu.VMEM((16 * groups, total, LANES), f32),
            pltpu.VMEM((8 * groups, total + 16, LANES), f32),
        ],
        name="krylov",
    )(spread, right, left, scale)

    parts = lax.all_to_all(part, AXES, 0, 0, tiled=True)

    out = jax.ShapeDtypeStruct((modes, rows, cols), f32)
    anywhere = pl.BlockSpec(memory_space=pl.ANY)
    return tuple(
        pl.pallas_call(
            combine_kernel,
            in_specs=[vmem] * 8,
            out_specs=[anywhere] * 2,
            out_shape=[out] * 2,
            scratch_shapes=[
                pltpu.VMEM((halves, modes, rows, LANES), f32),
                pltpu.VMEM((halves, modes, rows, LANES), f32),
                pltpu.VMEM((2, 4 * groups, LANES, LANES), f32),
                pltpu.VMEM((2, 4 * groups, LANES, LANES), f32),
                pltpu.SemaphoreType.DMA((halves, 2)),
            ],
            name="combine",
        )(parts, scale, u0, u1, u2, w3, mass_sum, lap_sum)
    )


def solution(mesh):
    in_specs = (P(None, "curve", "sub"), P("curve", "sub"), P("curve", "sub"), P())
    out_specs = (P(None, "curve", "sub"), P(None, "curve", "sub"))
    return jax.shard_map(
        shards, mesh=mesh, in_specs=in_specs, out_specs=out_specs, check_vma=False
    )
```

time: 269 us -> 72.7 us (0.27)
  the two profiles are of different devices: /device:TPU:40 before, /device:TPU:1 now
where the time goes in v1:
time: 72.7 us; the launch traced here: 72.4 us
  blocking collectives  26.7 us (37%)
  Pallas kernels  25.4 us (35%)
  waiting for transfers between devices  9.73 us (13%)
  starting transfers between devices  5.9 us (8%)
  local copies, waits for them, and re-layouts  3.93 us (5%)
    all_to_all x1, blocking collectives, shards(): parts = lax.all_to_all(part, AXES, 0, 0, tiled=True)  26.7 us
    pallas_call x1, Pallas kernels, shards(): pl.pallas_call(functools.partial(krylov_kernel, rows), in_specs=[vmem] *...  15.7 us
    ppermute x4, waiting for transfers between devices, shift(): lax.ppermute(x, axis, [(i, (i + step) % count) for i in range(count)])  9.73 us
    pallas_call x1, Pallas kernels, shards(): pl.pallas_call(combine_kernel, in_specs=[vmem] * 8, out_specs=[anywhere]...  6.51 us
    ppermute x4, starting transfers between devices, shift(): lax.ppermute(x, axis, [(i, (i + step) % count) for i in range(count)])  5.9 us
    pallas_call x1, Pallas kernels, shards(): pl.pallas_call(functools.partial(spread_kernel, rows), grid=(halves,), in...  3.24 us
  transfers between devices with their start and end apart: 4, of which 4 were waited for; matrix products, arithmetic and copies ran while one was open for 1% of the time, Pallas kernels for 0%

profile of v1, /device:TPU:1, one launch (start us, length us, event | category | flops | bytes accessed | tf_op | source)
XLA Modules:
  0.0 72.4 jit_solution(3777404471707579008)
XLA Ops:
  0.6 0.0 copy-start.4
  0.6 1.1 %fusion = (f32[12,16,256]{2,1,0:T(8,128)S(1)}, f32[12,16,256]{2,1,0:T(8,128)S(1)}) fusion(f32[12,96,256]{2,1,0:T(8,128)} %f_ref.1), kind=kLoop, calls=%fused_computation.6 | loop fusion | bytes 786432 | tf_op jit(solution)/shard_map/slice | solution.py:382
  1.7 0.8 %slice_bitcast_fusion = (f32[1,16,256]{2,1,0:T(8,128)S(1)}, f32[1,16,256]{2,1,0:T(8,128)S(1)}, f32[1,16,256]{2,1,0:T(8,128)S(1)}, f32[1,16,256]{2,1,0:T(8,128)S(1)}) fusion(f32[96,256]{1,0:T(8,128)} %jacobian_ref.1, f32[96,256]{1,0:T(8,128)} %metric_ref.1), kind=kLoop, calls=%fused_computation.2 | loop fusion | bytes 131072 | tf_op jit(solution)/shard_map/broadcast_in_dim | solution.py:382
  2.5 3.1 %collective-permute-start = (f32[14,16,256]{2,1,0:T(8,128)S(1)}, f32[14,16,256]{2,1,0:T(8,128)S(1)}, u32[]{:S(2)}, u32[]{:S(2)}) collective-permute-start(f32[14,16,256]{2,1,0:T(8,128)S(1)} %pad_maximum_fusion), channel_id=1, source_target_pairs={{0,4},{4,8},{8,12},{12,16},{16,20},{20,24},{24,28},{28,32},{32,36}... | collective-permute-start | bytes 688136 | tf_op jit(solution)/shard_map/ppermute | solution.py:379
  5.6 0.3 collective-permute-start.1
  5.9 2.7 %collective-permute-done.up_ref = f32[14,16,256]{2,1,0:T(8,128)S(1)} collective-permute-done((f32[14,16,256]{2,1,0:T(8,128)S(1)}, f32[14,16,256]{2,1,0:T(8,128)S(1)}, u32[]{:S(2)}, u32[]{:S(2)}) %collective-permute-start) | collective-permute-done | bytes 229408 | tf_op jit(solution)/shard_map/ppermute | solution.py:379
  8.6 0.0 copy-start
  8.6 2.6 %collective-permute-done.1.down_ref = f32[14,16,256]{2,1,0:T(8,128)S(1)} collective-permute-done((f32[14,16,256]{2,1,0:T(8,128)S(1)}, f32[14,16,256]{2,1,0:T(8,128)S(1)}, u32[]{:S(2)}, u32[]{:S(2)}) %collective-permute-start.1) | collective-permute-done | bytes 229408 | tf_op jit(solution)/shard_map/ppermute | solution.py:379
  11.1 0.0 copy-done
  11.1 0.0 copy-start.1
  11.1 0.7 copy-done.1
  11.8 3.2 %spread.1 = (f32[64,64,128]{2,1,0:T(8,128)}, f32[64,4,128]{2,1,0:T(4,128)}, f32[64,4,128]{2,1,0:T(4,128)}) custom-call(f32[12,96,256]{2,1,0:T(8,128)} %f_ref.1, f32[96,256]{1,0:T(8,128)} %metric_ref.1, f32[96,256]{1,0:T(8,128)} %jacobian_ref.1, f32[14,16,256]{2,1,0:T(8,128)} %copy-done, f32[14,16,256]{2,1,0:T(8,128)} %copy-done.1), custom_call_target="tpu_custom_call" | custom-call | tf_op jit(solution)/shard_map/spread/pallas_call | solution.py:392
  15.1 2.5 %collective-permute-start.2 = (f32[64,4,128]{2,1,0:T(4,128)}, f32[64,4,128]{2,1,0:T(4,128)S(1)}, u32[]{:S(2)}, u32[]{:S(2)}) collective-permute-start(f32[64,4,128]{2,1,0:T(4,128)} %get-tuple-element.13), channel_id=1, source_target_pairs={{0,3},{1,0},{2,1},{3,2},{4,7},{5,4},{6,5},{7,6},{8,11},{9,8},{10,9... | collective-permute-start | bytes 393224 | tf_op jit(solution)/shard_map/ppermute | solution.py:379
  17.6 0.0 collective-permute-start.3
  17.6 0.0 copy-done.4
  17.6 0.1 tile.10
  17.7 0.6 tile.12.scale_ref
  18.3 1.5 %collective-permute-done.2.right_ref = f32[64,4,128]{2,1,0:T(4,128)S(1)} collective-permute-done((f32[64,4,128]{2,1,0:T(4,128)}, f32[64,4,128]{2,1,0:T(4,128)S(1)}, u32[]{:S(2)}, u32[]{:S(2)}) %collective-permute-start.2) | collective-permute-done | bytes 131104 | tf_op jit(solution)/shard_map/ppermute | solution.py:379
  19.9 0.0 copy-start.2
  19.9 3.0 %collective-permute-done.3.left_ref = f32[64,4,128]{2,1,0:T(4,128)S(1)} collective-permute-done((f32[64,4,128]{2,1,0:T(4,128)}, f32[64,4,128]{2,1,0:T(4,128)S(1)}, u32[]{:S(2)}, u32[]{:S(2)}) %collective-permute-start.3) | collective-permute-done | bytes 131104 | tf_op jit(solution)/shard_map/ppermute | solution.py:379
  22.8 0.0 copy-start.3
  22.8 0.0 copy-done.2
  22.8 0.7 copy-done.3
  23.5 15.7 %krylov.1 = (f32[48,72,128]{2,1,0:T(8,128)}, f32[48,72,128]{2,1,0:T(8,128)}, f32[48,72,128]{2,1,0:T(8,128)}, f32[48,72,128]{2,1,0:T(8,128)}, f32[16,72,128]{2,1,...) custom-call(f32[64,64,128]{2,1,0:T(8,128)} %get-tuple-element.12.t_ref, f32[64,4,128]{2,1,0:T(4,128)} %copy-done.2, ...), custom_call_target="tpu_custom_call" | custom-call | tf_op jit(solution)/shard_map/krylov/pallas_call | solution.py:425
  39.2 26.7 %all_to_all.11 = f32[256,1,128]{2,1,0:T(1,128)} all-to-all(f32[256,1,128]{2,1,0:T(1,128)} %bitcast.13), channel_id=1, replica_groups=mesh['curve'=64,'sub'=4] {'curve','sub'}, dimensions={0} | all-to-all | bytes 262144 | tf_op jit(solution)/shard_map/all_to_all | solution.py:440
  65.9 6.5 %combine.1 = (f32[12,96,256]{2,1,0:T(8,128)}, f32[12,96,256]{2,1,0:T(8,128)}) custom-call(f32[256,128]{1,0:T(8,128)} %bitcast.12, f32[3,128]{1,0:T(4,128)} %tile.12.scale_ref, f32[48,72,128]{2,1,0:T(8,128)} %get-tuple-element.16.u0_ref, f32[48,72,128]{2,1,0:T(8,128)} %get-tuple-element.17.u1_ref, f32[48,72,128]{2,1,0:T(8,128)} %get-tuple-element.18.u2_ref, ...), custom_call_target="tpu_custom_call" | custom-call | tf_op jit(solution)/shard_map/combine/pallas_call | solution.py:445
  (3 shorter events, 0.0 us)
Async XLA Ops:
  0.6 17.0 %copy-start.4 = (f32[12]{0:T(128)S(1)}, f32[12]{0:T(128)}, u32[]{:S(2)}) copy-start(f32[12]{0:T(128)} %param.7) | copy-start | bytes 148
  2.5 6.1 %collective-permute-start = (f32[14,16,256]{2,1,0:T(8,128)S(1)}, f32[14,16,256]{2,1,0:T(8,128)S(1)}, u32[]{:S(2)}, u32[]{:S(2)}) collective-permute-start(f32[14,16,256]{2,1,0:T(8,128)S(1)} %pad_maximum_fusion), channel_id=1, source_target_pairs={{0,4},{4,8},{8,12},{12,16},{16,20},{20,24},{24,28},{28,32},{32,36}... | collective-permute-start | bytes 688136 | tf_op jit(solution)/shard_map/ppermute | solution.py:379
  5.6 5.5 %collective-permute-start.1 = (f32[14,16,256]{2,1,0:T(8,128)S(1)}, f32[14,16,256]{2,1,0:T(8,128)S(1)}, u32[]{:S(2)}, u32[]{:S(2)}) collective-permute-start(f32[14,16,256]{2,1,0:T(8,128)S(1)} %pad_maximum_fusion.1), channel_id=1, source_target_pairs={{0,252},{4,0},{8,4},{12,8},{16,12},{20,16},{24,20},{28,24},{32,28}... | collective-permute-start | bytes 688136 | tf_op jit(solution)/shard_map/ppermute | solution.py:379
  8.6 2.6 %copy-start = (f32[14,16,256]{2,1,0:T(8,128)}, f32[14,16,256]{2,1,0:T(8,128)S(1)}, u32[]{:S(2)}) copy-start(f32[14,16,256]{2,1,0:T(8,128)S(1)} %collective-permute-done.up_ref) | copy-start | bytes 688132
  11.1 0.7 copy-start.1
  15.1 4.8 %collective-permute-start.2 = (f32[64,4,128]{2,1,0:T(4,128)}, f32[64,4,128]{2,1,0:T(4,128)S(1)}, u32[]{:S(2)}, u32[]{:S(2)}) collective-permute-start(f32[64,4,128]{2,1,0:T(4,128)} %get-tuple-element.13), channel_id=1, source_target_pairs={{0,3},{1,0},{2,1},{3,2},{4,7},{5,4},{6,5},{7,6},{8,11},{9,8},{10,9... | collective-permute-start | bytes 393224 | tf_op jit(solution)/shard_map/ppermute | solution.py:379
  17.6 5.2 %collective-permute-start.3 = (f32[64,4,128]{2,1,0:T(4,128)}, f32[64,4,128]{2,1,0:T(4,128)S(1)}, u32[]{:S(2)}, u32[]{:S(2)}) collective-permute-start(f32[64,4,128]{2,1,0:T(4,128)} %get-tuple-element.14), channel_id=1, source_target_pairs={{0,1},{1,2},{2,3},{3,0},{4,5},{5,6},{6,7},{7,4},{8,9},{9,10},{10,1... | collective-permute-start | bytes 393224 | tf_op jit(solution)/shard_map/ppermute | solution.py:379
  19.9 3.0 %copy-start.2 = (f32[64,4,128]{2,1,0:T(4,128)}, f32[64,4,128]{2,1,0:T(4,128)S(1)}, u32[]{:S(2)}) copy-start(f32[64,4,128]{2,1,0:T(4,128)S(1)} %collective-permute-done.2.right_ref) | copy-start | bytes 393220
  22.8 0.7 copy-start.3

commit v2 on v1

--- a/solution.py
+++ b/solution.py
@@ -36,6 +36,23 @@
 
 def plane(group, a, b):
     return (group * 4 + a) * 4 + b
+
+
+def strips_kernel(f_hbm, metric_hbm, jacobian_hbm, top, bottom, sems):
+    modes, rows, _ = f_hbm.shape
+    halo = top.shape[1]
+    copies = []
+    for side, (out, at) in enumerate(((top, 0), (bottom, rows - halo))):
+        span = pl.ds(at, halo)
+        copies += [
+            pltpu.make_async_copy(f_hbm.at[:, span, :], out.at[pl.ds(0, modes)], sems.at[side, 0]),
+            pltpu.make_async_copy(metric_hbm.at[span, :], out.at[modes], sems.at[side, 1]),
+            pltpu.make_async_copy(jacobian_hbm.at[span, :], out.at[modes + 1], sems.at[side, 2]),
+        ]
+    for copy in copies:
+        copy.start()
+    for copy in copies:
+        copy.wait()
 
 
 def spread_kernel(rows, f_ref, metric_ref, jacobian_ref, up_ref, down_ref, t_ref, low_ref, high_ref, xs, xt):
@@ -378,11 +395,18 @@
         count = lax.axis_size(axis)
         return lax.ppermute(x, axis, [(i, (i + step) % count) for i in range(count)])
 
-    def stack(span):
-        return jnp.concatenate([forcing[:, span], metric[None, span], jacobian[None, span]], axis=0)
-
-    up = shift(stack(slice(rows - halo, rows)), "curve", 1)
-    down = shift(stack(slice(0, halo)), "curve", -1)
+    vmem = pl.BlockSpec(memory_space=pltpu.VMEM)
+    anywhere = pl.BlockSpec(memory_space=pl.ANY)
+    top, bottom = pl.pallas_call(
+        strips_kernel,
+        in_specs=[anywhere] * 3,
+        out_specs=[vmem] * 2,
+        out_shape=[jax.ShapeDtypeStruct((modes + 2, halo, cols), f32)] * 2,
+        scratch_shapes=[pltpu.SemaphoreType.DMA((2, 3))],
+        name="strips",
+    )(forcing, metric, jacobian)
+    up = shift(bottom, "curve", 1)
+    down = shift(top, "curve", -1)
 
     planes = 16 * (groups + 1)
     ecols = cols // 4
@@ -410,6 +434,7 @@
             jax.ShapeDtypeStruct((planes, GHOST, LANES), f32),
         ],
         scratch_shapes=[pltpu.VMEM((planes // 4, LANES, LANES), f32)] * 2,
+        compiler_params=pltpu.CompilerParams(vmem_limit_bytes=12 << 20),
         name="spread",
     )(forcing, metric, jacobian, up, down)
 
@@ -421,7 +446,6 @@
     state = jax.ShapeDtypeStruct((16 * groups, total, LANES), f32)
     shared = jax.ShapeDtypeStruct((16, total, LANES), f32)
     devices = lax.axis_size(AXES[0]) * lax.axis_size(AXES[1])
-    vmem = pl.BlockSpec(memory_space=pltpu.VMEM)
     u0, u1, u2, w3, mass_sum, lap_sum, part = pl.pallas_call(
         functools.partial(krylov_kernel, rows),
         in_specs=[vmem] * 4,
@@ -434,13 +458,13 @@
             pltpu.VMEM((16 * groups, total, LANES), f32),
             pltpu.VMEM((8 * groups, total + 16, LANES), f32),
         ],
+        compiler_params=pltpu.CompilerParams(vmem_limit_bytes=24 << 20),
         name="krylov",
     )(spread, right, left, scale)
 
     parts = lax.all_to_all(part, AXES, 0, 0, tiled=True)
 
     out = jax.ShapeDtypeStruct((modes, rows, cols), f32)
-    anywhere = pl.BlockSpec(memory_space=pl.ANY)
     return tuple(
         pl.pallas_call(
             combine_kernel,
@@ -454,6 +478,7 @@
                 pltpu.VMEM((2, 4 * groups, LANES, LANES), f32),
                 pltpu.SemaphoreType.DMA((halves, 2)),
             ],
+            compiler_params=pltpu.CompilerParams(vmem_limit_bytes=20 << 20),
             name="combine",
         )(parts, scale, u0, u1, u2, w3, mass_sum, lap_sum)
     )

time: 72.7 us -> 62.1 us (0.85)
  Pallas kernels: 25.4 us -> 17.5 us
  local copies, waits for them, and re-layouts: 3.93 us -> 1.99 us
  blocking collectives: 26.7 us -> 25.6 us
    pallas_call x1, Pallas kernels: 15.7 us -> 11.1 us  [shards(): pl.pallas_call(functools.partial(krylov_kernel, rows), in_specs=[vmem] *...]
    pallas_call x1, Pallas kernels: 6.51 us -> 3.24 us  [shards(): pl.pallas_call(combine_kernel, in_specs=[vmem] * 8, out_specs=[anywhere]...]
    pallas_call x1, Pallas kernels: 3.24 us -> 1.22 us  [shards(): pl.pallas_call(functools.partial(spread_kernel, rows), grid=(halves,), in...]
    pallas_call x0 -> x1, Pallas kernels: none -> 1.97 us  [shards(): pl.pallas_call(strips_kernel, in_specs=[anywhere] * 3, out_specs=[vmem] *...]
    all_to_all x1, blocking collectives: 26.7 us -> 25.6 us  [shards(): parts = lax.all_to_all(part, AXES, 0, 0, tiled=True)]
    slice x1 -> x0, local copies, waits for them, and re-layouts: 1.06 us -> none  [stack(): forcing[:, span]]
    broadcast_in_dim x1 -> x0, local copies, waits for them, and re-layouts: 0.78 us -> none  [stack(): jacobian[None, span]]
    unnamed x10 -> x8, local copies, waits for them, and re-layouts: 1.35 us -> 1.79 us
  transfers between devices with their start and end apart: 4 -> 4, of which waited for: 4 -> 4; matrix products, arithmetic and copies ran while one was open for 1% -> 0% of each run, Pallas kernels for 0% -> 0%
where the time goes in v2:
time: 62.1 us; the launch traced here: 61.9 us
  blocking collectives  25.6 us (41%)
  Pallas kernels  17.5 us (28%)
  waiting for transfers between devices  10.2 us (16%)
  starting transfers between devices  5.93 us (10%)
  local copies, waits for them, and re-layouts  1.99 us (3%)
  between operations  0.67 us (1%)
    all_to_all x1, blocking collectives, shards(): parts = lax.all_to_all(part, AXES, 0, 0, tiled=True)  25.6 us
    pallas_call x1, Pallas kernels, shards(): pl.pallas_call(functools.partial(krylov_kernel, rows), in_specs=[vmem] *...  11.1 us
    ppermute x4, waiting for transfers between devices, shift(): lax.ppermute(x, axis, [(i, (i + step) % count) for i in range(count)])  10.2 us
    ppermute x4, starting transfers between devices, shift(): lax.ppermute(x, axis, [(i, (i + step) % count) for i in range(count)])  5.93 us
    pallas_call x1, Pallas kernels, shards(): pl.pallas_call(combine_kernel, in_specs=[vmem] * 8, out_specs=[anywhere]...  3.24 us
    pallas_call x1, Pallas kernels, shards(): pl.pallas_call(strips_kernel, in_specs=[anywhere] * 3, out_specs=[vmem] *...  1.97 us
    unnamed x8, local copies, waits for them, and re-layouts  1.79 us
  transfers between devices with their start and end apart: 4, of which 4 were waited for; matrix products, arithmetic and copies ran while one was open for 0% of the time, Pallas kernels for 0%

profile of v2, /device:TPU:1, one launch (start us, length us, event | category | flops | bytes accessed | tf_op | source)
XLA Modules:
  0.0 61.9 jit_solution(17756284569488638337)
XLA Ops:
  0.6 0.0 copy-start
  0.6 0.0 copy-start.3
  0.6 2.0 %strips.1 = (f32[14,16,256]{2,1,0:T(8,128)}, f32[14,16,256]{2,1,0:T(8,128)}) custom-call(f32[12,96,256]{2,1,0:T(8,128)} %f_ref.1, f32[96,256]{1,0:T(8,128)} %metric_ref.1, f32[96,256]{1,0:T(8,128)} %jacobian_ref.1), custom_call_target="tpu_custom_call" | custom-call | tf_op jit(solution)/shard_map/strips/pallas_call | solution.py:400
  2.6 3.1 %collective-permute-start = (f32[14,16,256]{2,1,0:T(8,128)}, f32[14,16,256]{2,1,0:T(8,128)S(1)}, u32[]{:S(2)}, u32[]{:S(2)}) collective-permute-start(f32[14,16,256]{2,1,0:T(8,128)} %get-tuple-element.14), channel_id=1, source_target_pairs={{0,4},{4,8},{8,12},{12,16},{16,20},{20,24},{24,28},{28,32},{32,36}... | collective-permute-start | bytes 688136 | tf_op jit(solution)/shard_map/ppermute | solution.py:396
  5.7 0.3 collective-permute-start.1
  6.0 3.0 %collective-permute-done.up_ref = f32[14,16,256]{2,1,0:T(8,128)S(1)} collective-permute-done((f32[14,16,256]{2,1,0:T(8,128)}, f32[14,16,256]{2,1,0:T(8,128)S(1)}, u32[]{:S(2)}, u32[]{:S(2)}) %collective-permute-start) | collective-permute-done | bytes 229408 | tf_op jit(solution)/shard_map/ppermute | solution.py:396
  9.0 2.4 %collective-permute-done.1.down_ref = f32[14,16,256]{2,1,0:T(8,128)S(1)} collective-permute-done((f32[14,16,256]{2,1,0:T(8,128)}, f32[14,16,256]{2,1,0:T(8,128)S(1)}, u32[]{:S(2)}, u32[]{:S(2)}) %collective-permute-start.1) | collective-permute-done | bytes 229408 | tf_op jit(solution)/shard_map/ppermute | solution.py:396
  11.4 0.0 copy-done
  11.4 0.0 copy-start.1
  11.4 0.9 %copy-done.1 = f32[96,256]{1,0:T(8,128)S(1)} copy-done((f32[96,256]{1,0:T(8,128)S(1)}, f32[96,256]{1,0:T(8,128)}, u32[]{:S(2)}) %copy-start.1) | copy-done | bytes 98328
  12.3 0.0 copy-start.2
  12.3 0.9 %copy-done.2 = f32[96,256]{1,0:T(8,128)S(1)} copy-done((f32[96,256]{1,0:T(8,128)S(1)}, f32[96,256]{1,0:T(8,128)}, u32[]{:S(2)}) %copy-start.2) | copy-done | bytes 98328
  13.2 1.2 %spread.1 = (f32[64,64,128]{2,1,0:T(8,128)S(1)}, f32[64,4,128]{2,1,0:T(4,128)S(1)}, f32[64,4,128]{2,1,0:T(4,128)S(1)}) custom-call(f32[12,96,256]{2,1,0:T(8,128)S(1)} %copy-done, f32[96,256]{1,0:T(8,128)S(1)} %copy-done.1, f32[96,256]{1,0:T(8,128)S(1)} %copy-done.2, f32[14,16,256]{2,1,0:T(8,128)S(1)} %collective-permute-done.up_ref, ...), custom_call_target="tpu_custom_call" | custom-call | tf_op jit(solution)/shard_map/spread/pallas_call | solution.py:416
  14.4 2.6 %collective-permute-start.2 = (f32[64,4,128]{2,1,0:T(4,128)S(1)}, f32[64,4,128]{2,1,0:T(4,128)S(1)}, u32[]{:S(2)}, u32[]{:S(2)}) collective-permute-start(f32[64,4,128]{2,1,0:T(4,128)S(1)} %get-tuple-element.17), channel_id=1, source_target_pairs={{0,3},{1,0},{2,1},{3,2},{4,7},{5,4},{6,5},{7,6},{8,11},{9,8},{10,9... | collective-permute-start | bytes 393224 | tf_op jit(solution)/shard_map/ppermute | solution.py:396
  16.9 0.0 collective-permute-start.3
  17.0 0.0 copy-done.3
  17.0 0.1 tile.10
  17.0 0.1 tile.12.scale_ref
  17.2 1.7 %collective-permute-done.2.right_ref = f32[64,4,128]{2,1,0:T(4,128)S(1)} collective-permute-done((f32[64,4,128]{2,1,0:T(4,128)S(1)}, f32[64,4,128]{2,1,0:T(4,128)S(1)}, u32[]{:S(2)}, u32[]{:S(2)}) %collective-permute-start.2) | collective-permute-done | bytes 131104 | tf_op jit(solution)/shard_map/ppermute | solution.py:396
  18.9 3.1 %collective-permute-done.3.left_ref = f32[64,4,128]{2,1,0:T(4,128)S(1)} collective-permute-done((f32[64,4,128]{2,1,0:T(4,128)S(1)}, f32[64,4,128]{2,1,0:T(4,128)S(1)}, u32[]{:S(2)}, u32[]{:S(2)}) %collective-permute-start.3) | collective-permute-done | bytes 131104 | tf_op jit(solution)/shard_map/ppermute | solution.py:396
  22.0 11.1 %krylov.1 = (f32[48,72,128]{2,1,0:T(8,128)S(1)}, f32[48,72,128]{2,1,0:T(8,128)S(1)}, f32[48,72,128]{2,1,0:T(8,128)S(1)}, f32[48,72,128]{2,1,0:T(8,128)S(1)}, f32...) custom-call(f32[64,64,128]{2,1,0:T(8,128)S(1)} %get-tuple-element.16.t_ref, ...), custom_call_target="tpu_custom_call" | custom-call | tf_op jit(solution)/shard_map/krylov/pallas_call | solution.py:449
  33.0 25.6 %all_to_all.11 = f32[256,1,128]{2,1,0:T(1,128)S(1)} all-to-all(f32[256,1,128]{2,1,0:T(1,128)S(1)} %bitcast.5), channel_id=1, replica_groups=mesh['curve'=64,'sub'=4] {'curve','sub'}, dimensions={0} | all-to-all | bytes 262144 | tf_op jit(solution)/shard_map/all_to_all | solution.py:465
  58.7 3.2 %combine.1 = (f32[12,96,256]{2,1,0:T(8,128)}, f32[12,96,256]{2,1,0:T(8,128)}) custom-call(f32[256,128]{1,0:T(8,128)S(1)} %bitcast.4, f32[3,128]{1,0:T(4,128)S(1)} %tile.12.scale_ref, f32[48,72,128]{2,1,0:T(8,128)S(1)} %get-tuple-element.20.u0_ref, f32[48,72,128]{2,1,0:T(8,128)S(1)} %get-tuple-element.21.u1_ref, f32[48,72,128]{2,1,0:T(8,128)S(1)} %get-tuple-element.22.u2_ref, ...), custom_call_target="tpu_custom_call" | custom-call | tf_op jit(solution)/shard_map/combine/pallas_call | solution.py:469
  (1 shorter events, 0.0 us)
Async XLA Ops:
  0.6 10.7 %copy-start = (f32[12,96,256]{2,1,0:T(8,128)S(1)}, f32[12,96,256]{2,1,0:T(8,128)}, u32[]{:S(2)}) copy-start(f32[12,96,256]{2,1,0:T(8,128)} %f_ref.1) | copy-start | bytes 3538948
  0.6 16.3 %copy-start.3 = (f32[12]{0:T(128)S(1)}, f32[12]{0:T(128)}, u32[]{:S(2)}) copy-start(f32[12]{0:T(128)} %param.7) | copy-start | bytes 148
  2.6 6.4 %collective-permute-start = (f32[14,16,256]{2,1,0:T(8,128)}, f32[14,16,256]{2,1,0:T(8,128)S(1)}, u32[]{:S(2)}, u32[]{:S(2)}) collective-permute-start(f32[14,16,256]{2,1,0:T(8,128)} %get-tuple-element.14), channel_id=1, source_target_pairs={{0,4},{4,8},{8,12},{12,16},{16,20},{20,24},{24,28},{28,32},{32,36}... | collective-permute-start | bytes 688136 | tf_op jit(solution)/shard_map/ppermute | solution.py:396
  5.7 5.7 %collective-permute-start.1 = (f32[14,16,256]{2,1,0:T(8,128)}, f32[14,16,256]{2,1,0:T(8,128)S(1)}, u32[]{:S(2)}, u32[]{:S(2)}) collective-permute-start(f32[14,16,256]{2,1,0:T(8,128)} %get-tuple-element.15), channel_id=1, source_target_pairs={{0,252},{4,0},{8,4},{12,8},{16,12},{20,16},{24,20},{28,24},{32,28}... | collective-permute-start | bytes 688136 | tf_op jit(solution)/shard_map/ppermute | solution.py:396
  11.4 0.9 %copy-start.1 = (f32[96,256]{1,0:T(8,128)S(1)}, f32[96,256]{1,0:T(8,128)}, u32[]{:S(2)}) copy-start(f32[96,256]{1,0:T(8,128)} %metric_ref.1) | copy-start | bytes 294916
  12.3 0.9 %copy-start.2 = (f32[96,256]{1,0:T(8,128)S(1)}, f32[96,256]{1,0:T(8,128)}, u32[]{:S(2)}) copy-start(f32[96,256]{1,0:T(8,128)} %jacobian_ref.1) | copy-start | bytes 294916
  14.4 4.5 %collective-permute-start.2 = (f32[64,4,128]{2,1,0:T(4,128)S(1)}, f32[64,4,128]{2,1,0:T(4,128)S(1)}, u32[]{:S(2)}, u32[]{:S(2)}) collective-permute-start(f32[64,4,128]{2,1,0:T(4,128)S(1)} %get-tuple-element.17), channel_id=1, source_target_pairs={{0,3},{1,0},{2,1},{3,2},{4,7},{5,4},{6,5},{7,6},{8,11},{9,8},{10,9... | collective-permute-start | bytes 393224 | tf_op jit(solution)/shard_map/ppermute | solution.py:396
  16.9 5.0 %collective-permute-start.3 = (f32[64,4,128]{2,1,0:T(4,128)S(1)}, f32[64,4,128]{2,1,0:T(4,128)S(1)}, u32[]{:S(2)}, u32[]{:S(2)}) collective-permute-start(f32[64,4,128]{2,1,0:T(4,128)S(1)} %get-tuple-element.18), channel_id=1, source_target_pairs={{0,1},{1,2},{2,3},{3,0},{4,5},{5,6},{6,7},{7,4},{8,9},{9,10},{10,1... | collective-permute-start | bytes 393224 | tf_op jit(solution)/shard_map/ppermute | solution.py:396

commit v3 on v2

v3 whole, which is shorter than its diff:
```python
import functools
import math

import jax
import jax.numpy as jnp
import numpy as np
from jax import lax
from jax.experimental import pallas as pl
from jax.experimental.pallas import tpu as pltpu
from jax.sharding import PartitionSpec as P

GHOST = 4
PACK = 4
LANES = 128
AXES = ("curve", "sub")


def gll_tables():
    points = np.array([-1.0, -1.0 / math.sqrt(5.0), 1.0 / math.sqrt(5.0), 1.0])
    weights = np.array([1.0 / 6.0, 5.0 / 6.0, 5.0 / 6.0, 1.0 / 6.0])
    factor = np.array(
        [np.prod([points[j] - points[m] for m in range(4) if m != j]) for j in range(4)]
    )
    slopes = np.zeros((4, 4))
    for i in range(4):
        for j in range(4):
            if i != j:
                slopes[i, j] = factor[i] / (factor[j] * (points[i] - points[j]))
        slopes[i, i] = sum((1.0 / (points[i] - points[m]) for m in range(4) if m != i))
    return (slopes, weights)


SLOPES, WEIGHTS = gll_tables()
PAIRS = [(a, k) for a in range(4) for k in range(a + 1, 4)]


def plane(group, a, b):
    return (group * 4 + a) * 4 + b


def strips_kernel(f_hbm, metric_hbm, jacobian_hbm, top, bottom, shared, sems):
    modes, rows, _ = f_hbm.shape
    halo = top.shape[1]
    copies = []
    for side, (out, at) in enumerate(((top, 0), (bottom, rows - halo))):
        span = pl.ds(at, halo)
        copies += [
            pltpu.make_async_copy(f_hbm.at[:, span, :], out.at[pl.ds(0, modes)], sems.at[side, 0]),
            pltpu.make_async_copy(metric_hbm.at[span, :], out.at[modes], sems.at[side, 1]),
            pltpu.make_async_copy(jacobian_hbm.at[span, :], out.at[modes + 1], sems.at[side, 2]),
        ]
    copies += [
        pltpu.make_async_copy(metric_hbm, shared.at[0], sems.at[2, 0]),
        pltpu.make_async_copy(jacobian_hbm, shared.at[1], sems.at[2, 1]),
    ]
    for copy in copies:
        copy.start()
    for copy in copies:
        copy.wait()


def spread_kernel(rows, f_ref, shared_ref, up_ref, down_ref, t_ref, low_ref, high_ref, xs, xt):
    half = pl.program_id(0)
    own = rows // 4
    groups = f_ref.shape[0] // PACK
    per_half = LANES // 4
    for group in range(groups + 1):
        for a in range(4):
            at = group * 4 + a
            for m in range(PACK):
                if group < groups:
                    index = group * PACK + m
                    mine = f_ref[index, pl.ds(a, own, stride=4), :]
                else:
                    index = groups * PACK + m % 2
                    mine = shared_ref[m % 2, pl.ds(a, own, stride=4), :]
                xs[at, pl.ds(m, own, stride=PACK), :] = mine
                xs[at, pl.ds(own * PACK + m, GHOST, stride=PACK), :] = down_ref[
                    index, pl.ds(a, GHOST, stride=4), :
                ]
                xs[at, pl.ds((own + GHOST) * PACK + m, GHOST, stride=PACK), :] = up_ref[
                    index, pl.ds(a, GHOST, stride=4), :
                ]
            xt[at] = xs[at].T
            for b in range(4):
                t_ref[at * 4 + b] = xt[at, pl.ds(b, per_half, stride=4), :]

    @pl.when(half == 0)
    def _():
        for p in range(t_ref.shape[0]):
            low_ref[p] = t_ref[p, :GHOST, :]

    @pl.when(half == pl.num_programs(0) - 1)
    def _():
        for p in range(t_ref.shape[0]):
            high_ref[p] = t_ref[p, per_half - GHOST :, :]


def line_operator(coefs, values):
    f01, f02, f03, f12, f13, f23 = [
        coef * (values[k] - values[a]) for (a, k), coef in zip(PAIRS, coefs)
    ]
    return f01 + f02 + f03, f12 + f13 - f01, f23 - f02 - f12, f03 + f13 + f23


def tile(t):
    return pl.ds(pl.multiple_of(t * 8, 8), 8)


def spare(t):
    return pl.ds(pl.multiple_of(t * 8 + 8, 8), 8)


def join_rows(first, last):
    shared = last + pltpu.roll(first, LANES - PACK, 1)
    return pltpu.roll(shared, PACK, 1), shared


def join_cols(edge, i, total):
    edge[2 * i, total + 8 : total + 16, :] = edge[2 * i, 8:16, :]
    edge[2 * i + 1, 0:8, :] = edge[2 * i + 1, total : total + 8, :]
    first = edge[2 * i, 8 : total + 8, :] + edge[2 * i + 1, 7 : total + 7, :]
    last = edge[2 * i + 1, 8 : total + 8, :] + edge[2 * i, 9 : total + 9, :]
    return first, last


def prepare(t, fetch, scale_ref, mass_ref, krow, kcol, mass_sum_ref, lap_sum_ref, minv, u0_ref, source_ref, cedge, redge):
    groups = u0_ref.shape[0] // 16
    lane = lax.broadcasted_iota(jnp.int32, (8, LANES), 1)
    even = lane % 2 == 0
    grid = [(a, b) for a in range(4) for b in range(4)]
    scales = [scale_ref[group : group + 1, :] for group in range(groups)]
    flux, mass, lap = {}, {}, {}
    for a, b in grid:
        x = fetch(plane(groups, a, b))
        w = np.float32(WEIGHTS[a] * WEIGHTS[b])
        flux[a, b] = jnp.where(even, x, pltpu.roll(x, 1, 1)) * w
        mass[a, b] = jnp.where(even, pltpu.roll(x, LANES - 1, 1), x) * w
    for group in range(groups):
        inverse = 1.0 / scales[group]
        for a, b in grid:
            mass_ref[plane(group, a, b), tile(t), :] = mass[a, b] * inverse
            source_ref[plane(group, a, b), tile(t), :] = fetch(plane(group, a, b)) * mass[a, b]

    def less(a, b, value):
        lap[a, b] = lap[a, b] + value if (a, b) in lap else value

    for line in range(4):
        for i, (p, q) in enumerate(PAIRS):
            c = [np.float32(SLOPES[j, p] * SLOPES[j, q]) for j in range(4)]
            kr = sum(flux[j, line] * c[j] for j in range(4))
            kc = sum(flux[line, j] * c[j] for j in range(4))
            krow[line * 6 + i, tile(t), :] = kr
            kcol[line * 6 + i, tile(t), :] = kc
            less(p, line, kr)
            less(q, line, kr)
            less(line, p, kc)
            less(line, q, kc)
    for a, b in grid:
        lap[a, b] = -lap[a, b]
    for values, out, base in ((mass, mass_sum_ref, 0), (lap, lap_sum_ref, 4)):
        for b in range(4):
            values[0, b], values[3, b] = join_rows(values[0, b], values[3, b])
            for a in range(4):
                if b in (1, 2):
                    out[a * 4 + b, tile(t), :] = values[a, b]
                else:
                    cedge[2 * (base + a) + b // 3, spare(t), :] = values[a, b]
    for group in range(groups):
        for b in range(4):
            column = [source_ref[plane(group, a, b), tile(t), :] for a in range(4)]
            column[0], column[3] = join_rows(column[0], column[3])
            for a in range(4):
                p = plane(group, a, b)
                if b in (1, 2):
                    inverse = 1.0 / (mass[a, b] + scales[group] * lap[a, b])
                    u0_ref[p, tile(t), :] = column[a] * inverse
                    minv[p, tile(t), :] = inverse * scales[group]
                else:
                    redge[2 * (group * 4 + a) + b // 3, spare(t), :] = column[a]


def prep_kernel(t_ref, scale_ref, *refs):
    @pl.loop(0, t_ref.shape[1] // 8)
    def _(t):
        prepare(t, lambda p: t_ref[p, tile(t), :], scale_ref, *refs)


def krylov_kernel(own_rows, cols, right_ref, left_ref, scale_ref, *refs):
    state = refs[10:20]
    u1_ref, u2_ref, part_ref, edge = refs[20:]
    mass_ref, krow, kcol, mass_sum_ref, lap_sum_ref, minv, u0_ref, w_ref, cedge, redge = state
    groups = u0_ref.shape[0] // 16
    total = u0_ref.shape[1]
    tiles = total // 8
    own_tiles = cols // 8
    scales = [scale_ref[group : group + 1, :] for group in range(groups)]
    prepare(
        own_tiles, lambda p: jnp.concatenate([right_ref[p], left_ref[p]], axis=0), scale_ref, *state
    )

    @pl.loop(0, 4)
    def _(a):
        mass_sums = join_cols(cedge, a, total)
        lap_sums = join_cols(cedge, 4 + a, total)
        for side, b in enumerate((0, 3)):
            mass_sum_ref[a * 4 + b] = mass_sums[side]
            lap_sum_ref[a * 4 + b] = lap_sums[side]
        for group in range(groups):
            source = join_cols(redge, group * 4 + a, total)
            for side, b in enumerate((0, 3)):
                inverse = 1.0 / (mass_sums[side] + scales[group] * lap_sums[side])
                u0_ref[plane(group, a, b)] = source[side] * inverse
                minv[plane(group, a, b)] = inverse * scales[group]

    zero = jnp.zeros((8, LANES), jnp.float32)

    def apply(now_ref, old_ref, new_ref):
        def body(t, sums):
            sums = list(sums)
            own = (t < own_tiles).astype(jnp.float32)
            for group in range(groups):
                u = [[now_ref[plane(group, a, b), tile(t), :] for b in range(4)] for a in range(4)]
                along_rows = [
                    line_operator(
                        [krow[line * 6 + i, tile(t), :] for i in range(6)],
                        [u[a][line] for a in range(4)],
                    )
                    for line in range(4)
                ]
                along_cols = [
                    line_operator([kcol[line * 6 + i, tile(t), :] for i in range(6)], u[line])
                    for line in range(4)
                ]
                with_now, with_old = zero, zero
                y = [[None] * 4 for _ in range(4)]
                for a in range(4):
                    for b in range(4):
                        p = plane(group, a, b)
                        value = mass_ref[p, tile(t), :] * u[a][b]
                        row, col = along_rows[b][a], along_cols[a][b]
                        value = value - row if a == 3 else value + row
                        value = value - col if b == 3 else value + col
                        y[a][b] = value
                        with_now += u[a][b] * value
                        if old_ref is None:
                            with_old += w_ref[p, tile(t), :] * u[a][b]
                        else:
                            with_old += old_ref[p, tile(t), :] * value
                sums[group] += own * with_now
                sums[groups + group] += own * with_old
                for b in range(4):
                    column = [y[a][b] for a in range(4)]
                    column[0], column[3] = join_rows(column[0], column[3])
                    for a in range(4):
                        p = plane(group, a, b)
                        if b in (1, 2):
                            if new_ref is None:
                                w_ref[p, tile(t), :] = column[a]
                            else:
                                new_ref[p, tile(t), :] = column[a] * minv[p, tile(t), :] - u[a][b]
                        else:
                            edge[2 * (group * 4 + a) + b // 3, spare(t), :] = column[a]
            return tuple(sums)

        sums = lax.fori_loop(0, tiles, body, (zero,) * (2 * groups))

        @pl.loop(0, groups * 4)
        def _(i):
            for b, value in zip((0, 3), join_cols(edge, i, total)):
                p = i * 4 + b
                if new_ref is None:
                    w_ref[p] = value
                else:
                    new_ref[p] = value * minv[p] - now_ref[p]

        return sums[:groups], sums[groups:]

    g00, b0 = apply(u0_ref, None, u1_ref)
    g11, g01 = apply(u1_ref, u0_ref, u2_ref)
    g22, g12 = apply(u2_ref, u1_ref, None)
    rows = [jnp.sum(x, axis=0, keepdims=True) for x in b0]
    for q in (g00, g01, g11, g12, g22):
        rows += [scale * jnp.sum(x, axis=0, keepdims=True) for scale, x in zip(scales, q)]
    rows += [jnp.zeros((1, LANES), jnp.float32)] * (-len(rows) % 8)
    table = jnp.concatenate(rows, axis=0)
    lanes = lax.broadcasted_iota(jnp.int32, table.shape, 1)
    lines = lax.broadcasted_iota(jnp.int32, table.shape, 0)
    table = jnp.where(lanes < own_rows // 4 * PACK, table, 0.0)
    shift = PACK
    while shift < LANES:
        table = table + pltpu.roll(table, shift, 1)
        shift *= 2
    table = jnp.where(lanes // PACK == lines, table, 0.0)
    part_ref[...] = jnp.broadcast_to(jnp.sum(table, axis=0, keepdims=True), part_ref.shape)


def combine_kernel(
    parts_ref, scale_ref, u0_ref, u1_ref, u2_ref, w_ref, mass_sum_ref, lap_sum_ref, sol_hbm, res_hbm, sol, res, xs, xt, sems
):
    halves, modes, rows, _ = sol.shape
    groups = modes // PACK
    own = rows // 4
    per_half = LANES // 4
    total = jnp.sum(parts_ref[...], axis=0, keepdims=True)
    table = jnp.broadcast_to(total, (24, LANES))
    lanes = lax.broadcasted_iota(jnp.int32, table.shape, 1)
    lines = lax.broadcasted_iota(jnp.int32, table.shape, 0)
    table = jnp.where(lanes // PACK == lines, table, 0.0)
    shift = PACK
    while shift < LANES:
        table = table + pltpu.roll(table, shift, 1)
        shift *= 2
    b0, g00, g01, g11, g12, g22 = [table[q * groups : (q + 1) * groups] for q in range(6)]
    g02 = g11
    b1 = g00 - b0
    b2 = g01 - b1
    l10 = g01 / g00
    l20 = g02 / g00
    d1 = g11 - l10 * g01
    t12 = g12 - l20 * g01
    l21 = t12 / d1
    d2 = g22 - l20 * g02 - l21 * t12
    y1 = b1 - l10 * b0
    y2 = b2 - l20 * b0 - l21 * y1
    c2 = y2 / d2
    c1 = y1 / d1 - l21 * c2
    c0 = b0 / g00 - l10 * c1 - l20 * c2
    copies = []
    for half in range(halves):
        span = slice(half * per_half, (half + 1) * per_half)
        for group in range(groups):
            k0, k1, k2 = [c[group : group + 1, :] for c in (c0, c1, c2)]
            scale = scale_ref[group : group + 1, :]
            for a in range(4):
                slot = group * 4 + a
                for b in range(4):
                    p = plane(group, a, b)
                    u0, u1, u2 = u0_ref[p, span, :], u1_ref[p, span, :], u2_ref[p, span, :]
                    diag = mass_sum_ref[a * 4 + b, span, :] + scale * lap_sum_ref[a * 4 + b, span, :]
                    xs[0, slot, pl.ds(b, per_half, stride=4), :] = k0 * u0 + k1 * u1 + k2 * u2
                    xs[1, slot, pl.ds(b, per_half, stride=4), :] = (
                        diag * (u0 - k0 * (u1 + u0) - k1 * (u2 + u1)) - (k2 * scale) * w_ref[p, span, :]
                    )
                for i, out in enumerate((sol, res)):
                    xt[i, slot] = xs[i, slot].T
                    for m in range(PACK):
                        out[half, group * PACK + m, pl.ds(a, own, stride=4), :] = xt[
                            i, slot, pl.ds(m, own, stride=PACK), :
                        ]
        for i, (out, hbm) in enumerate(((sol, sol_hbm), (res, res_hbm))):
            copy = pltpu.make_async_copy(
                out.at[half], hbm.at[:, :, pl.ds(half * LANES, LANES)], sems.at[half, i]
            )
            copy.start()
            copies.append(copy)
    for copy in copies:
        copy.wait()


def shards(forcing, metric, jacobian, mode_scale):
    modes, rows, cols = forcing.shape
    groups = modes // PACK
    halo = 4 * GHOST
    f32 = jnp.float32

    def shift(x, axis, step):
        count = lax.axis_size(axis)
        return lax.ppermute(x, axis, [(i, (i + step) % count) for i in range(count)])

    vmem = pl.BlockSpec(memory_space=pltpu.VMEM)
    anywhere = pl.BlockSpec(memory_space=pl.ANY)
    hbm = pl.BlockSpec(memory_space=pltpu.HBM)
    top, bottom, shared = pl.pallas_call(
        strips_kernel,
        in_specs=[hbm] * 3,
        out_specs=[vmem] * 3,
        out_shape=[jax.ShapeDtypeStruct((modes + 2, halo, cols), f32)] * 2
        + [jax.ShapeDtypeStruct((2, rows, cols), f32)],
        scratch_shapes=[pltpu.SemaphoreType.DMA((3, 3))],
        compiler_params=pltpu.CompilerParams(vmem_limit_bytes=4 << 20),
        name="strips",
    )(forcing, metric, jacobian)
    up = shift(bottom, "curve", 1)
    down = shift(top, "curve", -1)

    planes = 16 * (groups + 1)
    ecols = cols // 4
    halves = cols // LANES
    per_half = LANES // 4
    whole = lambda *shape: pl.BlockSpec(shape, lambda h: (0,) * len(shape))
    spread, low, high = pl.pallas_call(
        functools.partial(spread_kernel, rows),
        grid=(halves,),
        in_specs=[
            pl.BlockSpec((modes, rows, LANES), lambda h: (0, 0, h)),
            pl.BlockSpec((2, rows, LANES), lambda h: (0, 0, h)),
            pl.BlockSpec((modes + 2, halo, LANES), lambda h: (0, 0, h)),
            pl.BlockSpec((modes + 2, halo, LANES), lambda h: (0, 0, h)),
        ],
        out_specs=[
            pl.BlockSpec((planes, per_half, LANES), lambda h: (0, h, 0)),
            whole(planes, GHOST, LANES),
            whole(planes, GHOST, LANES),
        ],
        out_shape=[
            jax.ShapeDtypeStruct((planes, ecols, LANES), f32),
            jax.ShapeDtypeStruct((planes, GHOST, LANES), f32),
            jax.ShapeDtypeStruct((planes, GHOST, LANES), f32),
        ],
        scratch_shapes=[pltpu.VMEM((planes // 4, LANES, LANES), f32)] * 2,
        compiler_params=pltpu.CompilerParams(vmem_limit_bytes=12 << 20),
        name="spread",
    )(forcing, shared, up, down)

    left = shift(high, "sub", 1)
    right = shift(low, "sub", -1)
    scale = jnp.tile(mode_scale.reshape(groups, PACK), (1, LANES // PACK))

    total = ecols + 2 * GHOST
    array = lambda *shape: jax.ShapeDtypeStruct(shape, f32)
    field = array(16 * groups, total, LANES)
    lines = array(24, total, LANES)
    nodes = array(16, total, LANES)
    state = pl.pallas_call(
        prep_kernel,
        in_specs=[vmem] * 2,
        out_specs=[vmem] * 10,
        out_shape=[field, lines, lines, nodes, nodes, field, field, field]
        + [array(16, total + 16, LANES), array(8 * groups, total + 16, LANES)],
        compiler_params=pltpu.CompilerParams(vmem_limit_bytes=20 << 20),
        cost_estimate=pl.CostEstimate(flops=20_000_000, bytes_accessed=0, transcendentals=0),
        name="prep",
    )(spread, scale)
    devices = lax.axis_size(AXES[0]) * lax.axis_size(AXES[1])
    out = pl.pallas_call(
        functools.partial(krylov_kernel, rows, ecols),
        in_specs=[vmem] * 13,
        out_specs=[vmem] * 13,
        out_shape=[array(*x.shape) for x in state] + [field, field, array(devices, LANES)],
        scratch_shapes=[pltpu.VMEM((8 * groups, total + 16, LANES), f32)],
        input_output_aliases={3 + i: i for i in range(10)},
        compiler_params=pltpu.CompilerParams(vmem_limit_bytes=24 << 20),
        name="krylov",
    )(right, left, scale, *state)
    mass_sum, lap_sum, u0, w3 = out[3], out[4], out[6], out[7]
    u1, u2, part = out[10:]

    parts = lax.all_to_all(part, AXES, 0, 0, tiled=True)

    out = jax.ShapeDtypeStruct((modes, rows, cols), f32)
    return tuple(
        pl.pallas_call(
            combine_kernel,
            in_specs=[vmem] * 8,
            out_specs=[anywhere] * 2,
            out_shape=[out] * 2,
            scratch_shapes=[
                pltpu.VMEM((halves, modes, rows, LANES), f32),
                pltpu.VMEM((halves, modes, rows, LANES), f32),
                pltpu.VMEM((2, 4 * groups, LANES, LANES), f32),
                pltpu.VMEM((2, 4 * groups, LANES, LANES), f32),
                pltpu.SemaphoreType.DMA((halves, 2)),
            ],
            compiler_params=pltpu.CompilerParams(vmem_limit_bytes=20 << 20),
            name="combine",
        )(parts, scale, u0, u1, u2, w3, mass_sum, lap_sum)
    )


def solution(mesh):
    in_specs = (P(None, "curve", "sub"), P("curve", "sub"), P("curve", "sub"), P())
    out_specs = (P(None, "curve", "sub"), P(None, "curve", "sub"))
    return jax.shard_map(
        shards, mesh=mesh, in_specs=in_specs, out_specs=out_specs, check_vma=False
    )
```

time: 62.1 us -> 57.5 us (0.926)
  Pallas kernels: 17.5 us -> 13.9 us
  waiting for transfers between devices: 10.2 us -> 7.86 us
  local copies, waits for them, and re-layouts: 1.99 us -> 3.25 us
    pallas_call x2 -> x3, Pallas kernels: 13 us -> 9.46 us  [the longest x1 6.85 us: shards(): pl.pallas_call(functools.partial(krylov_kernel, rows, ecols), in_specs=[v...]
    ppermute x4, waiting for transfers between devices: 10.2 us -> 7.86 us  [shift(): lax.ppermute(x, axis, [(i, (i + step) % count) for i in range(count)])]
    unnamed x8 -> x10, local copies, waits for them, and re-layouts: 1.79 us -> 3.06 us
  transfers between devices with their start and end apart: 4 -> 4, of which waited for: 4 -> 3; matrix products, arithmetic and copies ran while one was open for 0% -> 0% of each run, Pallas kernels for 0% -> 4%
where the time goes in v3:
time: 57.5 us; the launch traced here: 57.3 us
  blocking collectives  25.6 us (45%)
  Pallas kernels  13.9 us (24%)
  waiting for transfers between devices  7.86 us (14%)
  starting transfers between devices  5.93 us (10%)
  local copies, waits for them, and re-layouts  3.25 us (6%)
  between operations  0.68 us (1%)
    all_to_all x1, blocking collectives, shards(): parts = lax.all_to_all(part, AXES, 0, 0, tiled=True)  25.6 us
    ppermute x4, waiting for transfers between devices, shift(): lax.ppermute(x, axis, [(i, (i + step) % count) for i in range(count)])  7.86 us
    pallas_call x1, Pallas kernels, shards(): pl.pallas_call(functools.partial(krylov_kernel, rows, ecols), in_specs=[v...  6.85 us
    ppermute x4, starting transfers between devices, shift(): lax.ppermute(x, axis, [(i, (i + step) % count) for i in range(count)])  5.93 us
    pallas_call x1, Pallas kernels, shards(): pl.pallas_call(combine_kernel, in_specs=[vmem] * 8, out_specs=[anywhere]...  3.25 us
    unnamed x10, local copies, waits for them, and re-layouts  3.06 us
    pallas_call x1, Pallas kernels, shards(): pl.pallas_call(prep_kernel, in_specs=[vmem] * 2, out_specs=[vmem] * 10, o...  2.12 us
    pallas_call x1, Pallas kernels, shards(): pl.pallas_call(functools.partial(spread_kernel, rows), grid=(halves,), in...  1.22 us
  transfers between devices with their start and end apart: 4, of which 3 were waited for; matrix products, arithmetic and copies ran while one was open for 0% of the time, Pallas kernels for 4%

profile of v3, /device:TPU:1, one launch (start us, length us, event | category | flops | bytes accessed | tf_op | source)
XLA Modules:
  0.0 57.3 jit_solution(5899400322180752011)
XLA Ops:
  0.6 0.0 copy-start
  0.6 1.3 %copy-done = f32[12,96,256]{2,1,0:T(8,128)S(1)} copy-done((f32[12,96,256]{2,1,0:T(8,128)S(1)}, f32[12,96,256]{2,1,0:T(8,128)}, u32[]{:S(2)}) %copy-start) | copy-done | bytes 1179672
  1.9 0.0 copy-start.2
  1.9 0.9 %copy-done.2 = f32[96,256]{1,0:T(8,128)S(1)} copy-done((f32[96,256]{1,0:T(8,128)S(1)}, f32[96,256]{1,0:T(8,128)}, u32[]{:S(2)}) %copy-start.2) | copy-done | bytes 98328
  2.8 0.0 copy-start.3
  2.8 0.9 %copy-done.3 = f32[96,256]{1,0:T(8,128)S(1)} copy-done((f32[96,256]{1,0:T(8,128)S(1)}, f32[96,256]{1,0:T(8,128)}, u32[]{:S(2)}) %copy-start.3) | copy-done | bytes 98328
  3.7 0.0 copy-start.1
  3.7 0.0 copy-start.4
  3.7 0.5 strips.1
  4.2 3.1 %collective-permute-start = (f32[14,16,256]{2,1,0:T(8,128)S(1)}, f32[14,16,256]{2,1,0:T(8,128)S(1)}, u32[]{:S(2)}, u32[]{:S(2)}) collective-permute-start(f32[14,16,256]{2,1,0:T(8,128)S(1)} %get-tuple-element.26), channel_id=1, source_target_pairs={{0,4},{4,8},{8,12},{12,16},{16,20},{20,24},{24,28},{28,32},{32,36}... | collective-permute-start | bytes 688136 | tf_op jit(solution)/shard_map/ppermute | solution.py:369
  7.3 0.3 collective-permute-start.1
  7.6 2.7 %collective-permute-done.up_ref = f32[14,16,256]{2,1,0:T(8,128)S(1)} collective-permute-done((f32[14,16,256]{2,1,0:T(8,128)S(1)}, f32[14,16,256]{2,1,0:T(8,128)S(1)}, u32[]{:S(2)}, u32[]{:S(2)}) %collective-permute-start) | collective-permute-done | bytes 229408 | tf_op jit(solution)/shard_map/ppermute | solution.py:369
  10.2 2.5 %collective-permute-done.1.down_ref = f32[14,16,256]{2,1,0:T(8,128)S(1)} collective-permute-done((f32[14,16,256]{2,1,0:T(8,128)S(1)}, f32[14,16,256]{2,1,0:T(8,128)S(1)}, u32[]{:S(2)}, u32[]{:S(2)}) %collective-permute-start.1) | collective-permute-done | bytes 229408 | tf_op jit(solution)/shard_map/ppermute | solution.py:369
  12.7 0.0 copy-done.1
  12.7 1.2 %spread.1 = (f32[64,64,128]{2,1,0:T(8,128)S(1)}, f32[64,4,128]{2,1,0:T(4,128)S(1)}, f32[64,4,128]{2,1,0:T(4,128)S(1)}) custom-call(f32[12,96,256]{2,1,0:T(8,128)S(1)} %copy-done.1, f32[2,96,256]{2,1,0:T(8,128)S(1)} %get-tuple-element.25.shared_ref, f32[14,16,256]{2,1,0:T(8,128)S(1)} %collective-permute-done.up_ref, ...), custom_call_target="tpu_custom_call" | custom-call | tf_op jit(solution)/shard_map/spread/pallas_call | solution.py:392
  14.0 2.6 %collective-permute-start.2 = (f32[64,4,128]{2,1,0:T(4,128)S(1)}, f32[64,4,128]{2,1,0:T(4,128)S(1)}, u32[]{:S(2)}, u32[]{:S(2)}) collective-permute-start(f32[64,4,128]{2,1,0:T(4,128)S(1)} %get-tuple-element.28), channel_id=1, source_target_pairs={{0,3},{1,0},{2,1},{3,2},{4,7},{5,4},{6,5},{7,6},{8,11},{9,8},{10,9... | collective-permute-start | bytes 393224 | tf_op jit(solution)/shard_map/ppermute | solution.py:369
  16.5 0.0 collective-permute-start.3
  16.5 0.0 copy-done.4
  16.5 0.1 tile.10
  16.6 0.1 tile.12.scale_ref
  16.7 2.1 %prep.1 = (f32[48,72,128]{2,1,0:T(8,128)S(1)}, f32[24,72,128]{2,1,0:T(8,128)S(1)}, f32[24,72,128]{2,1,0:T(8,128)S(1)}, f32[16,72,128]{2,1,0:T(8,128)S(1)}, f32[1...) custom-call(f32[64,64,128]{2,1,0:T(8,128)S(1)} %get-tuple-element.30, ...), custom_call_target="tpu_custom_call" | custom-call | flops 20000000 | tf_op jit(solution)/shard_map/prep/pallas_call | solution.py:425
  18.8 0.0 collective-permute-done.2.right_ref
  18.8 2.7 %collective-permute-done.3.left_ref = f32[64,4,128]{2,1,0:T(4,128)S(1)} collective-permute-done((f32[64,4,128]{2,1,0:T(4,128)S(1)}, f32[64,4,128]{2,1,0:T(4,128)S(1)}, u32[]{:S(2)}, u32[]{:S(2)}) %collective-permute-start.3) | collective-permute-done | bytes 131104 | tf_op jit(solution)/shard_map/ppermute | solution.py:369
  21.5 6.8 %krylov.1 = (f32[48,72,128]{2,1,0:T(8,128)S(1)}, f32[24,72,128]{2,1,0:T(8,128)S(1)}, f32[24,72,128]{2,1,0:T(8,128)S(1)}, f32[16,72,128]{2,1,0:T(8,128)S(1)}, f32...) custom-call(f32[64,4,128]{2,1,0:T(4,128)S(1)} %collective-permute-do, ...), custom_call_target="tpu_custom_call", output_to_operand_aliasing={{0}: (3, {}), {1}: (4, {}), {2}: (5, {}), {3}: (6, {}), {4}... | custom-call | tf_op jit(solution)/shard_map/krylov/pallas_call | solution.py:436
  28.4 25.6 %all_to_all.11 = f32[256,1,128]{2,1,0:T(1,128)S(1)} all-to-all(f32[256,1,128]{2,1,0:T(1,128)S(1)} %bitcast.5), channel_id=1, replica_groups=mesh['curve'=64,'sub'=4] {'curve','sub'}, dimensions={0} | all-to-all | bytes 262144 | tf_op jit(solution)/shard_map/all_to_all | solution.py:449
  54.0 3.2 %combine.1 = (f32[12,96,256]{2,1,0:T(8,128)}, f32[12,96,256]{2,1,0:T(8,128)}) custom-call(f32[256,128]{1,0:T(8,128)S(1)} %bitcast.4, f32[3,128]{1,0:T(4,128)S(1)} %tile.12.scale_ref, f32[48,72,128]{2,1,0:T(8,128)S(1)} %get-tuple-element.42.u0_ref, f32[48,72,128]{2,1,0:T(8,128)S(1)} %get-tuple-element.43.u1_ref, f32[48,72,128]{2,1,0:T(8,128)S(1)} %get-tuple-element.44.u2_ref, ...), custom_call_target="tpu_custom_call" | custom-call | tf_op jit(solution)/shard_map/combine/pallas_call | solution.py:453
  (1 shorter events, 0.0 us)
Async XLA Ops:
  0.6 1.3 %copy-start = (f32[12,96,256]{2,1,0:T(8,128)S(1)}, f32[12,96,256]{2,1,0:T(8,128)}, u32[]{:S(2)}) copy-start(f32[12,96,256]{2,1,0:T(8,128)} %f_ref.1) | copy-start | bytes 3538948
  1.9 0.9 %copy-start.2 = (f32[96,256]{1,0:T(8,128)S(1)}, f32[96,256]{1,0:T(8,128)}, u32[]{:S(2)}) copy-start(f32[96,256]{1,0:T(8,128)} %metric_hbm.1) | copy-start | bytes 294916
  2.8 0.9 %copy-start.3 = (f32[96,256]{1,0:T(8,128)S(1)}, f32[96,256]{1,0:T(8,128)}, u32[]{:S(2)}) copy-start(f32[96,256]{1,0:T(8,128)} %jacobian_hbm.1) | copy-start | bytes 294916
  3.7 9.0 %copy-start.1 = (f32[12,96,256]{2,1,0:T(8,128)S(1)}, f32[12,96,256]{2,1,0:T(8,128)}, u32[]{:S(2)}) copy-start(f32[12,96,256]{2,1,0:T(8,128)} %f_ref.1) | copy-start | bytes 3538948
  3.7 12.8 %copy-start.4 = (f32[12]{0:T(128)S(1)}, f32[12]{0:T(128)}, u32[]{:S(2)}) copy-start(f32[12]{0:T(128)} %param.7) | copy-start | bytes 148
  4.2 6.1 %collective-permute-start = (f32[14,16,256]{2,1,0:T(8,128)S(1)}, f32[14,16,256]{2,1,0:T(8,128)S(1)}, u32[]{:S(2)}, u32[]{:S(2)}) collective-permute-start(f32[14,16,256]{2,1,0:T(8,128)S(1)} %get-tuple-element.26), channel_id=1, source_target_pairs={{0,4},{4,8},{8,12},{12,16},{16,20},{20,24},{24,28},{28,32},{32,36}... | collective-permute-start | bytes 688136 | tf_op jit(solution)/shard_map/ppermute | solution.py:369
  7.3 5.4 %collective-permute-start.1 = (f32[14,16,256]{2,1,0:T(8,128)S(1)}, f32[14,16,256]{2,1,0:T(8,128)S(1)}, u32[]{:S(2)}, u32[]{:S(2)}) collective-permute-start(f32[14,16,256]{2,1,0:T(8,128)S(1)} %get-tuple-element.27), channel_id=1, source_target_pairs={{0,252},{4,0},{8,4},{12,8},{16,12},{20,16},{24,20},{28,24},{32,28}... | collective-permute-start | bytes 688136 | tf_op jit(solution)/shard_map/ppermute | solution.py:369
  14.0 4.9 %collective-permute-start.2 = (f32[64,4,128]{2,1,0:T(4,128)S(1)}, f32[64,4,128]{2,1,0:T(4,128)S(1)}, u32[]{:S(2)}, u32[]{:S(2)}) collective-permute-start(f32[64,4,128]{2,1,0:T(4,128)S(1)} %get-tuple-element.28), channel_id=1, source_target_pairs={{0,3},{1,0},{2,1},{3,2},{4,7},{5,4},{6,5},{7,6},{8,11},{9,8},{10,9... | collective-permute-start | bytes 393224 | tf_op jit(solution)/shard_map/ppermute | solution.py:369
  16.5 5.0 %collective-permute-start.3 = (f32[64,4,128]{2,1,0:T(4,128)S(1)}, f32[64,4,128]{2,1,0:T(4,128)S(1)}, u32[]{:S(2)}, u32[]{:S(2)}) collective-permute-start(f32[64,4,128]{2,1,0:T(4,128)S(1)} %get-tuple-element.29), channel_id=1, source_target_pairs={{0,1},{1,2},{2,3},{3,0},{4,5},{5,6},{6,7},{7,4},{8,9},{9,10},{10,1... | collective-permute-start | bytes 393224 | tf_op jit(solution)/shard_map/ppermute | solution.py:369

commit v4 on v3

--- a/solution.py
+++ b/solution.py
@@ -13,6 +13,7 @@
 PACK = 4
 LANES = 128
 AXES = ("curve", "sub")
+LOAD_LIMIT = 4 << 20
 
 
 def gll_tables():
@@ -38,42 +39,45 @@
     return (group * 4 + a) * 4 + b
 
 
-def strips_kernel(f_hbm, metric_hbm, jacobian_hbm, top, bottom, shared, sems):
+def load_kernel(f_hbm, metric_hbm, jacobian_hbm, scale_hbm, top, bottom, fields, scale_ref, scales, sems):
     modes, rows, _ = f_hbm.shape
     halo = top.shape[1]
+    scale_copy = pltpu.make_async_copy(scale_hbm, scales, sems.at[3, 0])
+    scale_copy.start()
     copies = []
-    for side, (out, at) in enumerate(((top, 0), (bottom, rows - halo))):
-        span = pl.ds(at, halo)
+    for part, (out, at, size) in enumerate(
+        ((top, 0, halo), (bottom, rows - halo, halo), (fields, 0, rows))
+    ):
+        span = pl.ds(at, size)
         copies += [
-            pltpu.make_async_copy(f_hbm.at[:, span, :], out.at[pl.ds(0, modes)], sems.at[side, 0]),
-            pltpu.make_async_copy(metric_hbm.at[span, :], out.at[modes], sems.at[side, 1]),
-            pltpu.make_async_copy(jacobian_hbm.at[span, :], out.at[modes + 1], sems.at[side, 2]),
+            pltpu.make_async_copy(f_hbm.at[:, span, :], out.at[pl.ds(0, modes)], sems.at[part, 0]),
+            pltpu.make_async_copy(metric_hbm.at[span, :], out.at[modes], sems.at[part, 1]),
+            pltpu.make_async_copy(jacobian_hbm.at[span, :], out.at[modes + 1], sems.at[part, 2]),
         ]
-    copies += [
-        pltpu.make_async_copy(metric_hbm, shared.at[0], sems.at[2, 0]),
-        pltpu.make_async_copy(jacobian_hbm, shared.at[1], sems.at[2, 1]),
-    ]
     for copy in copies:
         copy.start()
+    scale_copy.wait()
+    member = lax.broadcasted_iota(jnp.int32, (1, LANES), 1) % PACK
+    for group in range(modes // PACK):
+        row = jnp.zeros((1, LANES), jnp.float32)
+        for m in range(PACK):
+            row = jnp.where(member == m, scales[group * PACK + m], row)
+        scale_ref[group : group + 1, :] = row
     for copy in copies:
         copy.wait()
 
 
-def spread_kernel(rows, f_ref, shared_ref, up_ref, down_ref, t_ref, low_ref, high_ref, xs, xt):
+def spread_kernel(rows, f_ref, up_ref, down_ref, t_ref, low_ref, high_ref, xs, xt):
     half = pl.program_id(0)
     own = rows // 4
-    groups = f_ref.shape[0] // PACK
+    groups = (f_ref.shape[0] - 2) // PACK
     per_half = LANES // 4
     for group in range(groups + 1):
         for a in range(4):
             at = group * 4 + a
             for m in range(PACK):
-                if group < groups:
-                    index = group * PACK + m
-                    mine = f_ref[index, pl.ds(a, own, stride=4), :]
-                else:
-                    index = groups * PACK + m % 2
-                    mine = shared_ref[m % 2, pl.ds(a, own, stride=4), :]
+                index = group * PACK + (m if group < groups else m % 2)
+                mine = f_ref[index, pl.ds(a, own, stride=4), :]
                 xs[at, pl.ds(m, own, stride=PACK), :] = mine
                 xs[at, pl.ds(own * PACK + m, GHOST, stride=PACK), :] = down_ref[
                     index, pl.ds(a, GHOST, stride=4), :
@@ -348,12 +352,15 @@
                         out[half, group * PACK + m, pl.ds(a, own, stride=4), :] = xt[
                             i, slot, pl.ds(m, own, stride=PACK), :
                         ]
-        for i, (out, hbm) in enumerate(((sol, sol_hbm), (res, res_hbm))):
-            copy = pltpu.make_async_copy(
-                out.at[half], hbm.at[:, :, pl.ds(half * LANES, LANES)], sems.at[half, i]
-            )
-            copy.start()
-            copies.append(copy)
+            span_modes = pl.ds(group * PACK, PACK)
+            for i, (out, hbm) in enumerate(((sol, sol_hbm), (res, res_hbm))):
+                copy = pltpu.make_async_copy(
+                    out.at[half, span_modes],
+                    hbm.at[span_modes, :, pl.ds(half * LANES, LANES)],
+                    sems.at[half, group, i],
+                )
+                copy.start()
+                copies.append(copy)
     for copy in copies:
         copy.wait()
 
@@ -370,17 +377,17 @@
 
     vmem = pl.BlockSpec(memory_space=pltpu.VMEM)
     anywhere = pl.BlockSpec(memory_space=pl.ANY)
-    hbm = pl.BlockSpec(memory_space=pltpu.HBM)
-    top, bottom, shared = pl.pallas_call(
-        strips_kernel,
-        in_specs=[hbm] * 3,
-        out_specs=[vmem] * 3,
-        out_shape=[jax.ShapeDtypeStruct((modes + 2, halo, cols), f32)] * 2
-        + [jax.ShapeDtypeStruct((2, rows, cols), f32)],
-        scratch_shapes=[pltpu.SemaphoreType.DMA((3, 3))],
-        compiler_params=pltpu.CompilerParams(vmem_limit_bytes=4 << 20),
-        name="strips",
-    )(forcing, metric, jacobian)
+    array = lambda *shape: jax.ShapeDtypeStruct(shape, f32)
+    top, bottom, fields, scale = pl.pallas_call(
+        load_kernel,
+        in_specs=[anywhere] * 4,
+        out_specs=[vmem] * 4,
+        out_shape=[array(modes + 2, halo, cols)] * 2
+        + [array(modes + 2, rows, cols), array(groups, LANES)],
+        scratch_shapes=[pltpu.SMEM((modes,), f32), pltpu.SemaphoreType.DMA((4, 3))],
+        compiler_params=pltpu.CompilerParams(vmem_limit_bytes=LOAD_LIMIT),
+        name="load",
+    )(*[pltpu.with_memory_space_constraint(x, pltpu.HBM) for x in (forcing, metric, jacobian, mode_scale)])
     up = shift(bottom, "curve", 1)
     down = shift(top, "curve", -1)
 
@@ -393,8 +400,7 @@
         functools.partial(spread_kernel, rows),
         grid=(halves,),
         in_specs=[
-            pl.BlockSpec((modes, rows, LANES), lambda h: (0, 0, h)),
-            pl.BlockSpec((2, rows, LANES), lambda h: (0, 0, h)),
+            pl.BlockSpec((modes + 2, rows, LANES), lambda h: (0, 0, h)),
             pl.BlockSpec((modes + 2, halo, LANES), lambda h: (0, 0, h)),
             pl.BlockSpec((modes + 2, halo, LANES), lambda h: (0, 0, h)),
         ],
@@ -411,14 +417,12 @@
         scratch_shapes=[pltpu.VMEM((planes // 4, LANES, LANES), f32)] * 2,
         compiler_params=pltpu.CompilerParams(vmem_limit_bytes=12 << 20),
         name="spread",
-    )(forcing, shared, up, down)
+    )(fields, up, down)
 
     left = shift(high, "sub", 1)
     right = shift(low, "sub", -1)
-    scale = jnp.tile(mode_scale.reshape(groups, PACK), (1, LANES // PACK))
 
     total = ecols + 2 * GHOST
-    array = lambda *shape: jax.ShapeDtypeStruct(shape, f32)
     field = array(16 * groups, total, LANES)
     lines = array(24, total, LANES)
     nodes = array(16, total, LANES)
@@ -460,7 +464,7 @@
                 pltpu.VMEM((halves, modes, rows, LANES), f32),
                 pltpu.VMEM((2, 4 * groups, LANES, LANES), f32),
                 pltpu.VMEM((2, 4 * groups, LANES, LANES), f32),
-                pltpu.SemaphoreType.DMA((halves, 2)),
+                pltpu.SemaphoreType.DMA((halves, groups, 2)),
             ],
             compiler_params=pltpu.CompilerParams(vmem_limit_bytes=20 << 20),
             name="combine",

time: 57.5 us -> 55.4 us (0.963)
  local copies, waits for them, and re-layouts: 3.25 us -> 0 us
  Pallas kernels: 13.9 us -> 14.9 us
    unnamed x10 -> x0, local copies, waits for them, and re-layouts: 3.06 us -> none
    pallas_call x1, Pallas kernels: 0.48 us -> 1.66 us  [shards(): pl.pallas_call(load_kernel, in_specs=[anywhere] * 4, out_specs=[vmem] * 4...]
where the time goes in v4:
time: 55.4 us; the launch traced here: 55.2 us
  blocking collectives  25.6 us (46%)
  Pallas kernels  14.9 us (27%)
  waiting for transfers between devices  8.07 us (15%)
  starting transfers between devices  5.93 us (11%)
  between operations  0.66 us (1%)
    all_to_all x1, blocking collectives, shards(): parts = lax.all_to_all(part, AXES, 0, 0, tiled=True)  25.6 us
    ppermute x4, waiting for transfers between devices, shift(): lax.ppermute(x, axis, [(i, (i + step) % count) for i in range(count)])  8.07 us
    pallas_call x1, Pallas kernels, shards(): pl.pallas_call(functools.partial(krylov_kernel, rows, ecols), in_specs=[v...  6.85 us
    ppermute x4, starting transfers between devices, shift(): lax.ppermute(x, axis, [(i, (i + step) % count) for i in range(count)])  5.93 us
    pallas_call x1, Pallas kernels, shards(): pl.pallas_call(combine_kernel, in_specs=[vmem] * 8, out_specs=[anywhere]...  3.1 us
    pallas_call x1, Pallas kernels, shards(): pl.pallas_call(prep_kernel, in_specs=[vmem] * 2, out_specs=[vmem] * 10, o...  2.12 us
    pallas_call x1, Pallas kernels, shards(): pl.pallas_call(load_kernel, in_specs=[anywhere] * 4, out_specs=[vmem] * 4...  1.66 us
    pallas_call x1, Pallas kernels, shards(): pl.pallas_call(functools.partial(spread_kernel, rows), grid=(halves,), in...  1.21 us
  transfers between devices with their start and end apart: 4, of which 3 were waited for; matrix products, arithmetic and copies ran while one was open for 0% of the time, Pallas kernels for 4%

profile of v4, /device:TPU:1, one launch (start us, length us, event | category | flops | bytes accessed | tf_op | source)
XLA Modules:
  0.0 55.2 jit_solution(5036616538518291920)
XLA Ops:
  0.6 1.7 %load.1 = (f32[14,16,256]{2,1,0:T(8,128)S(1)}, f32[14,16,256]{2,1,0:T(8,128)S(1)}, f32[14,96,256]{2,1,0:T(8,128)S(1)}, f32[3,128]{1,0:T(4,128)S(1)}) custom-call(f32[12,96,256]{2,1,0:T(8,128)} %f_hbm.1, f32[96,256]{1,0:T(8,128)} %metric_hbm.1, f32[96,256]{1,0:T(8,128)} %jacobian_hbm.1, f32[12]{0:T(128)} %scale_hbm.1), custom_call_target="tpu_custom_call" | custom-call | tf_op jit(solution)/shard_map/load/pallas_call | solution.py:381
  2.3 3.1 %collective-permute-start = (f32[14,16,256]{2,1,0:T(8,128)S(1)}, f32[14,16,256]{2,1,0:T(8,128)S(1)}, u32[]{:S(2)}, u32[]{:S(2)}) collective-permute-start(f32[14,16,256]{2,1,0:T(8,128)S(1)} %get-tuple-element.27), channel_id=1, source_target_pairs={{0,4},{4,8},{8,12},{12,16},{16,20},{20,24},{24,28},{28,32},{32,36}... | collective-permute-start | bytes 688136 | tf_op jit(solution)/shard_map/ppermute | solution.py:376
  5.4 0.3 collective-permute-start.1
  5.7 2.7 %collective-permute-done.up_ref = f32[14,16,256]{2,1,0:T(8,128)S(1)} collective-permute-done((f32[14,16,256]{2,1,0:T(8,128)S(1)}, f32[14,16,256]{2,1,0:T(8,128)S(1)}, u32[]{:S(2)}, u32[]{:S(2)}) %collective-permute-start) | collective-permute-done | bytes 229408 | tf_op jit(solution)/shard_map/ppermute | solution.py:376
  8.4 2.5 %collective-permute-done.1.down_ref = f32[14,16,256]{2,1,0:T(8,128)S(1)} collective-permute-done((f32[14,16,256]{2,1,0:T(8,128)S(1)}, f32[14,16,256]{2,1,0:T(8,128)S(1)}, u32[]{:S(2)}, u32[]{:S(2)}) %collective-permute-start.1) | collective-permute-done | bytes 229408 | tf_op jit(solution)/shard_map/ppermute | solution.py:376
  10.8 1.2 %spread.1 = (f32[64,64,128]{2,1,0:T(8,128)S(1)}, f32[64,4,128]{2,1,0:T(4,128)S(1)}, f32[64,4,128]{2,1,0:T(4,128)S(1)}) custom-call(f32[14,96,256]{2,1,0:T(8,128)S(1)} %get-tuple-element.26.f_ref, f32[14,16,256]{2,1,0:T(8,128)S(1)} %collective-permute-done.up_ref, f32[14,16,256]{2,1,0:T(8,128)S(1)} %collective-permute-done.1.down_ref), custom_call_target="tpu_custom_call" | custom-call | tf_op jit(solution)/shard_map/spread/pallas_call | solution.py:399
  12.1 2.6 %collective-permute-start.2 = (f32[64,4,128]{2,1,0:T(4,128)S(1)}, f32[64,4,128]{2,1,0:T(4,128)S(1)}, u32[]{:S(2)}, u32[]{:S(2)}) collective-permute-start(f32[64,4,128]{2,1,0:T(4,128)S(1)} %get-tuple-element.29), channel_id=1, source_target_pairs={{0,3},{1,0},{2,1},{3,2},{4,7},{5,4},{6,5},{7,6},{8,11},{9,8},{10,9... | collective-permute-start | bytes 393224 | tf_op jit(solution)/shard_map/ppermute | solution.py:376
  14.6 0.0 collective-permute-start.3
  14.6 2.1 %prep.1 = (f32[48,72,128]{2,1,0:T(8,128)S(1)}, f32[24,72,128]{2,1,0:T(8,128)S(1)}, f32[24,72,128]{2,1,0:T(8,128)S(1)}, f32[16,72,128]{2,1,0:T(8,128)S(1)}, f32[1...) custom-call(f32[64,64,128]{2,1,0:T(8,128)S(1)} %get-tuple-element.32, ...), custom_call_target="tpu_custom_call" | custom-call | flops 20000000 | tf_op jit(solution)/shard_map/prep/pallas_call | solution.py:429
  16.7 0.0 collective-permute-done.2.right_ref
  16.7 2.9 %collective-permute-done.3.left_ref = f32[64,4,128]{2,1,0:T(4,128)S(1)} collective-permute-done((f32[64,4,128]{2,1,0:T(4,128)S(1)}, f32[64,4,128]{2,1,0:T(4,128)S(1)}, u32[]{:S(2)}, u32[]{:S(2)}) %collective-permute-start.3) | collective-permute-done | bytes 131104 | tf_op jit(solution)/shard_map/ppermute | solution.py:376
  19.6 6.9 %krylov.1 = (f32[48,72,128]{2,1,0:T(8,128)S(1)}, f32[24,72,128]{2,1,0:T(8,128)S(1)}, f32[24,72,128]{2,1,0:T(8,128)S(1)}, f32[16,72,128]{2,1,0:T(8,128)S(1)}, f32...) custom-call(f32[64,4,128]{2,1,0:T(4,128)S(1)} %collective-permute-do, ...), custom_call_target="tpu_custom_call", output_to_operand_aliasing={{0}: (3, {}), {1}: (4, {}), {2}: (5, {}), {3}: (6, {}), {4}... | custom-call | tf_op jit(solution)/shard_map/krylov/pallas_call | solution.py:440
  26.5 25.6 %all_to_all.11 = f32[256,1,128]{2,1,0:T(1,128)S(1)} all-to-all(f32[256,1,128]{2,1,0:T(1,128)S(1)} %bitcast.5), channel_id=1, replica_groups=mesh['curve'=64,'sub'=4] {'curve','sub'}, dimensions={0} | all-to-all | bytes 262144 | tf_op jit(solution)/shard_map/all_to_all | solution.py:453
  52.1 3.1 %combine.1 = (f32[12,96,256]{2,1,0:T(8,128)}, f32[12,96,256]{2,1,0:T(8,128)}) custom-call(f32[256,128]{1,0:T(8,128)S(1)} %bitcast.4, f32[3,128]{1,0:T(4,128)S(1)} %get-tuple-element.31.scale_ref, f32[48,72,128]{2,1,0:T(8,128)S(1)} %get-tuple-element.44.u0_ref, f32[48,72,128]{2,1,0:T(8,128)S(1)} %get-tuple-element.45.u1_ref, ...), custom_call_target="tpu_custom_call" | custom-call | tf_op jit(solution)/shard_map/combine/pallas_call | solution.py:457
Async XLA Ops:
  2.3 6.1 %collective-permute-start = (f32[14,16,256]{2,1,0:T(8,128)S(1)}, f32[14,16,256]{2,1,0:T(8,128)S(1)}, u32[]{:S(2)}, u32[]{:S(2)}) collective-permute-start(f32[14,16,256]{2,1,0:T(8,128)S(1)} %get-tuple-element.27), channel_id=1, source_target_pairs={{0,4},{4,8},{8,12},{12,16},{16,20},{20,24},{24,28},{28,32},{32,36}... | collective-permute-start | bytes 688136 | tf_op jit(solution)/shard_map/ppermute | solution.py:376
  5.4 5.4 %collective-permute-start.1 = (f32[14,16,256]{2,1,0:T(8,128)S(1)}, f32[14,16,256]{2,1,0:T(8,128)S(1)}, u32[]{:S(2)}, u32[]{:S(2)}) collective-permute-start(f32[14,16,256]{2,1,0:T(8,128)S(1)} %get-tuple-element.28), channel_id=1, source_target_pairs={{0,252},{4,0},{8,4},{12,8},{16,12},{20,16},{24,20},{28,24},{32,28}... | collective-permute-start | bytes 688136 | tf_op jit(solution)/shard_map/ppermute | solution.py:376
  12.1 4.7 %collective-permute-start.2 = (f32[64,4,128]{2,1,0:T(4,128)S(1)}, f32[64,4,128]{2,1,0:T(4,128)S(1)}, u32[]{:S(2)}, u32[]{:S(2)}) collective-permute-start(f32[64,4,128]{2,1,0:T(4,128)S(1)} %get-tuple-element.29), channel_id=1, source_target_pairs={{0,3},{1,0},{2,1},{3,2},{4,7},{5,4},{6,5},{7,6},{8,11},{9,8},{10,9... | collective-permute-start | bytes 393224 | tf_op jit(solution)/shard_map/ppermute | solution.py:376
  14.6 5.0 %collective-permute-start.3 = (f32[64,4,128]{2,1,0:T(4,128)S(1)}, f32[64,4,128]{2,1,0:T(4,128)S(1)}, u32[]{:S(2)}, u32[]{:S(2)}) collective-permute-start(f32[64,4,128]{2,1,0:T(4,128)S(1)} %get-tuple-element.30), channel_id=1, source_target_pairs={{0,1},{1,2},{2,3},{3,0},{4,5},{5,6},{6,7},{7,4},{8,9},{9,10},{10,1... | collective-permute-start | bytes 393224 | tf_op jit(solution)/shard_map/ppermute | solution.py:376

commit v5 on v4

--- a/solution.py
+++ b/solution.py
@@ -120,11 +120,14 @@
     return pltpu.roll(shared, PACK, 1), shared
 
 
-def join_cols(edge, i, total):
+def wrap_cols(edge, i, total):
     edge[2 * i, total + 8 : total + 16, :] = edge[2 * i, 8:16, :]
     edge[2 * i + 1, 0:8, :] = edge[2 * i + 1, total : total + 8, :]
-    first = edge[2 * i, 8 : total + 8, :] + edge[2 * i + 1, 7 : total + 7, :]
-    last = edge[2 * i + 1, 8 : total + 8, :] + edge[2 * i, 9 : total + 9, :]
+
+
+def join_cols(edge, i, low, high):
+    first = edge[2 * i, low + 8 : high + 8, :] + edge[2 * i + 1, low + 7 : high + 7, :]
+    last = edge[2 * i + 1, low + 8 : high + 8, :] + edge[2 * i, low + 9 : high + 9, :]
     return first, last
 
 
@@ -184,15 +187,100 @@
                     redge[2 * (group * 4 + a) + b // 3, spare(t), :] = column[a]
 
 
+def finish(a, low, high, scale_ref, mass_sum_ref, lap_sum_ref, minv, u0_ref, cedge, redge):
+    groups = u0_ref.shape[0] // 16
+    span = slice(low, high)
+    mass_sums = join_cols(cedge, a, low, high)
+    lap_sums = join_cols(cedge, 4 + a, low, high)
+    for side, b in enumerate((0, 3)):
+        mass_sum_ref[a * 4 + b, span, :] = mass_sums[side]
+        lap_sum_ref[a * 4 + b, span, :] = lap_sums[side]
+    for group in range(groups):
+        scale = scale_ref[group : group + 1, :]
+        source = join_cols(redge, group * 4 + a, low, high)
+        for side, b in enumerate((0, 3)):
+            inverse = 1.0 / (mass_sums[side] + scale * lap_sums[side])
+            u0_ref[plane(group, a, b), span, :] = source[side] * inverse
+            minv[plane(group, a, b), span, :] = inverse * scale
+
+
+def operator_tile(t, own, sums, now_ref, old_ref, new_ref, mass_ref, krow, kcol, minv, w_ref, edge):
+    groups = now_ref.shape[0] // 16
+    zero = jnp.zeros((8, LANES), jnp.float32)
+    sums = list(sums)
+    for group in range(groups):
+        u = [[now_ref[plane(group, a, b), tile(t), :] for b in range(4)] for a in range(4)]
+        along_rows = [
+            line_operator(
+                [krow[line * 6 + i, tile(t), :] for i in range(6)], [u[a][line] for a in range(4)]
+            )
+            for line in range(4)
+        ]
+        along_cols = [
+            line_operator([kcol[line * 6 + i, tile(t), :] for i in range(6)], u[line])
+            for line in range(4)
+        ]
+        with_now, with_old = zero, zero
+        y = [[None] * 4 for _ in range(4)]
+        for a in range(4):
+            for b in range(4):
+                p = plane(group, a, b)
+                value = mass_ref[p, tile(t), :] * u[a][b]
+                row, col = along_rows[b][a], along_cols[a][b]
+                value = value - row if a == 3 else value + row
+                value = value - col if b == 3 else value + col
+                y[a][b] = value
+                with_now += u[a][b] * value
+                if old_ref is None:
+                    with_old += w_ref[p, tile(t), :] * u[a][b]
+                else:
+                    with_old += old_ref[p, tile(t), :] * value
+        sums[group] += with_now if own is None else own * with_now
+        sums[groups + group] += with_old if own is None else own * with_old
+        for b in range(4):
+            column = [y[a][b] for a in range(4)]
+            column[0], column[3] = join_rows(column[0], column[3])
+            for a in range(4):
+                p = plane(group, a, b)
+                if b in (1, 2):
+                    if new_ref is None:
+                        w_ref[p, tile(t), :] = column[a]
+                    else:
+                        new_ref[p, tile(t), :] = column[a] * minv[p, tile(t), :] - u[a][b]
+                else:
+                    edge[2 * (group * 4 + a) + b // 3, spare(t), :] = column[a]
+    return tuple(sums)
+
+
 def prep_kernel(t_ref, scale_ref, *refs):
-    @pl.loop(0, t_ref.shape[1] // 8)
+    state, (u1_ref, edge, sums_ref) = refs[:10], refs[10:]
+    mass_ref, krow, kcol, mass_sum_ref, lap_sum_ref, minv, u0_ref, w_ref, cedge, redge = state
+    cols = t_ref.shape[1]
+
+    @pl.loop(0, cols // 8)
     def _(t):
-        prepare(t, lambda p: t_ref[p, tile(t), :], scale_ref, *refs)
-
-
-def krylov_kernel(own_rows, cols, right_ref, left_ref, scale_ref, *refs):
-    state = refs[10:20]
-    u1_ref, u2_ref, part_ref, edge = refs[20:]
+        prepare(t, lambda p: t_ref[p, tile(t), :], scale_ref, *state)
+
+    @pl.loop(0, 4)
+    def _(a):
+        finish(a, 8, cols - 8, scale_ref, mass_sum_ref, lap_sum_ref, minv, u0_ref, cedge, redge)
+
+    zero = jnp.zeros((8, LANES), jnp.float32)
+    sums = lax.fori_loop(
+        1,
+        cols // 8 - 1,
+        lambda t, sums: operator_tile(
+            t, None, sums, u0_ref, None, u1_ref, mass_ref, krow, kcol, minv, w_ref, edge
+        ),
+        (zero,) * sums_ref.shape[0],
+    )
+    for i, value in enumerate(sums):
+        sums_ref[i] = value
+
+
+def krylov_kernel(own_rows, cols, count, right_ref, left_ref, scale_ref, *refs):
+    state = refs[count : count + 10]
+    u1_ref, edge, sums_ref, u2_ref, part_ref = refs[count + 10 :]
     mass_ref, krow, kcol, mass_sum_ref, lap_sum_ref, minv, u0_ref, w_ref, cedge, redge = state
     groups = u0_ref.shape[0] // 16
     total = u0_ref.shape[1]
@@ -205,73 +293,34 @@
 
     @pl.loop(0, 4)
     def _(a):
-        mass_sums = join_cols(cedge, a, total)
-        lap_sums = join_cols(cedge, 4 + a, total)
-        for side, b in enumerate((0, 3)):
-            mass_sum_ref[a * 4 + b] = mass_sums[side]
-            lap_sum_ref[a * 4 + b] = lap_sums[side]
+        wrap_cols(cedge, a, total)
+        wrap_cols(cedge, 4 + a, total)
         for group in range(groups):
-            source = join_cols(redge, group * 4 + a, total)
-            for side, b in enumerate((0, 3)):
-                inverse = 1.0 / (mass_sums[side] + scales[group] * lap_sums[side])
-                u0_ref[plane(group, a, b)] = source[side] * inverse
-                minv[plane(group, a, b)] = inverse * scales[group]
+            wrap_cols(redge, group * 4 + a, total)
+        for low, high in ((0, 8), (cols - 8, total)):
+            finish(a, low, high, scale_ref, mass_sum_ref, lap_sum_ref, minv, u0_ref, cedge, redge)
 
     zero = jnp.zeros((8, LANES), jnp.float32)
+    shared = (mass_ref, krow, kcol, minv, w_ref, edge)
 
     def apply(now_ref, old_ref, new_ref):
-        def body(t, sums):
-            sums = list(sums)
+        def body(i, sums):
+            if old_ref is None:
+                t = jnp.where(i == 0, 0, i + own_tiles - 2)
+            else:
+                t = i
             own = (t < own_tiles).astype(jnp.float32)
-            for group in range(groups):
-                u = [[now_ref[plane(group, a, b), tile(t), :] for b in range(4)] for a in range(4)]
-                along_rows = [
-                    line_operator(
-                        [krow[line * 6 + i, tile(t), :] for i in range(6)],
-                        [u[a][line] for a in range(4)],
-                    )
-                    for line in range(4)
-                ]
-                along_cols = [
-                    line_operator([kcol[line * 6 + i, tile(t), :] for i in range(6)], u[line])
-                    for line in range(4)
-                ]
-                with_now, with_old = zero, zero
-                y = [[None] * 4 for _ in range(4)]
-                for a in range(4):
-                    for b in range(4):
-                        p = plane(group, a, b)
-                        value = mass_ref[p, tile(t), :] * u[a][b]
-                        row, col = along_rows[b][a], along_cols[a][b]
-                        value = value - row if a == 3 else value + row
-                        value = value - col if b == 3 else value + col
-                        y[a][b] = value
-                        with_now += u[a][b] * value
-                        if old_ref is None:
-                            with_old += w_ref[p, tile(t), :] * u[a][b]
-                        else:
-                            with_old += old_ref[p, tile(t), :] * value
-                sums[group] += own * with_now
-                sums[groups + group] += own * with_old
-                for b in range(4):
-                    column = [y[a][b] for a in range(4)]
-                    column[0], column[3] = join_rows(column[0], column[3])
-                    for a in range(4):
-                        p = plane(group, a, b)
-                        if b in (1, 2):
-                            if new_ref is None:
-                                w_ref[p, tile(t), :] = column[a]
-                            else:
-                                new_ref[p, tile(t), :] = column[a] * minv[p, tile(t), :] - u[a][b]
-                        else:
-                            edge[2 * (group * 4 + a) + b // 3, spare(t), :] = column[a]
-            return tuple(sums)
-
-        sums = lax.fori_loop(0, tiles, body, (zero,) * (2 * groups))
+            return operator_tile(t, own, sums, now_ref, old_ref, new_ref, *shared)
+
+        if old_ref is None:
+            sums = lax.fori_loop(0, 3, body, tuple(sums_ref[i] for i in range(2 * groups)))
+        else:
+            sums = lax.fori_loop(0, tiles, body, (zero,) * (2 * groups))
 
         @pl.loop(0, groups * 4)
         def _(i):
-            for b, value in zip((0, 3), join_cols(edge, i, total)):
+            wrap_cols(edge, i, total)
+            for b, value in zip((0, 3), join_cols(edge, i, 0, total)):
                 p = i * 4 + b
                 if new_ref is None:
                     w_ref[p] = value
@@ -429,26 +478,27 @@
     state = pl.pallas_call(
         prep_kernel,
         in_specs=[vmem] * 2,
-        out_specs=[vmem] * 10,
+        out_specs=[vmem] * 13,
         out_shape=[field, lines, lines, nodes, nodes, field, field, field]
-        + [array(16, total + 16, LANES), array(8 * groups, total + 16, LANES)],
-        compiler_params=pltpu.CompilerParams(vmem_limit_bytes=20 << 20),
+        + [array(16, total + 16, LANES), array(8 * groups, total + 16, LANES)]
+        + [field, array(8 * groups, total + 16, LANES), array(2 * groups, 8, LANES)],
+        compiler_params=pltpu.CompilerParams(vmem_limit_bytes=24 << 20),
         cost_estimate=pl.CostEstimate(flops=20_000_000, bytes_accessed=0, transcendentals=0),
         name="prep",
     )(spread, scale)
     devices = lax.axis_size(AXES[0]) * lax.axis_size(AXES[1])
+    count = len(state)
     out = pl.pallas_call(
-        functools.partial(krylov_kernel, rows, ecols),
-        in_specs=[vmem] * 13,
-        out_specs=[vmem] * 13,
-        out_shape=[array(*x.shape) for x in state] + [field, field, array(devices, LANES)],
-        scratch_shapes=[pltpu.VMEM((8 * groups, total + 16, LANES), f32)],
-        input_output_aliases={3 + i: i for i in range(10)},
+        functools.partial(krylov_kernel, rows, ecols, count),
+        in_specs=[vmem] * (3 + count),
+        out_specs=[vmem] * (count + 2),
+        out_shape=[array(*x.shape) for x in state] + [field, array(devices, LANES)],
+        input_output_aliases={3 + i: i for i in range(count)},
         compiler_params=pltpu.CompilerParams(vmem_limit_bytes=24 << 20),
         name="krylov",
     )(right, left, scale, *state)
-    mass_sum, lap_sum, u0, w3 = out[3], out[4], out[6], out[7]
-    u1, u2, part = out[10:]
+    mass_sum, lap_sum, u0, w3, u1 = out[3], out[4], out[6], out[7], out[10]
+    u2, part = out[count:]
 
     parts = lax.all_to_all(part, AXES, 0, 0, tiled=True)
 

time: 55.4 us -> 54.2 us (0.978)
  waiting for transfers between devices: 8.07 us -> 6.71 us
    ppermute x4, waiting for transfers between devices: 8.07 us -> 6.71 us  [shift(): lax.ppermute(x, axis, [(i, (i + step) % count) for i in range(count)])]
  transfers between devices with their start and end apart: 4 -> 4, of which waited for: 3 -> 3; matrix products, arithmetic and copies ran while one was open for 0% -> 0% of each run, Pallas kernels for 4% -> 6%
where the time goes in v5:
time: 54.2 us; the launch traced here: 54.1 us
  blocking collectives  25.6 us (47%)
  Pallas kernels  15.1 us (28%)
  waiting for transfers between devices  6.71 us (12%)
  starting transfers between devices  5.93 us (11%)
  between operations  0.65 us (1%)
    all_to_all x1, blocking collectives, shards(): parts = lax.all_to_all(part, AXES, 0, 0, tiled=True)  25.6 us
    ppermute x4, waiting for transfers between devices, shift(): lax.ppermute(x, axis, [(i, (i + step) % count) for i in range(count)])  6.71 us
    ppermute x4, starting transfers between devices, shift(): lax.ppermute(x, axis, [(i, (i + step) % count) for i in range(count)])  5.93 us
    pallas_call x1, Pallas kernels, shards(): pl.pallas_call(functools.partial(krylov_kernel, rows, ecols, count), in_s...  5.6 us
    pallas_call x1, Pallas kernels, shards(): pl.pallas_call(prep_kernel, in_specs=[vmem] * 2, out_specs=[vmem] * 13, o...  3.48 us
    pallas_call x1, Pallas kernels, shards(): pl.pallas_call(combine_kernel, in_specs=[vmem] * 8, out_specs=[anywhere]...  3.19 us
    pallas_call x1, Pallas kernels, shards(): pl.pallas_call(load_kernel, in_specs=[anywhere] * 4, out_specs=[vmem] * 4...  1.66 us
    pallas_call x1, Pallas kernels, shards(): pl.pallas_call(functools.partial(spread_kernel, rows), grid=(halves,), in...  1.21 us
  transfers between devices with their start and end apart: 4, of which 3 were waited for; matrix products, arithmetic and copies ran while one was open for 0% of the time, Pallas kernels for 6%

profile of v5, /device:TPU:1, one launch (start us, length us, event | category | flops | bytes accessed | tf_op | source)
XLA Modules:
  0.0 54.1 jit_solution(17299626216845988206)
XLA Ops:
  0.6 1.7 %load.1 = (f32[14,16,256]{2,1,0:T(8,128)S(1)}, f32[14,16,256]{2,1,0:T(8,128)S(1)}, f32[14,96,256]{2,1,0:T(8,128)S(1)}, f32[3,128]{1,0:T(4,128)S(1)}) custom-call(f32[12,96,256]{2,1,0:T(8,128)} %f_hbm.1, f32[96,256]{1,0:T(8,128)} %metric_hbm.1, f32[96,256]{1,0:T(8,128)} %jacobian_hbm.1, f32[12]{0:T(128)} %scale_hbm.1), custom_call_target="tpu_custom_call" | custom-call | tf_op jit(solution)/shard_map/load/pallas_call | solution.py:430
  2.3 3.1 %collective-permute-start = (f32[14,16,256]{2,1,0:T(8,128)S(1)}, f32[14,16,256]{2,1,0:T(8,128)S(1)}, u32[]{:S(2)}, u32[]{:S(2)}) collective-permute-start(f32[14,16,256]{2,1,0:T(8,128)S(1)} %get-tuple-element.30), channel_id=1, source_target_pairs={{0,4},{4,8},{8,12},{12,16},{16,20},{20,24},{24,28},{28,32},{32,36}... | collective-permute-start | bytes 688136 | tf_op jit(solution)/shard_map/ppermute | solution.py:425
  5.4 0.3 collective-permute-start.1
  5.7 2.7 %collective-permute-done.up_ref = f32[14,16,256]{2,1,0:T(8,128)S(1)} collective-permute-done((f32[14,16,256]{2,1,0:T(8,128)S(1)}, f32[14,16,256]{2,1,0:T(8,128)S(1)}, u32[]{:S(2)}, u32[]{:S(2)}) %collective-permute-start) | collective-permute-done | bytes 229408 | tf_op jit(solution)/shard_map/ppermute | solution.py:425
  8.4 2.5 %collective-permute-done.1.down_ref = f32[14,16,256]{2,1,0:T(8,128)S(1)} collective-permute-done((f32[14,16,256]{2,1,0:T(8,128)S(1)}, f32[14,16,256]{2,1,0:T(8,128)S(1)}, u32[]{:S(2)}, u32[]{:S(2)}) %collective-permute-start.1) | collective-permute-done | bytes 229408 | tf_op jit(solution)/shard_map/ppermute | solution.py:425
  10.8 1.2 %spread.1 = (f32[64,64,128]{2,1,0:T(8,128)S(1)}, f32[64,4,128]{2,1,0:T(4,128)S(1)}, f32[64,4,128]{2,1,0:T(4,128)S(1)}) custom-call(f32[14,96,256]{2,1,0:T(8,128)S(1)} %get-tuple-element.29.f_ref, f32[14,16,256]{2,1,0:T(8,128)S(1)} %collective-permute-done.up_ref, f32[14,16,256]{2,1,0:T(8,128)S(1)} %collective-permute-done.1.down_ref), custom_call_target="tpu_custom_call" | custom-call | tf_op jit(solution)/shard_map/spread/pallas_call | solution.py:448
  12.1 2.6 %collective-permute-start.2 = (f32[64,4,128]{2,1,0:T(4,128)S(1)}, f32[64,4,128]{2,1,0:T(4,128)S(1)}, u32[]{:S(2)}, u32[]{:S(2)}) collective-permute-start(f32[64,4,128]{2,1,0:T(4,128)S(1)} %get-tuple-element.32), channel_id=1, source_target_pairs={{0,3},{1,0},{2,1},{3,2},{4,7},{5,4},{6,5},{7,6},{8,11},{9,8},{10,9... | collective-permute-start | bytes 393224 | tf_op jit(solution)/shard_map/ppermute | solution.py:425
  14.6 0.0 collective-permute-start.3
  14.6 3.5 %prep.1 = (f32[48,72,128]{2,1,0:T(8,128)S(1)}, f32[24,72,128]{2,1,0:T(8,128)S(1)}, f32[24,72,128]{2,1,0:T(8,128)S(1)}, f32[16,72,128]{2,1,0:T(8,128)S(1)}, f32[1...) custom-call(f32[64,64,128]{2,1,0:T(8,128)S(1)} %get-tuple-element.35, ...), custom_call_target="tpu_custom_call" | custom-call | flops 20000000 | tf_op jit(solution)/shard_map/prep/pallas_call | solution.py:478
  18.1 0.0 collective-permute-done.2.right_ref
  18.1 1.5 %collective-permute-done.3.left_ref = f32[64,4,128]{2,1,0:T(4,128)S(1)} collective-permute-done((f32[64,4,128]{2,1,0:T(4,128)S(1)}, f32[64,4,128]{2,1,0:T(4,128)S(1)}, u32[]{:S(2)}, u32[]{:S(2)}) %collective-permute-start.3) | collective-permute-done | bytes 131104 | tf_op jit(solution)/shard_map/ppermute | solution.py:425
  19.6 5.6 %krylov.1 = (f32[48,72,128]{2,1,0:T(8,128)S(1)}, f32[24,72,128]{2,1,0:T(8,128)S(1)}, f32[24,72,128]{2,1,0:T(8,128)S(1)}, f32[16,72,128]{2,1,0:T(8,128)S(1)}, f32...) custom-call(f32[64,4,128]{2,1,0:T(4,128)S(1)} %collective-permute-do, ...), custom_call_target="tpu_custom_call", output_to_operand_aliasing={{0}: (3, {}), {1}: (4, {}), {2}: (5, {}), {3}: (6, {}), {4}... | custom-call | tf_op jit(solution)/shard_map/krylov/pallas_call | solution.py:491
  25.2 25.6 %all_to_all.11 = f32[256,1,128]{2,1,0:T(1,128)S(1)} all-to-all(f32[256,1,128]{2,1,0:T(1,128)S(1)} %bitcast.5), channel_id=1, replica_groups=mesh['curve'=64,'sub'=4] {'curve','sub'}, dimensions={0} | all-to-all | bytes 262144 | tf_op jit(solution)/shard_map/all_to_all | solution.py:503
  50.9 3.2 %combine.1 = (f32[12,96,256]{2,1,0:T(8,128)}, f32[12,96,256]{2,1,0:T(8,128)}) custom-call(f32[256,128]{1,0:T(8,128)S(1)} %bitcast.4, f32[3,128]{1,0:T(4,128)S(1)} %get-tuple-element.34.scale_ref, f32[48,72,128]{2,1,0:T(8,128)S(1)} %get-tuple-element.50.u0_ref, f32[48,72,128]{2,1,0:T(8,128)S(1)} %get-tuple-element.51.u1_ref, ...), custom_call_target="tpu_custom_call" | custom-call | tf_op jit(solution)/shard_map/combine/pallas_call | solution.py:507
Async XLA Ops:
  2.3 6.1 %collective-permute-start = (f32[14,16,256]{2,1,0:T(8,128)S(1)}, f32[14,16,256]{2,1,0:T(8,128)S(1)}, u32[]{:S(2)}, u32[]{:S(2)}) collective-permute-start(f32[14,16,256]{2,1,0:T(8,128)S(1)} %get-tuple-element.30), channel_id=1, source_target_pairs={{0,4},{4,8},{8,12},{12,16},{16,20},{20,24},{24,28},{28,32},{32,36}... | collective-permute-start | bytes 688136 | tf_op jit(solution)/shard_map/ppermute | solution.py:425
  5.4 5.4 %collective-permute-start.1 = (f32[14,16,256]{2,1,0:T(8,128)S(1)}, f32[14,16,256]{2,1,0:T(8,128)S(1)}, u32[]{:S(2)}, u32[]{:S(2)}) collective-permute-start(f32[14,16,256]{2,1,0:T(8,128)S(1)} %get-tuple-element.31), channel_id=1, source_target_pairs={{0,252},{4,0},{8,4},{12,8},{16,12},{20,16},{24,20},{28,24},{32,28}... | collective-permute-start | bytes 688136 | tf_op jit(solution)/shard_map/ppermute | solution.py:425
  12.1 6.0 %collective-permute-start.2 = (f32[64,4,128]{2,1,0:T(4,128)S(1)}, f32[64,4,128]{2,1,0:T(4,128)S(1)}, u32[]{:S(2)}, u32[]{:S(2)}) collective-permute-start(f32[64,4,128]{2,1,0:T(4,128)S(1)} %get-tuple-element.32), channel_id=1, source_target_pairs={{0,3},{1,0},{2,1},{3,2},{4,7},{5,4},{6,5},{7,6},{8,11},{9,8},{10,9... | collective-permute-start | bytes 393224 | tf_op jit(solution)/shard_map/ppermute | solution.py:425
  14.6 5.0 %collective-permute-start.3 = (f32[64,4,128]{2,1,0:T(4,128)S(1)}, f32[64,4,128]{2,1,0:T(4,128)S(1)}, u32[]{:S(2)}, u32[]{:S(2)}) collective-permute-start(f32[64,4,128]{2,1,0:T(4,128)S(1)} %get-tuple-element.33), channel_id=1, source_target_pairs={{0,1},{1,2},{2,3},{3,0},{4,5},{5,6},{6,7},{7,4},{8,9},{9,10},{10,1... | collective-permute-start | bytes 393224 | tf_op jit(solution)/shard_map/ppermute | solution.py:425

commit v6 on v5

--- a/solution.py
+++ b/solution.py
@@ -107,6 +107,15 @@
     return f01 + f02 + f03, f12 + f13 - f01, f23 - f02 - f12, f03 + f13 + f23
 
 
+def over_rows(table):
+    i = lax.broadcasted_iota(jnp.int32, (LANES, LANES), 0)
+    j = lax.broadcasted_iota(jnp.int32, (LANES, LANES), 1)
+    same = jnp.where(i % PACK == j % PACK, 1.0, 0.0).astype(jnp.float32)
+    return jnp.dot(
+        table, same, precision=lax.Precision.HIGHEST, preferred_element_type=jnp.float32
+    )
+
+
 def tile(t):
     return pl.ds(pl.multiple_of(t * 8, 8), 8)
 
@@ -131,7 +140,7 @@
     return first, last
 
 
-def prepare(t, fetch, scale_ref, mass_ref, krow, kcol, mass_sum_ref, lap_sum_ref, minv, u0_ref, source_ref, cedge, redge):
+def prepare(t, fetch, scale_ref, mass_ref, krow, kcol, diag_ref, minv, u0_ref, source_ref, cedge, redge):
     groups = u0_ref.shape[0] // 16
     lane = lax.broadcasted_iota(jnp.int32, (8, LANES), 1)
     even = lane % 2 == 0
@@ -165,13 +174,11 @@
             less(line, q, kc)
     for a, b in grid:
         lap[a, b] = -lap[a, b]
-    for values, out, base in ((mass, mass_sum_ref, 0), (lap, lap_sum_ref, 4)):
+    for values, base in ((mass, 0), (lap, 4)):
         for b in range(4):
             values[0, b], values[3, b] = join_rows(values[0, b], values[3, b])
             for a in range(4):
-                if b in (1, 2):
-                    out[a * 4 + b, tile(t), :] = values[a, b]
-                else:
+                if b in (0, 3):
                     cedge[2 * (base + a) + b // 3, spare(t), :] = values[a, b]
     for group in range(groups):
         for b in range(4):
@@ -180,26 +187,27 @@
             for a in range(4):
                 p = plane(group, a, b)
                 if b in (1, 2):
-                    inverse = 1.0 / (mass[a, b] + scales[group] * lap[a, b])
+                    diag = mass[a, b] + scales[group] * lap[a, b]
+                    inverse = 1.0 / diag
+                    diag_ref[p, tile(t), :] = diag
                     u0_ref[p, tile(t), :] = column[a] * inverse
                     minv[p, tile(t), :] = inverse * scales[group]
                 else:
                     redge[2 * (group * 4 + a) + b // 3, spare(t), :] = column[a]
 
 
-def finish(a, low, high, scale_ref, mass_sum_ref, lap_sum_ref, minv, u0_ref, cedge, redge):
+def finish(a, low, high, scale_ref, diag_ref, minv, u0_ref, cedge, redge):
     groups = u0_ref.shape[0] // 16
     span = slice(low, high)
     mass_sums = join_cols(cedge, a, low, high)
     lap_sums = join_cols(cedge, 4 + a, low, high)
-    for side, b in enumerate((0, 3)):
-        mass_sum_ref[a * 4 + b, span, :] = mass_sums[side]
-        lap_sum_ref[a * 4 + b, span, :] = lap_sums[side]
     for group in range(groups):
         scale = scale_ref[group : group + 1, :]
         source = join_cols(redge, group * 4 + a, low, high)
         for side, b in enumerate((0, 3)):
-            inverse = 1.0 / (mass_sums[side] + scale * lap_sums[side])
+            diag = mass_sums[side] + scale * lap_sums[side]
+            inverse = 1.0 / diag
+            diag_ref[plane(group, a, b), span, :] = diag
             u0_ref[plane(group, a, b), span, :] = source[side] * inverse
             minv[plane(group, a, b), span, :] = inverse * scale
 
@@ -253,8 +261,8 @@
 
 
 def prep_kernel(t_ref, scale_ref, *refs):
-    state, (u1_ref, edge, sums_ref) = refs[:10], refs[10:]
-    mass_ref, krow, kcol, mass_sum_ref, lap_sum_ref, minv, u0_ref, w_ref, cedge, redge = state
+    state, (u1_ref, edge, sums_ref) = refs[:9], refs[9:]
+    mass_ref, krow, kcol, diag_ref, minv, u0_ref, w_ref, cedge, redge = state
     cols = t_ref.shape[1]
 
     @pl.loop(0, cols // 8)
@@ -263,7 +271,7 @@
 
     @pl.loop(0, 4)
     def _(a):
-        finish(a, 8, cols - 8, scale_ref, mass_sum_ref, lap_sum_ref, minv, u0_ref, cedge, redge)
+        finish(a, 8, cols - 8, scale_ref, diag_ref, minv, u0_ref, cedge, redge)
 
     zero = jnp.zeros((8, LANES), jnp.float32)
     sums = lax.fori_loop(
@@ -279,9 +287,9 @@
 
 
 def krylov_kernel(own_rows, cols, count, right_ref, left_ref, scale_ref, *refs):
-    state = refs[count : count + 10]
-    u1_ref, edge, sums_ref, u2_ref, part_ref = refs[count + 10 :]
-    mass_ref, krow, kcol, mass_sum_ref, lap_sum_ref, minv, u0_ref, w_ref, cedge, redge = state
+    state = refs[count : count + 9]
+    u1_ref, edge, sums_ref, u2_ref, part_ref = refs[count + 9 :]
+    mass_ref, krow, kcol, diag_ref, minv, u0_ref, w_ref, cedge, redge = state
     groups = u0_ref.shape[0] // 16
     total = u0_ref.shape[1]
     tiles = total // 8
@@ -298,7 +306,7 @@
         for group in range(groups):
             wrap_cols(redge, group * 4 + a, total)
         for low, high in ((0, 8), (cols - 8, total)):
-            finish(a, low, high, scale_ref, mass_sum_ref, lap_sum_ref, minv, u0_ref, cedge, redge)
+            finish(a, low, high, scale_ref, diag_ref, minv, u0_ref, cedge, redge)
 
     zero = jnp.zeros((8, LANES), jnp.float32)
     shared = (mass_ref, krow, kcol, minv, w_ref, edge)
@@ -340,16 +348,13 @@
     lanes = lax.broadcasted_iota(jnp.int32, table.shape, 1)
     lines = lax.broadcasted_iota(jnp.int32, table.shape, 0)
     table = jnp.where(lanes < own_rows // 4 * PACK, table, 0.0)
-    shift = PACK
-    while shift < LANES:
-        table = table + pltpu.roll(table, shift, 1)
-        shift *= 2
+    table = over_rows(table)
     table = jnp.where(lanes // PACK == lines, table, 0.0)
     part_ref[...] = jnp.broadcast_to(jnp.sum(table, axis=0, keepdims=True), part_ref.shape)
 
 
 def combine_kernel(
-    parts_ref, scale_ref, u0_ref, u1_ref, u2_ref, w_ref, mass_sum_ref, lap_sum_ref, sol_hbm, res_hbm, sol, res, xs, xt, sems
+    parts_ref, scale_ref, u0_ref, u1_ref, u2_ref, w_ref, diag_ref, sol_hbm, res_hbm, sol, res, xs, xt, sems
 ):
     halves, modes, rows, _ = sol.shape
     groups = modes // PACK
@@ -360,10 +365,7 @@
     lanes = lax.broadcasted_iota(jnp.int32, table.shape, 1)
     lines = lax.broadcasted_iota(jnp.int32, table.shape, 0)
     table = jnp.where(lanes // PACK == lines, table, 0.0)
-    shift = PACK
-    while shift < LANES:
-        table = table + pltpu.roll(table, shift, 1)
-        shift *= 2
+    table = over_rows(table)
     b0, g00, g01, g11, g12, g22 = [table[q * groups : (q + 1) * groups] for q in range(6)]
     g02 = g11
     b1 = g00 - b0
@@ -384,16 +386,15 @@
         span = slice(half * per_half, (half + 1) * per_half)
         for group in range(groups):
             k0, k1, k2 = [c[group : group + 1, :] for c in (c0, c1, c2)]
-            scale = scale_ref[group : group + 1, :]
+            r0, r1, r2 = 1.0 - k0, k0 + k1, k2 * scale_ref[group : group + 1, :]
             for a in range(4):
                 slot = group * 4 + a
                 for b in range(4):
                     p = plane(group, a, b)
                     u0, u1, u2 = u0_ref[p, span, :], u1_ref[p, span, :], u2_ref[p, span, :]
-                    diag = mass_sum_ref[a * 4 + b, span, :] + scale * lap_sum_ref[a * 4 + b, span, :]
                     xs[0, slot, pl.ds(b, per_half, stride=4), :] = k0 * u0 + k1 * u1 + k2 * u2
                     xs[1, slot, pl.ds(b, per_half, stride=4), :] = (
-                        diag * (u0 - k0 * (u1 + u0) - k1 * (u2 + u1)) - (k2 * scale) * w_ref[p, span, :]
+                        diag_ref[p, span, :] * (r0 * u0 - r1 * u1 - k1 * u2) - r2 * w_ref[p, span, :]
                     )
                 for i, out in enumerate((sol, res)):
                     xt[i, slot] = xs[i, slot].T
@@ -474,12 +475,11 @@
     total = ecols + 2 * GHOST
     field = array(16 * groups, total, LANES)
     lines = array(24, total, LANES)
-    nodes = array(16, total, LANES)
     state = pl.pallas_call(
         prep_kernel,
         in_specs=[vmem] * 2,
-        out_specs=[vmem] * 13,
-        out_shape=[field, lines, lines, nodes, nodes, field, field, field]
+        out_specs=[vmem] * 12,
+        out_shape=[field, lines, lines, field, field, field, field]
         + [array(16, total + 16, LANES), array(8 * groups, total + 16, LANES)]
         + [field, array(8 * groups, total + 16, LANES), array(2 * groups, 8, LANES)],
         compiler_params=pltpu.CompilerParams(vmem_limit_bytes=24 << 20),
@@ -497,7 +497,7 @@
         compiler_params=pltpu.CompilerParams(vmem_limit_bytes=24 << 20),
         name="krylov",
     )(right, left, scale, *state)
-    mass_sum, lap_sum, u0, w3, u1 = out[3], out[4], out[6], out[7], out[10]
+    diag, u0, w3, u1 = out[3], out[5], out[6], out[9]
     u2, part = out[count:]
 
     parts = lax.all_to_all(part, AXES, 0, 0, tiled=True)
@@ -506,7 +506,7 @@
     return tuple(
         pl.pallas_call(
             combine_kernel,
-            in_specs=[vmem] * 8,
+            in_specs=[vmem] * 7,
             out_specs=[anywhere] * 2,
             out_shape=[out] * 2,
             scratch_shapes=[
@@ -518,7 +518,7 @@
             ],
             compiler_params=pltpu.CompilerParams(vmem_limit_bytes=20 << 20),
             name="combine",
-        )(parts, scale, u0, u1, u2, w3, mass_sum, lap_sum)
+        )(parts, scale, u0, u1, u2, w3, diag)
     )
 
 

time: 54.2 us -> 53.5 us (0.987)
  Pallas kernels: 15.1 us -> 14.5 us
  transfers between devices with their start and end apart: 4 -> 4, of which waited for: 3 -> 3; matrix products, arithmetic and copies ran while one was open for 0% -> 0% of each run, Pallas kernels for 6% -> 7%
where the time goes in v6:
time: 53.5 us; the launch traced here: 53.4 us
  blocking collectives  25.6 us (48%)
  Pallas kernels  14.5 us (27%)
  waiting for transfers between devices  6.69 us (13%)
  starting transfers between devices  5.93 us (11%)
  between operations  0.66 us (1%)
    all_to_all x1, blocking collectives, shards(): parts = lax.all_to_all(part, AXES, 0, 0, tiled=True)  25.6 us
    ppermute x4, waiting for transfers between devices, shift(): lax.ppermute(x, axis, [(i, (i + step) % count) for i in range(count)])  6.69 us
    ppermute x4, starting transfers between devices, shift(): lax.ppermute(x, axis, [(i, (i + step) % count) for i in range(count)])  5.93 us
    pallas_call x1, Pallas kernels, shards(): pl.pallas_call(functools.partial(krylov_kernel, rows, ecols, count), in_s...  5.43 us
    pallas_call x1, Pallas kernels, shards(): pl.pallas_call(prep_kernel, in_specs=[vmem] * 2, out_specs=[vmem] * 12, o...  3.5 us
    pallas_call x1, Pallas kernels, shards(): pl.pallas_call(combine_kernel, in_specs=[vmem] * 7, out_specs=[anywhere]...  2.65 us
    pallas_call x1, Pallas kernels, shards(): pl.pallas_call(load_kernel, in_specs=[anywhere] * 4, out_specs=[vmem] * 4...  1.66 us
    pallas_call x1, Pallas kernels, shards(): pl.pallas_call(functools.partial(spread_kernel, rows), grid=(halves,), in...  1.21 us
  transfers between devices with their start and end apart: 4, of which 3 were waited for; matrix products, arithmetic and copies ran while one was open for 0% of the time, Pallas kernels for 7%

profile of v6, /device:TPU:1, one launch (start us, length us, event | category | flops | bytes accessed | tf_op | source)
XLA Modules:
  0.0 53.4 jit_solution(6068474944852134056)
XLA Ops:
  0.6 1.7 %load.1 = (f32[14,16,256]{2,1,0:T(8,128)S(1)}, f32[14,16,256]{2,1,0:T(8,128)S(1)}, f32[14,96,256]{2,1,0:T(8,128)S(1)}, f32[3,128]{1,0:T(4,128)S(1)}) custom-call(f32[12,96,256]{2,1,0:T(8,128)} %f_hbm.1, f32[96,256]{1,0:T(8,128)} %metric_hbm.1, f32[96,256]{1,0:T(8,128)} %jacobian_hbm.1, f32[12]{0:T(128)} %scale_hbm.1), custom_call_target="tpu_custom_call" | custom-call | tf_op jit(solution)/shard_map/load/pallas_call | solution.py:431
  2.3 3.1 %collective-permute-start = (f32[14,16,256]{2,1,0:T(8,128)S(1)}, f32[14,16,256]{2,1,0:T(8,128)S(1)}, u32[]{:S(2)}, u32[]{:S(2)}) collective-permute-start(f32[14,16,256]{2,1,0:T(8,128)S(1)} %get-tuple-element.28), channel_id=1, source_target_pairs={{0,4},{4,8},{8,12},{12,16},{16,20},{20,24},{24,28},{28,32},{32,36}... | collective-permute-start | bytes 688136 | tf_op jit(solution)/shard_map/ppermute | solution.py:426
  5.4 0.3 collective-permute-start.1
  5.7 2.7 %collective-permute-done.up_ref = f32[14,16,256]{2,1,0:T(8,128)S(1)} collective-permute-done((f32[14,16,256]{2,1,0:T(8,128)S(1)}, f32[14,16,256]{2,1,0:T(8,128)S(1)}, u32[]{:S(2)}, u32[]{:S(2)}) %collective-permute-start) | collective-permute-done | bytes 229408 | tf_op jit(solution)/shard_map/ppermute | solution.py:426
  8.4 2.5 %collective-permute-done.1.down_ref = f32[14,16,256]{2,1,0:T(8,128)S(1)} collective-permute-done((f32[14,16,256]{2,1,0:T(8,128)S(1)}, f32[14,16,256]{2,1,0:T(8,128)S(1)}, u32[]{:S(2)}, u32[]{:S(2)}) %collective-permute-start.1) | collective-permute-done | bytes 229408 | tf_op jit(solution)/shard_map/ppermute | solution.py:426
  10.8 1.2 %spread.1 = (f32[64,64,128]{2,1,0:T(8,128)S(1)}, f32[64,4,128]{2,1,0:T(4,128)S(1)}, f32[64,4,128]{2,1,0:T(4,128)S(1)}) custom-call(f32[14,96,256]{2,1,0:T(8,128)S(1)} %get-tuple-element.27.f_ref, f32[14,16,256]{2,1,0:T(8,128)S(1)} %collective-permute-done.up_ref, f32[14,16,256]{2,1,0:T(8,128)S(1)} %collective-permute-done.1.down_ref), custom_call_target="tpu_custom_call" | custom-call | tf_op jit(solution)/shard_map/spread/pallas_call | solution.py:449
  12.1 2.6 %collective-permute-start.2 = (f32[64,4,128]{2,1,0:T(4,128)S(1)}, f32[64,4,128]{2,1,0:T(4,128)S(1)}, u32[]{:S(2)}, u32[]{:S(2)}) collective-permute-start(f32[64,4,128]{2,1,0:T(4,128)S(1)} %get-tuple-element.30), channel_id=1, source_target_pairs={{0,3},{1,0},{2,1},{3,2},{4,7},{5,4},{6,5},{7,6},{8,11},{9,8},{10,9... | collective-permute-start | bytes 393224 | tf_op jit(solution)/shard_map/ppermute | solution.py:426
  14.6 0.0 collective-permute-start.3
  14.6 3.5 %prep.1 = (f32[48,72,128]{2,1,0:T(8,128)S(1)}, f32[24,72,128]{2,1,0:T(8,128)S(1)}, f32[24,72,128]{2,1,0:T(8,128)S(1)}, f32[48,72,128]{2,1,0:T(8,128)S(1)}, f32[4...) custom-call(f32[64,64,128]{2,1,0:T(8,128)S(1)} %get-tuple-element.33, ...), custom_call_target="tpu_custom_call" | custom-call | flops 20000000 | tf_op jit(solution)/shard_map/prep/pallas_call | solution.py:478
  18.1 0.0 collective-permute-done.2.right_ref
  18.1 1.5 %collective-permute-done.3.left_ref = f32[64,4,128]{2,1,0:T(4,128)S(1)} collective-permute-done((f32[64,4,128]{2,1,0:T(4,128)S(1)}, f32[64,4,128]{2,1,0:T(4,128)S(1)}, u32[]{:S(2)}, u32[]{:S(2)}) %collective-permute-start.3) | collective-permute-done | bytes 131104 | tf_op jit(solution)/shard_map/ppermute | solution.py:426
  19.6 5.4 %krylov.1 = (f32[48,72,128]{2,1,0:T(8,128)S(1)}, f32[24,72,128]{2,1,0:T(8,128)S(1)}, f32[24,72,128]{2,1,0:T(8,128)S(1)}, f32[48,72,128]{2,1,0:T(8,128)S(1)}, f32...) custom-call(f32[64,4,128]{2,1,0:T(4,128)S(1)} %collective-permute-do, ...), custom_call_target="tpu_custom_call", output_to_operand_aliasing={{0}: (3, {}), {1}: (4, {}), {2}: (5, {}), {3}: (6, {}), {4}... | custom-call | tf_op jit(solution)/shard_map/krylov/pallas_call | solution.py:491
  25.1 25.6 %all_to_all.11 = f32[256,1,128]{2,1,0:T(1,128)S(1)} all-to-all(f32[256,1,128]{2,1,0:T(1,128)S(1)} %bitcast.5), channel_id=1, replica_groups=mesh['curve'=64,'sub'=4] {'curve','sub'}, dimensions={0} | all-to-all | bytes 262144 | tf_op jit(solution)/shard_map/all_to_all | solution.py:503
  50.7 2.7 %combine.1 = (f32[12,96,256]{2,1,0:T(8,128)}, f32[12,96,256]{2,1,0:T(8,128)}) custom-call(f32[256,128]{1,0:T(8,128)S(1)} %bitcast.4, f32[3,128]{1,0:T(4,128)S(1)} %get-tuple-element.32.scale_ref, f32[48,72,128]{2,1,0:T(8,128)S(1)} %get-tuple-element.47.u0_ref, f32[48,72,128]{2,1,0:T(8,128)S(1)} %get-tuple-element.48.u1_ref, ...), custom_call_target="tpu_custom_call" | custom-call | tf_op jit(solution)/shard_map/combine/pallas_call | solution.py:507
Async XLA Ops:
  2.3 6.1 %collective-permute-start = (f32[14,16,256]{2,1,0:T(8,128)S(1)}, f32[14,16,256]{2,1,0:T(8,128)S(1)}, u32[]{:S(2)}, u32[]{:S(2)}) collective-permute-start(f32[14,16,256]{2,1,0:T(8,128)S(1)} %get-tuple-element.28), channel_id=1, source_target_pairs={{0,4},{4,8},{8,12},{12,16},{16,20},{20,24},{24,28},{28,32},{32,36}... | collective-permute-start | bytes 688136 | tf_op jit(solution)/shard_map/ppermute | solution.py:426
  5.4 5.4 %collective-permute-start.1 = (f32[14,16,256]{2,1,0:T(8,128)S(1)}, f32[14,16,256]{2,1,0:T(8,128)S(1)}, u32[]{:S(2)}, u32[]{:S(2)}) collective-permute-start(f32[14,16,256]{2,1,0:T(8,128)S(1)} %get-tuple-element.29), channel_id=1, source_target_pairs={{0,252},{4,0},{8,4},{12,8},{16,12},{20,16},{24,20},{28,24},{32,28}... | collective-permute-start | bytes 688136 | tf_op jit(solution)/shard_map/ppermute | solution.py:426
  12.1 6.1 %collective-permute-start.2 = (f32[64,4,128]{2,1,0:T(4,128)S(1)}, f32[64,4,128]{2,1,0:T(4,128)S(1)}, u32[]{:S(2)}, u32[]{:S(2)}) collective-permute-start(f32[64,4,128]{2,1,0:T(4,128)S(1)} %get-tuple-element.30), channel_id=1, source_target_pairs={{0,3},{1,0},{2,1},{3,2},{4,7},{5,4},{6,5},{7,6},{8,11},{9,8},{10,9... | collective-permute-start | bytes 393224 | tf_op jit(solution)/shard_map/ppermute | solution.py:426
  14.6 5.0 %collective-permute-start.3 = (f32[64,4,128]{2,1,0:T(4,128)S(1)}, f32[64,4,128]{2,1,0:T(4,128)S(1)}, u32[]{:S(2)}, u32[]{:S(2)}) collective-permute-start(f32[64,4,128]{2,1,0:T(4,128)S(1)} %get-tuple-element.31), channel_id=1, source_target_pairs={{0,1},{1,2},{2,3},{3,0},{4,5},{5,6},{6,7},{7,4},{8,9},{9,10},{10,1... | collective-permute-start | bytes 393224 | tf_op jit(solution)/shard_map/ppermute | solution.py:426

commit v7 on v6

--- a/solution.py
+++ b/solution.py
@@ -13,7 +13,7 @@
 PACK = 4
 LANES = 128
 AXES = ("curve", "sub")
-LOAD_LIMIT = 4 << 20
+RIM = 2 * GHOST * PACK
 
 
 def gll_tables():
@@ -39,21 +39,26 @@
     return (group * 4 + a) * 4 + b
 
 
-def load_kernel(f_hbm, metric_hbm, jacobian_hbm, scale_hbm, top, bottom, fields, scale_ref, scales, sems):
+def load_kernel(f_hbm, metric_hbm, jacobian_hbm, scale_hbm, top, bottom, fields, scale_ref, scales, sems, scale_sem):
     modes, rows, _ = f_hbm.shape
-    halo = top.shape[1]
-    scale_copy = pltpu.make_async_copy(scale_hbm, scales, sems.at[3, 0])
+    halves, _, halo, _ = top.shape
+    scale_copy = pltpu.make_async_copy(scale_hbm, scales, scale_sem)
     scale_copy.start()
     copies = []
     for part, (out, at, size) in enumerate(
         ((top, 0, halo), (bottom, rows - halo, halo), (fields, 0, rows))
     ):
         span = pl.ds(at, size)
-        copies += [
-            pltpu.make_async_copy(f_hbm.at[:, span, :], out.at[pl.ds(0, modes)], sems.at[part, 0]),
-            pltpu.make_async_copy(metric_hbm.at[span, :], out.at[modes], sems.at[part, 1]),
-            pltpu.make_async_copy(jacobian_hbm.at[span, :], out.at[modes + 1], sems.at[part, 2]),
-        ]
+        for half in range(halves):
+            columns = pl.ds(half * LANES, LANES)
+            for i, (source, target) in enumerate(
+                (
+                    (f_hbm.at[:, span, columns], out.at[half, pl.ds(0, modes)]),
+                    (metric_hbm.at[span, columns], out.at[half, modes]),
+                    (jacobian_hbm.at[span, columns], out.at[half, modes + 1]),
+                )
+            ):
+                copies.append(pltpu.make_async_copy(source, target, sems.at[part, half, i]))
     for copy in copies:
         copy.start()
     scale_copy.wait()
@@ -67,37 +72,61 @@
         copy.wait()
 
 
-def spread_kernel(rows, f_ref, up_ref, down_ref, t_ref, low_ref, high_ref, xs, xt):
-    half = pl.program_id(0)
+def spread_kernel(fields_ref, t_ref, xs, xt):
+    halves, stack, rows, _ = fields_ref.shape
     own = rows // 4
-    groups = (f_ref.shape[0] - 2) // PACK
+    groups = (stack - 2) // PACK
     per_half = LANES // 4
+    for half in range(halves):
+        for group in range(groups + 1):
+            for a in range(4):
+                at = (half * (groups + 1) + group) * 4 + a
+                for m in range(PACK):
+                    index = group * PACK + (m if group < groups else m % 2)
+                    xs[at, pl.ds(RIM + m, own, stride=PACK), :] = fields_ref[
+                        half, index, pl.ds(a, own, stride=4), :
+                    ]
+                xs[at, :RIM, :] = jnp.zeros((RIM, LANES), jnp.float32)
+                xt[at] = xs[at].T
+                for b in range(4):
+                    t_ref[plane(group, a, b), half * per_half : (half + 1) * per_half, :] = xt[
+                        at, pl.ds(b, per_half, stride=4), :
+                    ]
+
+
+def ghost_kernel(up_ref, down_ref, own_ref, rim_ref, low_ref, high_ref, xs, ends):
+    halves, stack, _, _ = up_ref.shape
+    groups = (stack - 2) // PACK
+    per_half = rim_ref.shape[0] // halves
+    height = rim_ref.shape[2]
+    rim = lax.broadcasted_iota(jnp.int32, (GHOST, LANES), 1) < RIM
+    for half in range(halves):
+        for group in range(groups + 1):
+            at = half * (groups + 1) + group
+            for a in range(4):
+                for m in range(PACK):
+                    index = group * PACK + (m if group < groups else m % 2)
+                    for side, ref in enumerate((down_ref, up_ref)):
+                        start = a * RIM + side * GHOST * PACK + m
+                        xs[at, pl.ds(start, GHOST, stride=PACK), :] = ref[
+                            half, index, pl.ds(a, GHOST, stride=4), :
+                        ]
+            turned = xs[at].T
+            for i in range(per_half):
+                rim_ref[half * per_half + i, group] = turned[i * height : (i + 1) * height]
+    last = rim_ref.shape[0] - 1
+    total = own_ref.shape[1]
+    size = 4 * GHOST
     for group in range(groups + 1):
         for a in range(4):
             at = group * 4 + a
-            for m in range(PACK):
-                index = group * PACK + (m if group < groups else m % 2)
-                mine = f_ref[index, pl.ds(a, own, stride=4), :]
-                xs[at, pl.ds(m, own, stride=PACK), :] = mine
-                xs[at, pl.ds(own * PACK + m, GHOST, stride=PACK), :] = down_ref[
-                    index, pl.ds(a, GHOST, stride=4), :
-                ]
-                xs[at, pl.ds((own + GHOST) * PACK + m, GHOST, stride=PACK), :] = up_ref[
-                    index, pl.ds(a, GHOST, stride=4), :
-                ]
-            xt[at] = xs[at].T
+            for side, x in enumerate((rim_ref[0, group, :size], rim_ref[last, group, height - size :])):
+                ends[side, at] = pltpu.roll(x, LANES - a * RIM, 1) if a else x
             for b in range(4):
-                t_ref[at * 4 + b] = xt[at, pl.ds(b, per_half, stride=4), :]
-
-    @pl.when(half == 0)
-    def _():
-        for p in range(t_ref.shape[0]):
-            low_ref[p] = t_ref[p, :GHOST, :]
-
-    @pl.when(half == pl.num_programs(0) - 1)
-    def _():
-        for p in range(t_ref.shape[0]):
-            high_ref[p] = t_ref[p, per_half - GHOST :, :]
+                p = at * 4 + b
+                picked = pl.ds(b, GHOST, stride=4)
+                low_ref[p] = jnp.where(rim, ends[0, at, picked, :], own_ref[p, :GHOST, :])
+                high_ref[p] = jnp.where(rim, ends[1, at, picked, :], own_ref[p, total - GHOST :, :])
 
 
 def line_operator(coefs, values):
@@ -260,14 +289,22 @@
     return tuple(sums)
 
 
-def prep_kernel(t_ref, scale_ref, *refs):
+def prep_kernel(t_ref, rim_ref, scale_ref, *refs):
     state, (u1_ref, edge, sums_ref) = refs[:9], refs[9:]
     mass_ref, krow, kcol, diag_ref, minv, u0_ref, w_ref, cedge, redge = state
     cols = t_ref.shape[1]
+    rim = lax.broadcasted_iota(jnp.int32, (8, LANES), 1) < RIM
 
     @pl.loop(0, cols // 8)
     def _(t):
-        prepare(t, lambda p: t_ref[p, tile(t), :], scale_ref, *state)
+        def fetch(p):
+            group, a, b = p // 16, p // 4 % 4, p % 4
+            outer = rim_ref[t, group, pl.ds(b, 8, stride=4), :]
+            if a:
+                outer = pltpu.roll(outer, LANES - a * RIM, 1)
+            return jnp.where(rim, outer, t_ref[p, tile(t), :])
+
+        prepare(t, fetch, scale_ref, *state)
 
     @pl.loop(0, 4)
     def _(a):
@@ -286,7 +323,7 @@
         sums_ref[i] = value
 
 
-def krylov_kernel(own_rows, cols, count, right_ref, left_ref, scale_ref, *refs):
+def krylov_kernel(cols, count, right_ref, left_ref, scale_ref, *refs):
     state = refs[count : count + 9]
     u1_ref, edge, sums_ref, u2_ref, part_ref = refs[count + 9 :]
     mass_ref, krow, kcol, diag_ref, minv, u0_ref, w_ref, cedge, redge = state
@@ -347,7 +384,7 @@
     table = jnp.concatenate(rows, axis=0)
     lanes = lax.broadcasted_iota(jnp.int32, table.shape, 1)
     lines = lax.broadcasted_iota(jnp.int32, table.shape, 0)
-    table = jnp.where(lanes < own_rows // 4 * PACK, table, 0.0)
+    table = jnp.where(lanes >= RIM, table, 0.0)
     table = over_rows(table)
     table = jnp.where(lanes // PACK == lines, table, 0.0)
     part_ref[...] = jnp.broadcast_to(jnp.sum(table, axis=0, keepdims=True), part_ref.shape)
@@ -400,7 +437,7 @@
                     xt[i, slot] = xs[i, slot].T
                     for m in range(PACK):
                         out[half, group * PACK + m, pl.ds(a, own, stride=4), :] = xt[
-                            i, slot, pl.ds(m, own, stride=PACK), :
+                            i, slot, pl.ds(RIM + m, own, stride=PACK), :
                         ]
             span_modes = pl.ds(group * PACK, PACK)
             for i, (out, hbm) in enumerate(((sol, sol_hbm), (res, res_hbm))):
@@ -428,46 +465,48 @@
     vmem = pl.BlockSpec(memory_space=pltpu.VMEM)
     anywhere = pl.BlockSpec(memory_space=pl.ANY)
     array = lambda *shape: jax.ShapeDtypeStruct(shape, f32)
+    planes = 16 * (groups + 1)
+    ecols = cols // 4
+    halves = cols // LANES
     top, bottom, fields, scale = pl.pallas_call(
         load_kernel,
         in_specs=[anywhere] * 4,
         out_specs=[vmem] * 4,
-        out_shape=[array(modes + 2, halo, cols)] * 2
-        + [array(modes + 2, rows, cols), array(groups, LANES)],
-        scratch_shapes=[pltpu.SMEM((modes,), f32), pltpu.SemaphoreType.DMA((4, 3))],
-        compiler_params=pltpu.CompilerParams(vmem_limit_bytes=LOAD_LIMIT),
+        out_shape=[array(halves, modes + 2, halo, LANES)] * 2
+        + [array(halves, modes + 2, rows, LANES), array(groups, LANES)],
+        scratch_shapes=[
+            pltpu.SMEM((modes,), f32),
+            pltpu.SemaphoreType.DMA((3, halves, 3)),
+            pltpu.SemaphoreType.DMA,
+        ],
+        compiler_params=pltpu.CompilerParams(vmem_limit_bytes=4 << 20),
         name="load",
     )(*[pltpu.with_memory_space_constraint(x, pltpu.HBM) for x in (forcing, metric, jacobian, mode_scale)])
     up = shift(bottom, "curve", 1)
     down = shift(top, "curve", -1)
 
-    planes = 16 * (groups + 1)
-    ecols = cols // 4
-    halves = cols // LANES
-    per_half = LANES // 4
-    whole = lambda *shape: pl.BlockSpec(shape, lambda h: (0,) * len(shape))
-    spread, low, high = pl.pallas_call(
-        functools.partial(spread_kernel, rows),
-        grid=(halves,),
-        in_specs=[
-            pl.BlockSpec((modes + 2, rows, LANES), lambda h: (0, 0, h)),
-            pl.BlockSpec((modes + 2, halo, LANES), lambda h: (0, 0, h)),
-            pl.BlockSpec((modes + 2, halo, LANES), lambda h: (0, 0, h)),
+    spread = pl.pallas_call(
+        spread_kernel,
+        in_specs=[vmem],
+        out_specs=vmem,
+        out_shape=array(planes, ecols, LANES),
+        scratch_shapes=[pltpu.VMEM((halves * planes // 4, LANES, LANES), f32)] * 2,
+        compiler_params=pltpu.CompilerParams(vmem_limit_bytes=12 << 20),
+        cost_estimate=pl.CostEstimate(flops=10_000_000, bytes_accessed=0, transcendentals=0),
+        name="spread",
+    )(fields)
+    rim, low, high = pl.pallas_call(
+        ghost_kernel,
+        in_specs=[vmem] * 3,
+        out_specs=[vmem] * 3,
+        out_shape=[array(ecols // 8, groups + 1, 32, LANES)] + [array(planes, GHOST, LANES)] * 2,
+        scratch_shapes=[
+            pltpu.VMEM((halves * (groups + 1), LANES, LANES), f32),
+            pltpu.VMEM((2, planes // 4, 4 * GHOST, LANES), f32),
         ],
-        out_specs=[
-            pl.BlockSpec((planes, per_half, LANES), lambda h: (0, h, 0)),
-            whole(planes, GHOST, LANES),
-            whole(planes, GHOST, LANES),
-        ],
-        out_shape=[
-            jax.ShapeDtypeStruct((planes, ecols, LANES), f32),
-            jax.ShapeDtypeStruct((planes, GHOST, LANES), f32),
-            jax.ShapeDtypeStruct((planes, GHOST, LANES), f32),
-        ],
-        scratch_shapes=[pltpu.VMEM((planes // 4, LANES, LANES), f32)] * 2,
         compiler_params=pltpu.CompilerParams(vmem_limit_bytes=12 << 20),
-        name="spread",
-    )(fields, up, down)
+        name="ghost",
+    )(up, down, spread)
 
     left = shift(high, "sub", 1)
     right = shift(low, "sub", -1)
@@ -477,7 +516,7 @@
     lines = array(24, total, LANES)
     state = pl.pallas_call(
         prep_kernel,
-        in_specs=[vmem] * 2,
+        in_specs=[vmem] * 3,
         out_specs=[vmem] * 12,
         out_shape=[field, lines, lines, field, field, field, field]
         + [array(16, total + 16, LANES), array(8 * groups, total + 16, LANES)]
@@ -485,11 +524,11 @@
         compiler_params=pltpu.CompilerParams(vmem_limit_bytes=24 << 20),
         cost_estimate=pl.CostEstimate(flops=20_000_000, bytes_accessed=0, transcendentals=0),
         name="prep",
-    )(spread, scale)
+    )(spread, rim, scale)
     devices = lax.axis_size(AXES[0]) * lax.axis_size(AXES[1])
     count = len(state)
     out = pl.pallas_call(
-        functools.partial(krylov_kernel, rows, ecols, count),
+        functools.partial(krylov_kernel, ecols, count),
         in_specs=[vmem] * (3 + count),
         out_specs=[vmem] * (count + 2),
         out_shape=[array(*x.shape) for x in state] + [field, array(devices, LANES)],

time: 53.5 us -> 53 us (level)
  waiting for transfers between devices: 6.69 us -> 5.41 us
    ppermute x4, waiting for transfers between devices: 6.69 us -> 5.41 us  [shift(): lax.ppermute(x, axis, [(i, (i + step) % count) for i in range(count)])]
    pallas_call x3 -> x4, Pallas kernels: 10.1 us -> 10.6 us  [the longest x1 5.4 us: shards(): pl.pallas_call(functools.partial(krylov_kernel, ecols, count), in_specs=[...]
  transfers between devices with their start and end apart: 4 -> 4, of which waited for: 3 -> 3; matrix products, arithmetic and copies ran while one was open for 0% -> 0% of each run, Pallas kernels for 7% -> 9%
where the time goes in v7:
time: 53 us; the launch traced here: 52.8 us
  blocking collectives  25.9 us (49%)
  Pallas kernels  14.9 us (28%)
  starting transfers between devices  5.93 us (11%)
  waiting for transfers between devices  5.41 us (10%)
  between operations  0.67 us (1%)
    all_to_all x1, blocking collectives, shards(): parts = lax.all_to_all(part, AXES, 0, 0, tiled=True)  25.9 us
    ppermute x4, starting transfers between devices, shift(): lax.ppermute(x, axis, [(i, (i + step) % count) for i in range(count)])  5.93 us
    ppermute x4, waiting for transfers between devices, shift(): lax.ppermute(x, axis, [(i, (i + step) % count) for i in range(count)])  5.41 us
    pallas_call x1, Pallas kernels, shards(): pl.pallas_call(functools.partial(krylov_kernel, ecols, count), in_specs=[...  5.4 us
    pallas_call x1, Pallas kernels, shards(): pl.pallas_call(prep_kernel, in_specs=[vmem] * 3, out_specs=[vmem] * 12, o...  4 us
    pallas_call x1, Pallas kernels, shards(): pl.pallas_call(combine_kernel, in_specs=[vmem] * 7, out_specs=[anywhere]...  2.64 us
    pallas_call x1, Pallas kernels, shards(): pl.pallas_call(load_kernel, in_specs=[anywhere] * 4, out_specs=[vmem] * 4...  1.75 us
  transfers between devices with their start and end apart: 4, of which 3 were waited for; matrix products, arithmetic and copies ran while one was open for 0% of the time, Pallas kernels for 9%

profile of v7, /device:TPU:1, one launch (start us, length us, event | category | flops | bytes accessed | tf_op | source)
XLA Modules:
  0.0 52.8 jit_solution(16844255303108033640)
XLA Ops:
  0.6 1.7 %load.1 = (f32[2,14,16,128]{3,2,1,0:T(8,128)S(1)}, f32[2,14,16,128]{3,2,1,0:T(8,128)S(1)}, f32[2,14,96,128]{3,2,1,0:T(8,128)S(1)}, f32[3,128]{1,0:T(4,128)S(1)}) custom-call(f32[12,96,256]{2,1,0:T(8,128)} %f_hbm.1, f32[96,256]{1,0:T(8,128)} %metric_hbm.1, f32[96,256]{1,0:T(8,128)} %jacobian_hbm.1, f32[12]{0:T(128)} %scale_hbm.1), custom_call_target="tpu_custom_call" | custom-call | tf_op jit(solution)/shard_map/load/pallas_call | solution.py:471
  2.4 3.1 %collective-permute-start = (f32[2,14,16,128]{3,2,1,0:T(8,128)S(1)}, f32[2,14,16,128]{3,2,1,0:T(8,128)S(1)}, u32[]{:S(2)}, u32[]{:S(2)}) collective-permute-start(f32[2,14,16,128]{3,2,1,0:T(8,128)S(1)} %get-tuple-element.27), channel_id=1, source_target_pairs={{0,4},{4,8},{8,12},{12,16},{16,20},{20,24},{24,28},{28,32},{32,36}... | collective-permute-start | bytes 688136 | tf_op jit(solution)/shard_map/ppermute | solution.py:463
  5.5 0.3 collective-permute-start.1
  5.8 0.8 %spread.1.own_ref.t_ref = f32[64,64,128]{2,1,0:T(8,128)S(1)} custom-call(f32[2,14,96,128]{3,2,1,0:T(8,128)S(1)} %get-tuple-element.29.fields_ref), custom_call_target="tpu_custom_call" | custom-call | flops 10000000 | tf_op jit(solution)/shard_map/spread/pallas_call | solution.py:488
  6.5 1.9 %collective-permute-done.up_ref = f32[2,14,16,128]{3,2,1,0:T(8,128)S(1)} collective-permute-done((f32[2,14,16,128]{3,2,1,0:T(8,128)S(1)}, f32[2,14,16,128]{3,2,1,0:T(8,128)S(1)}, u32[]{:S(2)}, u32[]{:S(2)}) %collective-permute-start) | collective-permute-done | bytes 229408 | tf_op jit(solution)/shard_map/ppermute | solution.py:463
  8.4 2.5 %collective-permute-done.1.down_ref = f32[2,14,16,128]{3,2,1,0:T(8,128)S(1)} collective-permute-done((f32[2,14,16,128]{3,2,1,0:T(8,128)S(1)}, f32[2,14,16,128]{3,2,1,0:T(8,128)S(1)}, u32[]{:S(2)}, u32[]{:S(2)}) %collective-permute-start.1) | collective-permute-done | bytes 229408 | tf_op jit(solution)/shard_map/ppermute | solution.py:463
  10.9 0.4 ghost.1
  11.3 2.6 %collective-permute-start.2 = (f32[64,4,128]{2,1,0:T(4,128)S(1)}, f32[64,4,128]{2,1,0:T(4,128)S(1)}, u32[]{:S(2)}, u32[]{:S(2)}) collective-permute-start(f32[64,4,128]{2,1,0:T(4,128)S(1)} %get-tuple-element.30), channel_id=1, source_target_pairs={{0,3},{1,0},{2,1},{3,2},{4,7},{5,4},{6,5},{7,6},{8,11},{9,8},{10,9... | collective-permute-start | bytes 393224 | tf_op jit(solution)/shard_map/ppermute | solution.py:463
  13.9 0.0 collective-permute-start.3
  13.9 4.0 %prep.1 = (f32[48,72,128]{2,1,0:T(8,128)S(1)}, f32[24,72,128]{2,1,0:T(8,128)S(1)}, f32[24,72,128]{2,1,0:T(8,128)S(1)}, f32[48,72,128]{2,1,0:T(8,128)S(1)}, f32[4...) custom-call(f32[64,64,128]{2,1,0:T(8,128)S(1)} %spread.1.own_ref.t_r, ...), custom_call_target="tpu_custom_call" | custom-call | flops 20000000 | tf_op jit(solution)/shard_map/prep/pallas_call | solution.py:517
  17.9 0.0 collective-permute-done.2.right_ref
  17.9 1.0 %collective-permute-done.3.left_ref = f32[64,4,128]{2,1,0:T(4,128)S(1)} collective-permute-done((f32[64,4,128]{2,1,0:T(4,128)S(1)}, f32[64,4,128]{2,1,0:T(4,128)S(1)}, u32[]{:S(2)}, u32[]{:S(2)}) %collective-permute-start.3) | collective-permute-done | bytes 131104 | tf_op jit(solution)/shard_map/ppermute | solution.py:463
  18.9 5.4 %krylov.1 = (f32[48,72,128]{2,1,0:T(8,128)S(1)}, f32[24,72,128]{2,1,0:T(8,128)S(1)}, f32[24,72,128]{2,1,0:T(8,128)S(1)}, f32[48,72,128]{2,1,0:T(8,128)S(1)}, f32...) custom-call(f32[64,4,128]{2,1,0:T(4,128)S(1)} %collective-permute-do, ...), custom_call_target="tpu_custom_call", output_to_operand_aliasing={{0}: (3, {}), {1}: (4, {}), {2}: (5, {}), {3}: (6, {}), {4}... | custom-call | tf_op jit(solution)/shard_map/krylov/pallas_call | solution.py:530
  24.3 25.9 %all_to_all.11 = f32[256,1,128]{2,1,0:T(1,128)S(1)} all-to-all(f32[256,1,128]{2,1,0:T(1,128)S(1)} %bitcast.5), channel_id=1, replica_groups=mesh['curve'=64,'sub'=4] {'curve','sub'}, dimensions={0} | all-to-all | bytes 262144 | tf_op jit(solution)/shard_map/all_to_all | solution.py:542
  50.2 2.6 %combine.1 = (f32[12,96,256]{2,1,0:T(8,128)}, f32[12,96,256]{2,1,0:T(8,128)}) custom-call(f32[256,128]{1,0:T(8,128)S(1)} %bitcast.4, f32[3,128]{1,0:T(4,128)S(1)} %get-tuple-element.32.scale_ref, f32[48,72,128]{2,1,0:T(8,128)S(1)} %get-tuple-element.47.u0_ref, f32[48,72,128]{2,1,0:T(8,128)S(1)} %get-tuple-element.48.u1_ref, ...), custom_call_target="tpu_custom_call" | custom-call | tf_op jit(solution)/shard_map/combine/pallas_call | solution.py:546
Async XLA Ops:
  2.4 6.1 %collective-permute-start = (f32[2,14,16,128]{3,2,1,0:T(8,128)S(1)}, f32[2,14,16,128]{3,2,1,0:T(8,128)S(1)}, u32[]{:S(2)}, u32[]{:S(2)}) collective-permute-start(f32[2,14,16,128]{3,2,1,0:T(8,128)S(1)} %get-tuple-element.27), channel_id=1, source_target_pairs={{0,4},{4,8},{8,12},{12,16},{16,20},{20,24},{24,28},{28,32},{32,36}... | collective-permute-start | bytes 688136 | tf_op jit(solution)/shard_map/ppermute | solution.py:463
  5.5 5.4 %collective-permute-start.1 = (f32[2,14,16,128]{3,2,1,0:T(8,128)S(1)}, f32[2,14,16,128]{3,2,1,0:T(8,128)S(1)}, u32[]{:S(2)}, u32[]{:S(2)}) collective-permute-start(f32[2,14,16,128]{3,2,1,0:T(8,128)S(1)} %get-tuple-element.28), channel_id=1, source_target_pairs={{0,252},{4,0},{8,4},{12,8},{16,12},{20,16},{24,20},{28,24},{32,28}... | collective-permute-start | bytes 688136 | tf_op jit(solution)/shard_map/ppermute | solution.py:463
  11.3 6.6 %collective-permute-start.2 = (f32[64,4,128]{2,1,0:T(4,128)S(1)}, f32[64,4,128]{2,1,0:T(4,128)S(1)}, u32[]{:S(2)}, u32[]{:S(2)}) collective-permute-start(f32[64,4,128]{2,1,0:T(4,128)S(1)} %get-tuple-element.30), channel_id=1, source_target_pairs={{0,3},{1,0},{2,1},{3,2},{4,7},{5,4},{6,5},{7,6},{8,11},{9,8},{10,9... | collective-permute-start | bytes 393224 | tf_op jit(solution)/shard_map/ppermute | solution.py:463
  13.9 5.0 %collective-permute-start.3 = (f32[64,4,128]{2,1,0:T(4,128)S(1)}, f32[64,4,128]{2,1,0:T(4,128)S(1)}, u32[]{:S(2)}, u32[]{:S(2)}) collective-permute-start(f32[64,4,128]{2,1,0:T(4,128)S(1)} %get-tuple-element.31), channel_id=1, source_target_pairs={{0,1},{1,2},{2,3},{3,0},{4,5},{5,6},{6,7},{7,4},{8,9},{9,10},{10,1... | collective-permute-start | bytes 393224 | tf_op jit(solution)/shard_map/ppermute | solution.py:463

commit v8 on v7

--- a/solution.py
+++ b/solution.py
@@ -39,28 +39,33 @@
     return (group * 4 + a) * 4 + b
 
 
-def load_kernel(f_hbm, metric_hbm, jacobian_hbm, scale_hbm, top, bottom, fields, scale_ref, scales, sems, scale_sem):
+def stack_copies(f_hbm, metric_hbm, jacobian_hbm, out, at, sems):
+    halves, stack, size, _ = out.shape
+    span = pl.ds(at, size)
+    copies = []
+    for half in range(halves):
+        columns = pl.ds(half * LANES, LANES)
+        pairs = (
+            (f_hbm.at[:, span, columns], out.at[half, pl.ds(0, stack - 2)]),
+            (metric_hbm.at[span, columns], out.at[half, stack - 2]),
+            (jacobian_hbm.at[span, columns], out.at[half, stack - 1]),
+        )
+        copies.append(
+            [pltpu.make_async_copy(x, y, sems.at[half, i]) for i, (x, y) in enumerate(pairs)]
+        )
+    for per_half in copies:
+        for copy in per_half:
+            copy.start()
+    return copies
+
+
+def load_kernel(f_hbm, metric_hbm, jacobian_hbm, scale_hbm, top, bottom, scale_ref, scales, sems, scale_sem):
     modes, rows, _ = f_hbm.shape
-    halves, _, halo, _ = top.shape
+    halo = top.shape[2]
     scale_copy = pltpu.make_async_copy(scale_hbm, scales, scale_sem)
     scale_copy.start()
-    copies = []
-    for part, (out, at, size) in enumerate(
-        ((top, 0, halo), (bottom, rows - halo, halo), (fields, 0, rows))
-    ):
-        span = pl.ds(at, size)
-        for half in range(halves):
-            columns = pl.ds(half * LANES, LANES)
-            for i, (source, target) in enumerate(
-                (
-                    (f_hbm.at[:, span, columns], out.at[half, pl.ds(0, modes)]),
-                    (metric_hbm.at[span, columns], out.at[half, modes]),
-                    (jacobian_hbm.at[span, columns], out.at[half, modes + 1]),
-                )
-            ):
-                copies.append(pltpu.make_async_copy(source, target, sems.at[part, half, i]))
-    for copy in copies:
-        copy.start()
+    copies = stack_copies(f_hbm, metric_hbm, jacobian_hbm, top, 0, sems.at[0])
+    copies += stack_copies(f_hbm, metric_hbm, jacobian_hbm, bottom, rows - halo, sems.at[1])
     scale_copy.wait()
     member = lax.broadcasted_iota(jnp.int32, (1, LANES), 1) % PACK
     for group in range(modes // PACK):
@@ -68,16 +73,20 @@
         for m in range(PACK):
             row = jnp.where(member == m, scales[group * PACK + m], row)
         scale_ref[group : group + 1, :] = row
-    for copy in copies:
-        copy.wait()
-
-
-def spread_kernel(fields_ref, t_ref, xs, xt):
+    for per_half in copies:
+        for copy in per_half:
+            copy.wait()
+
+
+def spread_kernel(f_hbm, metric_hbm, jacobian_hbm, t_ref, fields_ref, xs, xt, sems):
     halves, stack, rows, _ = fields_ref.shape
     own = rows // 4
     groups = (stack - 2) // PACK
     per_half = LANES // 4
+    copies = stack_copies(f_hbm, metric_hbm, jacobian_hbm, fields_ref, 0, sems)
     for half in range(halves):
+        for copy in copies[half]:
+            copy.wait()
         for group in range(groups + 1):
             for a in range(4):
                 at = (half * (groups + 1) + group) * 4 + a
@@ -154,6 +163,10 @@
 
 
 def join_rows(first, last):
+    return first + pltpu.roll(last, PACK, 1), last + pltpu.roll(first, LANES - PACK, 1)
+
+
+def join_rows_in_turn(first, last):
     shared = last + pltpu.roll(first, LANES - PACK, 1)
     return pltpu.roll(shared, PACK, 1), shared
 
@@ -276,7 +289,7 @@
         sums[groups + group] += with_old if own is None else own * with_old
         for b in range(4):
             column = [y[a][b] for a in range(4)]
-            column[0], column[3] = join_rows(column[0], column[3])
+            column[0], column[3] = join_rows_in_turn(column[0], column[3])
             for a in range(4):
                 p = plane(group, a, b)
                 if b in (1, 2):
@@ -468,33 +481,41 @@
     planes = 16 * (groups + 1)
     ecols = cols // 4
     halves = cols // LANES
-    top, bottom, fields, scale = pl.pallas_call(
+    inputs = [
+        pltpu.with_memory_space_constraint(x, pltpu.HBM)
+        for x in (forcing, metric, jacobian, mode_scale)
+    ]
+    top, bottom, scale = pl.pallas_call(
         load_kernel,
         in_specs=[anywhere] * 4,
-        out_specs=[vmem] * 4,
-        out_shape=[array(halves, modes + 2, halo, LANES)] * 2
-        + [array(halves, modes + 2, rows, LANES), array(groups, LANES)],
+        out_specs=[vmem] * 3,
+        out_shape=[array(halves, modes + 2, halo, LANES)] * 2 + [array(groups, LANES)],
         scratch_shapes=[
             pltpu.SMEM((modes,), f32),
-            pltpu.SemaphoreType.DMA((3, halves, 3)),
+            pltpu.SemaphoreType.DMA((2, halves, 3)),
             pltpu.SemaphoreType.DMA,
         ],
         compiler_params=pltpu.CompilerParams(vmem_limit_bytes=4 << 20),
         name="load",
-    )(*[pltpu.with_memory_space_constraint(x, pltpu.HBM) for x in (forcing, metric, jacobian, mode_scale)])
+    )(*inputs)
     up = shift(bottom, "curve", 1)
     down = shift(top, "curve", -1)
 
     spread = pl.pallas_call(
         spread_kernel,
-        in_specs=[vmem],
+        in_specs=[anywhere] * 3,
         out_specs=vmem,
         out_shape=array(planes, ecols, LANES),
-        scratch_shapes=[pltpu.VMEM((halves * planes // 4, LANES, LANES), f32)] * 2,
+        scratch_shapes=[
+            pltpu.VMEM((halves, modes + 2, rows, LANES), f32),
+            pltpu.VMEM((halves * planes // 4, LANES, LANES), f32),
+            pltpu.VMEM((halves * planes // 4, LANES, LANES), f32),
+            pltpu.SemaphoreType.DMA((halves, 3)),
+        ],
         compiler_params=pltpu.CompilerParams(vmem_limit_bytes=12 << 20),
         cost_estimate=pl.CostEstimate(flops=10_000_000, bytes_accessed=0, transcendentals=0),
         name="spread",
-    )(fields)
+    )(*inputs[:3])
     rim, low, high = pl.pallas_call(
         ghost_kernel,
         in_specs=[vmem] * 3,

time: 53 us -> 52.3 us (0.987)
  waiting for transfers between devices: 5.41 us -> 4.43 us
    ppermute x4, waiting for transfers between devices: 5.41 us -> 4.43 us  [shift(): lax.ppermute(x, axis, [(i, (i + step) % count) for i in range(count)])]
    pallas_call x2, Pallas kernels: 2.53 us -> 3.19 us  [the longest x1 1.93 us: shards(): pl.pallas_call(spread_kernel, in_specs=[anywhere] * 3, out_specs=vmem, ou...]
  transfers between devices with their start and end apart: 4 -> 4, of which waited for: 3 -> 3; matrix products, arithmetic and copies ran while one was open for 0% -> 0% of each run, Pallas kernels for 9% -> 11%
where the time goes in v8:
time: 52.3 us; the launch traced here: 52.1 us
  blocking collectives  25.7 us (49%)
  Pallas kernels  15.4 us (29%)
  starting transfers between devices  5.93 us (11%)
  waiting for transfers between devices  4.43 us (8%)
  between operations  0.67 us (1%)
    all_to_all x1, blocking collectives, shards(): parts = lax.all_to_all(part, AXES, 0, 0, tiled=True)  25.7 us
    ppermute x4, starting transfers between devices, shift(): lax.ppermute(x, axis, [(i, (i + step) % count) for i in range(count)])  5.93 us
    pallas_call x1, Pallas kernels, shards(): pl.pallas_call(functools.partial(krylov_kernel, ecols, count), in_specs=[...  5.37 us
    ppermute x4, waiting for transfers between devices, shift(): lax.ppermute(x, axis, [(i, (i + step) % count) for i in range(count)])  4.43 us
    pallas_call x1, Pallas kernels, shards(): pl.pallas_call(prep_kernel, in_specs=[vmem] * 3, out_specs=[vmem] * 12, o...  3.82 us
    pallas_call x1, Pallas kernels, shards(): pl.pallas_call(combine_kernel, in_specs=[vmem] * 7, out_specs=[anywhere]...  2.64 us
    pallas_call x1, Pallas kernels, shards(): pl.pallas_call(spread_kernel, in_specs=[anywhere] * 3, out_specs=vmem, ou...  1.93 us
    pallas_call x1, Pallas kernels, shards(): pl.pallas_call(load_kernel, in_specs=[anywhere] * 4, out_specs=[vmem] * 3...  1.26 us
  transfers between devices with their start and end apart: 4, of which 3 were waited for; matrix products, arithmetic and copies ran while one was open for 0% of the time, Pallas kernels for 11%

profile of v8, /device:TPU:1, one launch (start us, length us, event | category | flops | bytes accessed | tf_op | source)
XLA Modules:
  0.0 52.1 jit_solution(12160190371517423910)
XLA Ops:
  0.6 1.3 %load.1 = (f32[2,14,16,128]{3,2,1,0:T(8,128)S(1)}, f32[2,14,16,128]{3,2,1,0:T(8,128)S(1)}, f32[3,128]{1,0:T(4,128)S(1)}) custom-call(f32[12,96,256]{2,1,0:T(8,128)} %f_hbm.3, f32[96,256]{1,0:T(8,128)} %metric_hbm.3, f32[96,256]{1,0:T(8,128)} %jacobian_hbm.3, f32[12]{0:T(128)} %scale_hbm.1), custom_call_target="tpu_custom_call" | custom-call | tf_op jit(solution)/shard_map/load/pallas_call | solution.py:488
  1.9 3.1 %collective-permute-start = (f32[2,14,16,128]{3,2,1,0:T(8,128)S(1)}, f32[2,14,16,128]{3,2,1,0:T(8,128)S(1)}, u32[]{:S(2)}, u32[]{:S(2)}) collective-permute-start(f32[2,14,16,128]{3,2,1,0:T(8,128)S(1)} %get-tuple-element.26), channel_id=1, source_target_pairs={{0,4},{4,8},{8,12},{12,16},{16,20},{20,24},{24,28},{28,32},{32,36}... | collective-permute-start | bytes 688136 | tf_op jit(solution)/shard_map/ppermute | solution.py:476
  5.0 0.3 collective-permute-start.1
  5.3 1.9 %spread.1.own_ref.t_ref = f32[64,64,128]{2,1,0:T(8,128)S(1)} custom-call(f32[12,96,256]{2,1,0:T(8,128)} %f_hbm.3, f32[96,256]{1,0:T(8,128)} %metric_hbm.3, f32[96,256]{1,0:T(8,128)} %jacobian_hbm.3), custom_call_target="tpu_custom_call" | custom-call | flops 10000000 | tf_op jit(solution)/shard_map/spread/pallas_call | solution.py:504
  7.2 0.7 %collective-permute-done.up_ref = f32[2,14,16,128]{3,2,1,0:T(8,128)S(1)} collective-permute-done((f32[2,14,16,128]{3,2,1,0:T(8,128)S(1)}, f32[2,14,16,128]{3,2,1,0:T(8,128)S(1)}, u32[]{:S(2)}, u32[]{:S(2)}) %collective-permute-start) | collective-permute-done | bytes 229408 | tf_op jit(solution)/shard_map/ppermute | solution.py:476
  8.0 2.5 %collective-permute-done.1.down_ref = f32[2,14,16,128]{3,2,1,0:T(8,128)S(1)} collective-permute-done((f32[2,14,16,128]{3,2,1,0:T(8,128)S(1)}, f32[2,14,16,128]{3,2,1,0:T(8,128)S(1)}, u32[]{:S(2)}, u32[]{:S(2)}) %collective-permute-start.1) | collective-permute-done | bytes 229408 | tf_op jit(solution)/shard_map/ppermute | solution.py:476
  10.4 0.4 ghost.1
  10.8 2.6 %collective-permute-start.2 = (f32[64,4,128]{2,1,0:T(4,128)S(1)}, f32[64,4,128]{2,1,0:T(4,128)S(1)}, u32[]{:S(2)}, u32[]{:S(2)}) collective-permute-start(f32[64,4,128]{2,1,0:T(4,128)S(1)} %get-tuple-element.28), channel_id=1, source_target_pairs={{0,3},{1,0},{2,1},{3,2},{4,7},{5,4},{6,5},{7,6},{8,11},{9,8},{10,9... | collective-permute-start | bytes 393224 | tf_op jit(solution)/shard_map/ppermute | solution.py:476
  13.4 0.0 collective-permute-start.3
  13.4 3.8 %prep.1 = (f32[48,72,128]{2,1,0:T(8,128)S(1)}, f32[24,72,128]{2,1,0:T(8,128)S(1)}, f32[24,72,128]{2,1,0:T(8,128)S(1)}, f32[48,72,128]{2,1,0:T(8,128)S(1)}, f32[4...) custom-call(f32[64,64,128]{2,1,0:T(8,128)S(1)} %spread.1.own_ref.t_r, ...), custom_call_target="tpu_custom_call" | custom-call | flops 20000000 | tf_op jit(solution)/shard_map/prep/pallas_call | solution.py:538
  17.2 0.0 collective-permute-done.2.right_ref
  17.2 1.2 %collective-permute-done.3.left_ref = f32[64,4,128]{2,1,0:T(4,128)S(1)} collective-permute-done((f32[64,4,128]{2,1,0:T(4,128)S(1)}, f32[64,4,128]{2,1,0:T(4,128)S(1)}, u32[]{:S(2)}, u32[]{:S(2)}) %collective-permute-start.3) | collective-permute-done | bytes 131104 | tf_op jit(solution)/shard_map/ppermute | solution.py:476
  18.4 5.4 %krylov.1 = (f32[48,72,128]{2,1,0:T(8,128)S(1)}, f32[24,72,128]{2,1,0:T(8,128)S(1)}, f32[24,72,128]{2,1,0:T(8,128)S(1)}, f32[48,72,128]{2,1,0:T(8,128)S(1)}, f32...) custom-call(f32[64,4,128]{2,1,0:T(4,128)S(1)} %collective-permute-do, ...), custom_call_target="tpu_custom_call", output_to_operand_aliasing={{0}: (3, {}), {1}: (4, {}), {2}: (5, {}), {3}: (6, {}), {4}... | custom-call | tf_op jit(solution)/shard_map/krylov/pallas_call | solution.py:551
  23.8 25.7 %all_to_all.11 = f32[256,1,128]{2,1,0:T(1,128)S(1)} all-to-all(f32[256,1,128]{2,1,0:T(1,128)S(1)} %bitcast.5), channel_id=1, replica_groups=mesh['curve'=64,'sub'=4] {'curve','sub'}, dimensions={0} | all-to-all | bytes 262144 | tf_op jit(solution)/shard_map/all_to_all | solution.py:563
  49.5 2.6 %combine.1 = (f32[12,96,256]{2,1,0:T(8,128)}, f32[12,96,256]{2,1,0:T(8,128)}) custom-call(f32[256,128]{1,0:T(8,128)S(1)} %bitcast.4, f32[3,128]{1,0:T(4,128)S(1)} %get-tuple-element.30.scale_ref, f32[48,72,128]{2,1,0:T(8,128)S(1)} %get-tuple-element.45.u0_ref, f32[48,72,128]{2,1,0:T(8,128)S(1)} %get-tuple-element.46.u1_ref, ...), custom_call_target="tpu_custom_call" | custom-call | tf_op jit(solution)/shard_map/combine/pallas_call | solution.py:567
Async XLA Ops:
  1.9 6.1 %collective-permute-start = (f32[2,14,16,128]{3,2,1,0:T(8,128)S(1)}, f32[2,14,16,128]{3,2,1,0:T(8,128)S(1)}, u32[]{:S(2)}, u32[]{:S(2)}) collective-permute-start(f32[2,14,16,128]{3,2,1,0:T(8,128)S(1)} %get-tuple-element.26), channel_id=1, source_target_pairs={{0,4},{4,8},{8,12},{12,16},{16,20},{20,24},{24,28},{28,32},{32,36}... | collective-permute-start | bytes 688136 | tf_op jit(solution)/shard_map/ppermute | solution.py:476
  5.0 5.4 %collective-permute-start.1 = (f32[2,14,16,128]{3,2,1,0:T(8,128)S(1)}, f32[2,14,16,128]{3,2,1,0:T(8,128)S(1)}, u32[]{:S(2)}, u32[]{:S(2)}) collective-permute-start(f32[2,14,16,128]{3,2,1,0:T(8,128)S(1)} %get-tuple-element.27), channel_id=1, source_target_pairs={{0,252},{4,0},{8,4},{12,8},{16,12},{20,16},{24,20},{28,24},{32,28}... | collective-permute-start | bytes 688136 | tf_op jit(solution)/shard_map/ppermute | solution.py:476
  10.8 6.4 %collective-permute-start.2 = (f32[64,4,128]{2,1,0:T(4,128)S(1)}, f32[64,4,128]{2,1,0:T(4,128)S(1)}, u32[]{:S(2)}, u32[]{:S(2)}) collective-permute-start(f32[64,4,128]{2,1,0:T(4,128)S(1)} %get-tuple-element.28), channel_id=1, source_target_pairs={{0,3},{1,0},{2,1},{3,2},{4,7},{5,4},{6,5},{7,6},{8,11},{9,8},{10,9... | collective-permute-start | bytes 393224 | tf_op jit(solution)/shard_map/ppermute | solution.py:476
  13.4 5.0 %collective-permute-start.3 = (f32[64,4,128]{2,1,0:T(4,128)S(1)}, f32[64,4,128]{2,1,0:T(4,128)S(1)}, u32[]{:S(2)}, u32[]{:S(2)}) collective-permute-start(f32[64,4,128]{2,1,0:T(4,128)S(1)} %get-tuple-element.29), channel_id=1, source_target_pairs={{0,1},{1,2},{2,3},{3,0},{4,5},{5,6},{6,7},{7,4},{8,9},{9,10},{10,1... | collective-permute-start | bytes 393224 | tf_op jit(solution)/shard_map/ppermute | solution.py:476

commit v9 on v8

--- a/solution.py
+++ b/solution.py
@@ -302,6 +302,19 @@
     return tuple(sums)
 
 
+def several(low, high, count, body, sums):
+    def step(i, sums):
+        for j in range(count):
+            sums = body(low + i * count + j, sums)
+        return sums
+
+    steps = (high - low) // count
+    sums = lax.fori_loop(0, steps, step, sums)
+    for t in range(low + steps * count, high):
+        sums = body(jnp.int32(t), sums)
+    return sums
+
+
 def prep_kernel(t_ref, rim_ref, scale_ref, *refs):
     state, (u1_ref, edge, sums_ref) = refs[:9], refs[9:]
     mass_ref, krow, kcol, diag_ref, minv, u0_ref, w_ref, cedge, redge = state
@@ -324,9 +337,10 @@
         finish(a, 8, cols - 8, scale_ref, diag_ref, minv, u0_ref, cedge, redge)
 
     zero = jnp.zeros((8, LANES), jnp.float32)
-    sums = lax.fori_loop(
+    sums = several(
         1,
         cols // 8 - 1,
+        3,
         lambda t, sums: operator_tile(
             t, None, sums, u0_ref, None, u1_ref, mass_ref, krow, kcol, minv, w_ref, edge
         ),
@@ -371,9 +385,9 @@
             return operator_tile(t, own, sums, now_ref, old_ref, new_ref, *shared)
 
         if old_ref is None:
-            sums = lax.fori_loop(0, 3, body, tuple(sums_ref[i] for i in range(2 * groups)))
+            sums = several(0, 3, 3, body, tuple(sums_ref[i] for i in range(2 * groups)))
         else:
-            sums = lax.fori_loop(0, tiles, body, (zero,) * (2 * groups))
+            sums = several(0, tiles, 3, body, (zero,) * (2 * groups))
 
         @pl.loop(0, groups * 4)
         def _(i):

time: 52.3 us -> 51.3 us (0.981)
  Pallas kernels: 15.4 us -> 14.3 us
    pallas_call x1, Pallas kernels: 5.37 us -> 4.48 us  [shards(): pl.pallas_call(functools.partial(krylov_kernel, ecols, count), in_specs=[...]
where the time goes in v9:
time: 51.3 us; the launch traced here: 51.2 us
  blocking collectives  25.6 us (50%)
  Pallas kernels  14.3 us (28%)
  starting transfers between devices  5.93 us (12%)
  waiting for transfers between devices  4.67 us (9%)
  between operations  0.67 us (1%)
    all_to_all x1, blocking collectives, shards(): parts = lax.all_to_all(part, AXES, 0, 0, tiled=True)  25.6 us
    ppermute x4, starting transfers between devices, shift(): lax.ppermute(x, axis, [(i, (i + step) % count) for i in range(count)])  5.93 us
    ppermute x4, waiting for transfers between devices, shift(): lax.ppermute(x, axis, [(i, (i + step) % count) for i in range(count)])  4.67 us
    pallas_call x1, Pallas kernels, shards(): pl.pallas_call(functools.partial(krylov_kernel, ecols, count), in_specs=[...  4.48 us
    pallas_call x1, Pallas kernels, shards(): pl.pallas_call(prep_kernel, in_specs=[vmem] * 3, out_specs=[vmem] * 12, o...  3.58 us
    pallas_call x1, Pallas kernels, shards(): pl.pallas_call(combine_kernel, in_specs=[vmem] * 7, out_specs=[anywhere]...  2.64 us
    pallas_call x1, Pallas kernels, shards(): pl.pallas_call(spread_kernel, in_specs=[anywhere] * 3, out_specs=vmem, ou...  1.93 us
    pallas_call x1, Pallas kernels, shards(): pl.pallas_call(load_kernel, in_specs=[anywhere] * 4, out_specs=[vmem] * 3...  1.26 us
  transfers between devices with their start and end apart: 4, of which 3 were waited for; matrix products, arithmetic and copies ran while one was open for 0% of the time, Pallas kernels for 11%

profile of v9, /device:TPU:1, one launch (start us, length us, event | category | flops | bytes accessed | tf_op | source)
XLA Modules:
  0.0 51.2 jit_solution(11880712430099408860)
XLA Ops:
  0.6 1.3 %load.1 = (f32[2,14,16,128]{3,2,1,0:T(8,128)S(1)}, f32[2,14,16,128]{3,2,1,0:T(8,128)S(1)}, f32[3,128]{1,0:T(4,128)S(1)}) custom-call(f32[12,96,256]{2,1,0:T(8,128)} %f_hbm.3, f32[96,256]{1,0:T(8,128)} %metric_hbm.3, f32[96,256]{1,0:T(8,128)} %jacobian_hbm.3, f32[12]{0:T(128)} %scale_hbm.1), custom_call_target="tpu_custom_call" | custom-call | tf_op jit(solution)/shard_map/load/pallas_call | solution.py:502
  1.9 3.1 %collective-permute-start = (f32[2,14,16,128]{3,2,1,0:T(8,128)S(1)}, f32[2,14,16,128]{3,2,1,0:T(8,128)S(1)}, u32[]{:S(2)}, u32[]{:S(2)}) collective-permute-start(f32[2,14,16,128]{3,2,1,0:T(8,128)S(1)} %get-tuple-element.26), channel_id=1, source_target_pairs={{0,4},{4,8},{8,12},{12,16},{16,20},{20,24},{24,28},{28,32},{32,36}... | collective-permute-start | bytes 688136 | tf_op jit(solution)/shard_map/ppermute | solution.py:490
  5.0 0.3 collective-permute-start.1
  5.3 1.9 %spread.1.own_ref.t_ref = f32[64,64,128]{2,1,0:T(8,128)S(1)} custom-call(f32[12,96,256]{2,1,0:T(8,128)} %f_hbm.3, f32[96,256]{1,0:T(8,128)} %metric_hbm.3, f32[96,256]{1,0:T(8,128)} %jacobian_hbm.3), custom_call_target="tpu_custom_call" | custom-call | flops 10000000 | tf_op jit(solution)/shard_map/spread/pallas_call | solution.py:518
  7.2 0.7 %collective-permute-done.up_ref = f32[2,14,16,128]{3,2,1,0:T(8,128)S(1)} collective-permute-done((f32[2,14,16,128]{3,2,1,0:T(8,128)S(1)}, f32[2,14,16,128]{3,2,1,0:T(8,128)S(1)}, u32[]{:S(2)}, u32[]{:S(2)}) %collective-permute-start) | collective-permute-done | bytes 229408 | tf_op jit(solution)/shard_map/ppermute | solution.py:490
  8.0 2.5 %collective-permute-done.1.down_ref = f32[2,14,16,128]{3,2,1,0:T(8,128)S(1)} collective-permute-done((f32[2,14,16,128]{3,2,1,0:T(8,128)S(1)}, f32[2,14,16,128]{3,2,1,0:T(8,128)S(1)}, u32[]{:S(2)}, u32[]{:S(2)}) %collective-permute-start.1) | collective-permute-done | bytes 229408 | tf_op jit(solution)/shard_map/ppermute | solution.py:490
  10.4 0.4 ghost.1
  10.8 2.6 %collective-permute-start.2 = (f32[64,4,128]{2,1,0:T(4,128)S(1)}, f32[64,4,128]{2,1,0:T(4,128)S(1)}, u32[]{:S(2)}, u32[]{:S(2)}) collective-permute-start(f32[64,4,128]{2,1,0:T(4,128)S(1)} %get-tuple-element.28), channel_id=1, source_target_pairs={{0,3},{1,0},{2,1},{3,2},{4,7},{5,4},{6,5},{7,6},{8,11},{9,8},{10,9... | collective-permute-start | bytes 393224 | tf_op jit(solution)/shard_map/ppermute | solution.py:490
  13.4 0.0 collective-permute-start.3
  13.4 3.6 %prep.1 = (f32[48,72,128]{2,1,0:T(8,128)S(1)}, f32[24,72,128]{2,1,0:T(8,128)S(1)}, f32[24,72,128]{2,1,0:T(8,128)S(1)}, f32[48,72,128]{2,1,0:T(8,128)S(1)}, f32[4...) custom-call(f32[64,64,128]{2,1,0:T(8,128)S(1)} %spread.1.own_ref.t_r, ...), custom_call_target="tpu_custom_call" | custom-call | flops 20000000 | tf_op jit(solution)/shard_map/prep/pallas_call | solution.py:552
  17.0 0.0 collective-permute-done.2.right_ref
  17.0 1.4 %collective-permute-done.3.left_ref = f32[64,4,128]{2,1,0:T(4,128)S(1)} collective-permute-done((f32[64,4,128]{2,1,0:T(4,128)S(1)}, f32[64,4,128]{2,1,0:T(4,128)S(1)}, u32[]{:S(2)}, u32[]{:S(2)}) %collective-permute-start.3) | collective-permute-done | bytes 131104 | tf_op jit(solution)/shard_map/ppermute | solution.py:490
  18.4 4.5 %krylov.1 = (f32[48,72,128]{2,1,0:T(8,128)S(1)}, f32[24,72,128]{2,1,0:T(8,128)S(1)}, f32[24,72,128]{2,1,0:T(8,128)S(1)}, f32[48,72,128]{2,1,0:T(8,128)S(1)}, f32...) custom-call(f32[64,4,128]{2,1,0:T(4,128)S(1)} %collective-permute-do, ...), custom_call_target="tpu_custom_call", output_to_operand_aliasing={{0}: (3, {}), {1}: (4, {}), {2}: (5, {}), {3}: (6, {}), {4}... | custom-call | tf_op jit(solution)/shard_map/krylov/pallas_call | solution.py:565
  22.9 25.6 %all_to_all.11 = f32[256,1,128]{2,1,0:T(1,128)S(1)} all-to-all(f32[256,1,128]{2,1,0:T(1,128)S(1)} %bitcast.5), channel_id=1, replica_groups=mesh['curve'=64,'sub'=4] {'curve','sub'}, dimensions={0} | all-to-all | bytes 262144 | tf_op jit(solution)/shard_map/all_to_all | solution.py:577
  48.5 2.6 %combine.1 = (f32[12,96,256]{2,1,0:T(8,128)}, f32[12,96,256]{2,1,0:T(8,128)}) custom-call(f32[256,128]{1,0:T(8,128)S(1)} %bitcast.4, f32[3,128]{1,0:T(4,128)S(1)} %get-tuple-element.30.scale_ref, f32[48,72,128]{2,1,0:T(8,128)S(1)} %get-tuple-element.45.u0_ref, f32[48,72,128]{2,1,0:T(8,128)S(1)} %get-tuple-element.46.u1_ref, ...), custom_call_target="tpu_custom_call" | custom-call | tf_op jit(solution)/shard_map/combine/pallas_call | solution.py:581
Async XLA Ops:
  1.9 6.1 %collective-permute-start = (f32[2,14,16,128]{3,2,1,0:T(8,128)S(1)}, f32[2,14,16,128]{3,2,1,0:T(8,128)S(1)}, u32[]{:S(2)}, u32[]{:S(2)}) collective-permute-start(f32[2,14,16,128]{3,2,1,0:T(8,128)S(1)} %get-tuple-element.26), channel_id=1, source_target_pairs={{0,4},{4,8},{8,12},{12,16},{16,20},{20,24},{24,28},{28,32},{32,36}... | collective-permute-start | bytes 688136 | tf_op jit(solution)/shard_map/ppermute | solution.py:490
  5.0 5.4 %collective-permute-start.1 = (f32[2,14,16,128]{3,2,1,0:T(8,128)S(1)}, f32[2,14,16,128]{3,2,1,0:T(8,128)S(1)}, u32[]{:S(2)}, u32[]{:S(2)}) collective-permute-start(f32[2,14,16,128]{3,2,1,0:T(8,128)S(1)} %get-tuple-element.27), channel_id=1, source_target_pairs={{0,252},{4,0},{8,4},{12,8},{16,12},{20,16},{24,20},{28,24},{32,28}... | collective-permute-start | bytes 688136 | tf_op jit(solution)/shard_map/ppermute | solution.py:490
  10.8 6.1 %collective-permute-start.2 = (f32[64,4,128]{2,1,0:T(4,128)S(1)}, f32[64,4,128]{2,1,0:T(4,128)S(1)}, u32[]{:S(2)}, u32[]{:S(2)}) collective-permute-start(f32[64,4,128]{2,1,0:T(4,128)S(1)} %get-tuple-element.28), channel_id=1, source_target_pairs={{0,3},{1,0},{2,1},{3,2},{4,7},{5,4},{6,5},{7,6},{8,11},{9,8},{10,9... | collective-permute-start | bytes 393224 | tf_op jit(solution)/shard_map/ppermute | solution.py:490
  13.4 5.0 %collective-permute-start.3 = (f32[64,4,128]{2,1,0:T(4,128)S(1)}, f32[64,4,128]{2,1,0:T(4,128)S(1)}, u32[]{:S(2)}, u32[]{:S(2)}) collective-permute-start(f32[64,4,128]{2,1,0:T(4,128)S(1)} %get-tuple-element.29), channel_id=1, source_target_pairs={{0,1},{1,2},{2,3},{3,0},{4,5},{5,6},{6,7},{7,4},{8,9},{9,10},{10,1... | collective-permute-start | bytes 393224 | tf_op jit(solution)/shard_map/ppermute | solution.py:490

commit v10 on v9

--- a/solution.py
+++ b/solution.py
@@ -332,8 +332,7 @@
 
         prepare(t, fetch, scale_ref, *state)
 
-    @pl.loop(0, 4)
-    def _(a):
+    for a in range(4):
         finish(a, 8, cols - 8, scale_ref, diag_ref, minv, u0_ref, cedge, redge)
 
     zero = jnp.zeros((8, LANES), jnp.float32)
@@ -363,8 +362,7 @@
         own_tiles, lambda p: jnp.concatenate([right_ref[p], left_ref[p]], axis=0), scale_ref, *state
     )
 
-    @pl.loop(0, 4)
-    def _(a):
+    for a in range(4):
         wrap_cols(cedge, a, total)
         wrap_cols(cedge, 4 + a, total)
         for group in range(groups):
@@ -389,8 +387,7 @@
         else:
             sums = several(0, tiles, 3, body, (zero,) * (2 * groups))
 
-        @pl.loop(0, groups * 4)
-        def _(i):
+        for i in range(groups * 4):
             wrap_cols(edge, i, total)
             for b, value in zip((0, 3), join_cols(edge, i, 0, total)):
                 p = i * 4 + b

time: 51.3 us -> 51.2 us (level)
  no operation moved by 1% of the time
where the time goes in v10:
time: 51.2 us; the launch traced here: 51 us
  blocking collectives  25.6 us (50%)
  Pallas kernels  14.1 us (28%)
  starting transfers between devices  5.93 us (12%)
  waiting for transfers between devices  4.7 us (9%)
  between operations  0.67 us (1%)
    all_to_all x1, blocking collectives, shards(): parts = lax.all_to_all(part, AXES, 0, 0, tiled=True)  25.6 us
    ppermute x4, starting transfers between devices, shift(): lax.ppermute(x, axis, [(i, (i + step) % count) for i in range(count)])  5.93 us
    ppermute x4, waiting for transfers between devices, shift(): lax.ppermute(x, axis, [(i, (i + step) % count) for i in range(count)])  4.7 us
    pallas_call x1, Pallas kernels, shards(): pl.pallas_call(functools.partial(krylov_kernel, ecols, count), in_specs=[...  4.3 us
    pallas_call x1, Pallas kernels, shards(): pl.pallas_call(prep_kernel, in_specs=[vmem] * 3, out_specs=[vmem] * 12, o...  3.56 us
    pallas_call x1, Pallas kernels, shards(): pl.pallas_call(combine_kernel, in_specs=[vmem] * 7, out_specs=[anywhere]...  2.64 us
    pallas_call x1, Pallas kernels, shards(): pl.pallas_call(spread_kernel, in_specs=[anywhere] * 3, out_specs=vmem, ou...  1.93 us
    pallas_call x1, Pallas kernels, shards(): pl.pallas_call(load_kernel, in_specs=[anywhere] * 4, out_specs=[vmem] * 3...  1.26 us
  transfers between devices with their start and end apart: 4, of which 3 were waited for; matrix products, arithmetic and copies ran while one was open for 0% of the time, Pallas kernels for 11%

profile of v10, /device:TPU:1, one launch (start us, length us, event | category | flops | bytes accessed | tf_op | source)
XLA Modules:
  0.0 51.0 jit_solution(8659324388322158395)
XLA Ops:
  0.6 1.3 %load.1 = (f32[2,14,16,128]{3,2,1,0:T(8,128)S(1)}, f32[2,14,16,128]{3,2,1,0:T(8,128)S(1)}, f32[3,128]{1,0:T(4,128)S(1)}) custom-call(f32[12,96,256]{2,1,0:T(8,128)} %f_hbm.3, f32[96,256]{1,0:T(8,128)} %metric_hbm.3, f32[96,256]{1,0:T(8,128)} %jacobian_hbm.3, f32[12]{0:T(128)} %scale_hbm.1), custom_call_target="tpu_custom_call" | custom-call | tf_op jit(solution)/shard_map/load/pallas_call | solution.py:499
  1.9 3.1 %collective-permute-start = (f32[2,14,16,128]{3,2,1,0:T(8,128)S(1)}, f32[2,14,16,128]{3,2,1,0:T(8,128)S(1)}, u32[]{:S(2)}, u32[]{:S(2)}) collective-permute-start(f32[2,14,16,128]{3,2,1,0:T(8,128)S(1)} %get-tuple-element.26), channel_id=1, source_target_pairs={{0,4},{4,8},{8,12},{12,16},{16,20},{20,24},{24,28},{28,32},{32,36}... | collective-permute-start | bytes 688136 | tf_op jit(solution)/shard_map/ppermute | solution.py:487
  5.0 0.3 collective-permute-start.1
  5.3 1.9 %spread.1.own_ref.t_ref = f32[64,64,128]{2,1,0:T(8,128)S(1)} custom-call(f32[12,96,256]{2,1,0:T(8,128)} %f_hbm.3, f32[96,256]{1,0:T(8,128)} %metric_hbm.3, f32[96,256]{1,0:T(8,128)} %jacobian_hbm.3), custom_call_target="tpu_custom_call" | custom-call | flops 10000000 | tf_op jit(solution)/shard_map/spread/pallas_call | solution.py:515
  7.2 0.7 %collective-permute-done.up_ref = f32[2,14,16,128]{3,2,1,0:T(8,128)S(1)} collective-permute-done((f32[2,14,16,128]{3,2,1,0:T(8,128)S(1)}, f32[2,14,16,128]{3,2,1,0:T(8,128)S(1)}, u32[]{:S(2)}, u32[]{:S(2)}) %collective-permute-start) | collective-permute-done | bytes 229408 | tf_op jit(solution)/shard_map/ppermute | solution.py:487
  8.0 2.5 %collective-permute-done.1.down_ref = f32[2,14,16,128]{3,2,1,0:T(8,128)S(1)} collective-permute-done((f32[2,14,16,128]{3,2,1,0:T(8,128)S(1)}, f32[2,14,16,128]{3,2,1,0:T(8,128)S(1)}, u32[]{:S(2)}, u32[]{:S(2)}) %collective-permute-start.1) | collective-permute-done | bytes 229408 | tf_op jit(solution)/shard_map/ppermute | solution.py:487
  10.4 0.4 ghost.1
  10.8 2.6 %collective-permute-start.2 = (f32[64,4,128]{2,1,0:T(4,128)S(1)}, f32[64,4,128]{2,1,0:T(4,128)S(1)}, u32[]{:S(2)}, u32[]{:S(2)}) collective-permute-start(f32[64,4,128]{2,1,0:T(4,128)S(1)} %get-tuple-element.28), channel_id=1, source_target_pairs={{0,3},{1,0},{2,1},{3,2},{4,7},{5,4},{6,5},{7,6},{8,11},{9,8},{10,9... | collective-permute-start | bytes 393224 | tf_op jit(solution)/shard_map/ppermute | solution.py:487
  13.4 0.0 collective-permute-start.3
  13.4 3.6 %prep.1 = (f32[48,72,128]{2,1,0:T(8,128)S(1)}, f32[24,72,128]{2,1,0:T(8,128)S(1)}, f32[24,72,128]{2,1,0:T(8,128)S(1)}, f32[48,72,128]{2,1,0:T(8,128)S(1)}, f32[4...) custom-call(f32[64,64,128]{2,1,0:T(8,128)S(1)} %spread.1.own_ref.t_r, ...), custom_call_target="tpu_custom_call" | custom-call | flops 20000000 | tf_op jit(solution)/shard_map/prep/pallas_call | solution.py:549
  16.9 0.0 collective-permute-done.2.right_ref
  16.9 1.5 %collective-permute-done.3.left_ref = f32[64,4,128]{2,1,0:T(4,128)S(1)} collective-permute-done((f32[64,4,128]{2,1,0:T(4,128)S(1)}, f32[64,4,128]{2,1,0:T(4,128)S(1)}, u32[]{:S(2)}, u32[]{:S(2)}) %collective-permute-start.3) | collective-permute-done | bytes 131104 | tf_op jit(solution)/shard_map/ppermute | solution.py:487
  18.4 4.3 %krylov.1 = (f32[48,72,128]{2,1,0:T(8,128)S(1)}, f32[24,72,128]{2,1,0:T(8,128)S(1)}, f32[24,72,128]{2,1,0:T(8,128)S(1)}, f32[48,72,128]{2,1,0:T(8,128)S(1)}, f32...) custom-call(f32[64,4,128]{2,1,0:T(4,128)S(1)} %collective-permute-do, ...), custom_call_target="tpu_custom_call", output_to_operand_aliasing={{0}: (3, {}), {1}: (4, {}), {2}: (5, {}), {3}: (6, {}), {4}... | custom-call | tf_op jit(solution)/shard_map/krylov/pallas_call | solution.py:562
  22.7 25.6 %all_to_all.11 = f32[256,1,128]{2,1,0:T(1,128)S(1)} all-to-all(f32[256,1,128]{2,1,0:T(1,128)S(1)} %bitcast.5), channel_id=1, replica_groups=mesh['curve'=64,'sub'=4] {'curve','sub'}, dimensions={0} | all-to-all | bytes 262144 | tf_op jit(solution)/shard_map/all_to_all | solution.py:574
  48.4 2.6 %combine.1 = (f32[12,96,256]{2,1,0:T(8,128)}, f32[12,96,256]{2,1,0:T(8,128)}) custom-call(f32[256,128]{1,0:T(8,128)S(1)} %bitcast.4, f32[3,128]{1,0:T(4,128)S(1)} %get-tuple-element.30.scale_ref, f32[48,72,128]{2,1,0:T(8,128)S(1)} %get-tuple-element.45.u0_ref, f32[48,72,128]{2,1,0:T(8,128)S(1)} %get-tuple-element.46.u1_ref, ...), custom_call_target="tpu_custom_call" | custom-call | tf_op jit(solution)/shard_map/combine/pallas_call | solution.py:578
Async XLA Ops:
  1.9 6.1 %collective-permute-start = (f32[2,14,16,128]{3,2,1,0:T(8,128)S(1)}, f32[2,14,16,128]{3,2,1,0:T(8,128)S(1)}, u32[]{:S(2)}, u32[]{:S(2)}) collective-permute-start(f32[2,14,16,128]{3,2,1,0:T(8,128)S(1)} %get-tuple-element.26), channel_id=1, source_target_pairs={{0,4},{4,8},{8,12},{12,16},{16,20},{20,24},{24,28},{28,32},{32,36}... | collective-permute-start | bytes 688136 | tf_op jit(solution)/shard_map/ppermute | solution.py:487
  5.0 5.4 %collective-permute-start.1 = (f32[2,14,16,128]{3,2,1,0:T(8,128)S(1)}, f32[2,14,16,128]{3,2,1,0:T(8,128)S(1)}, u32[]{:S(2)}, u32[]{:S(2)}) collective-permute-start(f32[2,14,16,128]{3,2,1,0:T(8,128)S(1)} %get-tuple-element.27), channel_id=1, source_target_pairs={{0,252},{4,0},{8,4},{12,8},{16,12},{20,16},{24,20},{28,24},{32,28}... | collective-permute-start | bytes 688136 | tf_op jit(solution)/shard_map/ppermute | solution.py:487
  10.8 6.1 %collective-permute-start.2 = (f32[64,4,128]{2,1,0:T(4,128)S(1)}, f32[64,4,128]{2,1,0:T(4,128)S(1)}, u32[]{:S(2)}, u32[]{:S(2)}) collective-permute-start(f32[64,4,128]{2,1,0:T(4,128)S(1)} %get-tuple-element.28), channel_id=1, source_target_pairs={{0,3},{1,0},{2,1},{3,2},{4,7},{5,4},{6,5},{7,6},{8,11},{9,8},{10,9... | collective-permute-start | bytes 393224 | tf_op jit(solution)/shard_map/ppermute | solution.py:487
  13.4 5.0 %collective-permute-start.3 = (f32[64,4,128]{2,1,0:T(4,128)S(1)}, f32[64,4,128]{2,1,0:T(4,128)S(1)}, u32[]{:S(2)}, u32[]{:S(2)}) collective-permute-start(f32[64,4,128]{2,1,0:T(4,128)S(1)} %get-tuple-element.29), channel_id=1, source_target_pairs={{0,1},{1,2},{2,3},{3,0},{4,5},{5,6},{6,7},{7,4},{8,9},{9,10},{10,1... | collective-permute-start | bytes 393224 | tf_op jit(solution)/shard_map/ppermute | solution.py:487

commit v11 on v9

--- a/solution.py
+++ b/solution.py
@@ -321,8 +321,7 @@
     cols = t_ref.shape[1]
     rim = lax.broadcasted_iota(jnp.int32, (8, LANES), 1) < RIM
 
-    @pl.loop(0, cols // 8)
-    def _(t):
+    def one(t):
         def fetch(p):
             group, a, b = p // 16, p // 4 % 4, p % 4
             outer = rim_ref[t, group, pl.ds(b, 8, stride=4), :]
@@ -331,6 +330,11 @@
             return jnp.where(rim, outer, t_ref[p, tile(t), :])
 
         prepare(t, fetch, scale_ref, *state)
+
+    @pl.loop(0, cols // 16)
+    def _(i):
+        one(2 * i)
+        one(2 * i + 1)
 
     @pl.loop(0, 4)
     def _(a):

time: 51.3 us -> 51.3 us (level)
  transfers between devices with their start and end apart: 4 -> 4, of which waited for: 3 -> 3; matrix products, arithmetic and copies ran while one was open for 0% -> 0% of each run, Pallas kernels for 11% -> 10%
where the time goes in v11:
time: 51.3 us; the launch traced here: 51.2 us
  blocking collectives  25.6 us (50%)
  Pallas kernels  13.9 us (27%)
  starting transfers between devices  5.93 us (12%)
  waiting for transfers between devices  5.09 us (10%)
  between operations  0.67 us (1%)
    all_to_all x1, blocking collectives, shards(): parts = lax.all_to_all(part, AXES, 0, 0, tiled=True)  25.6 us
    ppermute x4, starting transfers between devices, shift(): lax.ppermute(x, axis, [(i, (i + step) % count) for i in range(count)])  5.93 us
    ppermute x4, waiting for transfers between devices, shift(): lax.ppermute(x, axis, [(i, (i + step) % count) for i in range(count)])  5.09 us
    pallas_call x1, Pallas kernels, shards(): pl.pallas_call(functools.partial(krylov_kernel, ecols, count), in_specs=[...  4.48 us
    pallas_call x1, Pallas kernels, shards(): pl.pallas_call(prep_kernel, in_specs=[vmem] * 3, out_specs=[vmem] * 12, o...  3.17 us
    pallas_call x1, Pallas kernels, shards(): pl.pallas_call(combine_kernel, in_specs=[vmem] * 7, out_specs=[anywhere]...  2.64 us
    pallas_call x1, Pallas kernels, shards(): pl.pallas_call(spread_kernel, in_specs=[anywhere] * 3, out_specs=vmem, ou...  1.93 us
    pallas_call x1, Pallas kernels, shards(): pl.pallas_call(load_kernel, in_specs=[anywhere] * 4, out_specs=[vmem] * 3...  1.26 us
  transfers between devices with their start and end apart: 4, of which 3 were waited for; matrix products, arithmetic and copies ran while one was open for 0% of the time, Pallas kernels for 10%

profile of v11, /device:TPU:1, one launch (start us, length us, event | category | flops | bytes accessed | tf_op | source)
XLA Modules:
  0.0 51.2 jit_solution(2322486746259735940)
XLA Ops:
  0.6 1.3 %load.1 = (f32[2,14,16,128]{3,2,1,0:T(8,128)S(1)}, f32[2,14,16,128]{3,2,1,0:T(8,128)S(1)}, f32[3,128]{1,0:T(4,128)S(1)}) custom-call(f32[12,96,256]{2,1,0:T(8,128)} %f_hbm.3, f32[96,256]{1,0:T(8,128)} %metric_hbm.3, f32[96,256]{1,0:T(8,128)} %jacobian_hbm.3, f32[12]{0:T(128)} %scale_hbm.1), custom_call_target="tpu_custom_call" | custom-call | tf_op jit(solution)/shard_map/load/pallas_call | solution.py:506
  1.9 3.1 %collective-permute-start = (f32[2,14,16,128]{3,2,1,0:T(8,128)S(1)}, f32[2,14,16,128]{3,2,1,0:T(8,128)S(1)}, u32[]{:S(2)}, u32[]{:S(2)}) collective-permute-start(f32[2,14,16,128]{3,2,1,0:T(8,128)S(1)} %get-tuple-element.26), channel_id=1, source_target_pairs={{0,4},{4,8},{8,12},{12,16},{16,20},{20,24},{24,28},{28,32},{32,36}... | collective-permute-start | bytes 688136 | tf_op jit(solution)/shard_map/ppermute | solution.py:494
  5.0 0.3 collective-permute-start.1
  5.3 1.9 %spread.1.own_ref.t_ref = f32[64,64,128]{2,1,0:T(8,128)S(1)} custom-call(f32[12,96,256]{2,1,0:T(8,128)} %f_hbm.3, f32[96,256]{1,0:T(8,128)} %metric_hbm.3, f32[96,256]{1,0:T(8,128)} %jacobian_hbm.3), custom_call_target="tpu_custom_call" | custom-call | flops 10000000 | tf_op jit(solution)/shard_map/spread/pallas_call | solution.py:522
  7.2 0.7 %collective-permute-done.up_ref = f32[2,14,16,128]{3,2,1,0:T(8,128)S(1)} collective-permute-done((f32[2,14,16,128]{3,2,1,0:T(8,128)S(1)}, f32[2,14,16,128]{3,2,1,0:T(8,128)S(1)}, u32[]{:S(2)}, u32[]{:S(2)}) %collective-permute-start) | collective-permute-done | bytes 229408 | tf_op jit(solution)/shard_map/ppermute | solution.py:494
  8.0 2.5 %collective-permute-done.1.down_ref = f32[2,14,16,128]{3,2,1,0:T(8,128)S(1)} collective-permute-done((f32[2,14,16,128]{3,2,1,0:T(8,128)S(1)}, f32[2,14,16,128]{3,2,1,0:T(8,128)S(1)}, u32[]{:S(2)}, u32[]{:S(2)}) %collective-permute-start.1) | collective-permute-done | bytes 229408 | tf_op jit(solution)/shard_map/ppermute | solution.py:494
  10.4 0.4 ghost.1
  10.8 2.6 %collective-permute-start.2 = (f32[64,4,128]{2,1,0:T(4,128)S(1)}, f32[64,4,128]{2,1,0:T(4,128)S(1)}, u32[]{:S(2)}, u32[]{:S(2)}) collective-permute-start(f32[64,4,128]{2,1,0:T(4,128)S(1)} %get-tuple-element.28), channel_id=1, source_target_pairs={{0,3},{1,0},{2,1},{3,2},{4,7},{5,4},{6,5},{7,6},{8,11},{9,8},{10,9... | collective-permute-start | bytes 393224 | tf_op jit(solution)/shard_map/ppermute | solution.py:494
  13.4 0.0 collective-permute-start.3
  13.4 3.2 %prep.1 = (f32[48,72,128]{2,1,0:T(8,128)S(1)}, f32[24,72,128]{2,1,0:T(8,128)S(1)}, f32[24,72,128]{2,1,0:T(8,128)S(1)}, f32[48,72,128]{2,1,0:T(8,128)S(1)}, f32[4...) custom-call(f32[64,64,128]{2,1,0:T(8,128)S(1)} %spread.1.own_ref.t_r, ...), custom_call_target="tpu_custom_call" | custom-call | flops 20000000 | tf_op jit(solution)/shard_map/prep/pallas_call | solution.py:556
  16.6 0.0 collective-permute-done.2.right_ref
  16.6 1.9 %collective-permute-done.3.left_ref = f32[64,4,128]{2,1,0:T(4,128)S(1)} collective-permute-done((f32[64,4,128]{2,1,0:T(4,128)S(1)}, f32[64,4,128]{2,1,0:T(4,128)S(1)}, u32[]{:S(2)}, u32[]{:S(2)}) %collective-permute-start.3) | collective-permute-done | bytes 131104 | tf_op jit(solution)/shard_map/ppermute | solution.py:494
  18.4 4.5 %krylov.1 = (f32[48,72,128]{2,1,0:T(8,128)S(1)}, f32[24,72,128]{2,1,0:T(8,128)S(1)}, f32[24,72,128]{2,1,0:T(8,128)S(1)}, f32[48,72,128]{2,1,0:T(8,128)S(1)}, f32...) custom-call(f32[64,4,128]{2,1,0:T(4,128)S(1)} %collective-permute-do, ...), custom_call_target="tpu_custom_call", output_to_operand_aliasing={{0}: (3, {}), {1}: (4, {}), {2}: (5, {}), {3}: (6, {}), {4}... | custom-call | tf_op jit(solution)/shard_map/krylov/pallas_call | solution.py:569
  22.9 25.6 %all_to_all.11 = f32[256,1,128]{2,1,0:T(1,128)S(1)} all-to-all(f32[256,1,128]{2,1,0:T(1,128)S(1)} %bitcast.5), channel_id=1, replica_groups=mesh['curve'=64,'sub'=4] {'curve','sub'}, dimensions={0} | all-to-all | bytes 262144 | tf_op jit(solution)/shard_map/all_to_all | solution.py:581
  48.5 2.6 %combine.1 = (f32[12,96,256]{2,1,0:T(8,128)}, f32[12,96,256]{2,1,0:T(8,128)}) custom-call(f32[256,128]{1,0:T(8,128)S(1)} %bitcast.4, f32[3,128]{1,0:T(4,128)S(1)} %get-tuple-element.30.scale_ref, f32[48,72,128]{2,1,0:T(8,128)S(1)} %get-tuple-element.45.u0_ref, f32[48,72,128]{2,1,0:T(8,128)S(1)} %get-tuple-element.46.u1_ref, ...), custom_call_target="tpu_custom_call" | custom-call | tf_op jit(solution)/shard_map/combine/pallas_call | solution.py:585
Async XLA Ops:
  1.9 6.1 %collective-permute-start = (f32[2,14,16,128]{3,2,1,0:T(8,128)S(1)}, f32[2,14,16,128]{3,2,1,0:T(8,128)S(1)}, u32[]{:S(2)}, u32[]{:S(2)}) collective-permute-start(f32[2,14,16,128]{3,2,1,0:T(8,128)S(1)} %get-tuple-element.26), channel_id=1, source_target_pairs={{0,4},{4,8},{8,12},{12,16},{16,20},{20,24},{24,28},{28,32},{32,36}... | collective-permute-start | bytes 688136 | tf_op jit(solution)/shard_map/ppermute | solution.py:494
  5.0 5.4 %collective-permute-start.1 = (f32[2,14,16,128]{3,2,1,0:T(8,128)S(1)}, f32[2,14,16,128]{3,2,1,0:T(8,128)S(1)}, u32[]{:S(2)}, u32[]{:S(2)}) collective-permute-start(f32[2,14,16,128]{3,2,1,0:T(8,128)S(1)} %get-tuple-element.27), channel_id=1, source_target_pairs={{0,252},{4,0},{8,4},{12,8},{16,12},{20,16},{24,20},{28,24},{32,28}... | collective-permute-start | bytes 688136 | tf_op jit(solution)/shard_map/ppermute | solution.py:494
  10.8 5.7 %collective-permute-start.2 = (f32[64,4,128]{2,1,0:T(4,128)S(1)}, f32[64,4,128]{2,1,0:T(4,128)S(1)}, u32[]{:S(2)}, u32[]{:S(2)}) collective-permute-start(f32[64,4,128]{2,1,0:T(4,128)S(1)} %get-tuple-element.28), channel_id=1, source_target_pairs={{0,3},{1,0},{2,1},{3,2},{4,7},{5,4},{6,5},{7,6},{8,11},{9,8},{10,9... | collective-permute-start | bytes 393224 | tf_op jit(solution)/shard_map/ppermute | solution.py:494
  13.4 5.0 %collective-permute-start.3 = (f32[64,4,128]{2,1,0:T(4,128)S(1)}, f32[64,4,128]{2,1,0:T(4,128)S(1)}, u32[]{:S(2)}, u32[]{:S(2)}) collective-permute-start(f32[64,4,128]{2,1,0:T(4,128)S(1)} %get-tuple-element.29), channel_id=1, source_target_pairs={{0,1},{1,2},{2,3},{3,0},{4,5},{5,6},{6,7},{7,4},{8,9},{9,10},{10,1... | collective-permute-start | bytes 393224 | tf_op jit(solution)/shard_map/ppermute | solution.py:494
